TPU v7x, 256 devices: a whole 4x4x8 slice. The times are simulated.
256 devices in a mesh: gx: 8 (over x, core), gy: 32 (over z, y).
Axes of the slice: x: 4, y: 4, z: 8, core: 2. Of those that a mesh axis runs over, the one named last changes fastest.
Arguments:
- first_image: float32 [64, 256, 128], P('gx', 'gy'), may hold values from -6 to 6
- second_image: float32 [64, 256, 128], P('gx', 'gy'), may hold values from -6 to 6
- start_flow: float32 [3, 64, 256, 128], P(None, 'gx', 'gy'), may hold values from -3 to 3
Outputs:
- flow: float32 [3, 64, 256, 128], P(None, 'gx', 'gy')
All inputs are finite; a program needn't handle non-finite values.
Results may differ from a plain program's by a relative error of at most 0.0001.
Values sent between devices are 32-bit elements; how exact they have to be, the bound alone decides.
No kernel may reach another device: no remote copies, remote signals or barrier semaphores. Data moves between devices by JAX's collectives and lax.ppermute only.
A program may use at most 128 MiB of HBM per device.

v0:
```python
import functools

import jax
import jax.numpy as jnp
from jax import lax
from jax.experimental import pallas as pl
from jax.experimental.pallas import tpu as pltpu
from jax.sharding import Mesh
from jax.sharding import PartitionSpec as P


SWEEPS = 4
COARSE_SWEEPS = 12
CYCLES = 2
GX = ("gx_0", "gx_1")
GY = ("gy_0", "gy_1")

damping = 0.6
smooth_weight = 2.0
floor_grad = 0.5

NX, NY = 64, 256
ROWS = 24
WIDE = 20
MROWS = 16


def roll(v, shift, axis):
    return pltpu.roll(v, shift % v.shape[axis], axis)


def iota(shape, dim):
    return lax.broadcasted_iota(jnp.int32, shape, dim)


def face(a, b, scale):
    summed = a + b
    return (2.0 * scale) * a * b / jnp.where(summed > 0.0, summed, 1.0)


def inverse_sym(tensor, total):
    aaa = tensor[0] + total
    bbb = tensor[1]
    ccc = tensor[2]
    ddd = tensor[3] + total
    eee = tensor[4]
    fff = tensor[5] + total
    cof_a = ddd * fff - eee * eee
    cof_b = ccc * eee - bbb * fff
    cof_c = bbb * eee - ccc * ddd
    cof_d = aaa * fff - ccc * ccc
    cof_e = bbb * ccc - aaa * eee
    cof_f = aaa * ddd - bbb * bbb
    determinant = aaa * cof_a + bbb * cof_b + ccc * cof_c
    share = jnp.where(total > 0.0, damping / determinant, 0.0)
    return [cof * share for cof in (cof_a, cof_b, cof_c, cof_d, cof_e, cof_f)]


def apply_sym(m, v):
    return [
        m[0] * v[0] + m[1] * v[1] + m[2] * v[2],
        m[1] * v[0] + m[3] * v[1] + m[4] * v[2],
        m[2] * v[0] + m[4] * v[1] + m[5] * v[2],
    ]


def inflow(here, above, below, fx_up, fx_down, fy, fz):
    return (
        fx_up * above
        + fx_down * below
        + fy * roll(here, -1, 0)
        + roll(fy * here, 1, 0)
        + fz * roll(here, -1, 1)
        + roll(fz * here, 1, 1)
    )


def total_of(fx_up, fx_down, fy, fz):
    return fx_up + fx_down + fy + roll(fy, 1, 0) + fz + roll(fz, 1, 1)


def loop(low, high, turn, unroll=1):
    def step(index, carry):
        turn(index)
        return carry

    lax.fori_loop(low, high, step, 0, unroll=unroll)


def sides(par, which, shape):
    is_odd = (jnp.zeros(shape, jnp.int32) + (par[which] & 1)) == 1
    return (lambda a, b: jnp.where(is_odd, a, b)), (lambda a, b: jnp.where(is_odd, b, a))


def hat(distance):
    return jnp.maximum(1.0 - jnp.abs(distance), 0.0)


def dot(a, b):
    return jnp.dot(a, b, precision=lax.Precision.HIGHEST, preferred_element_type=jnp.float32)


def fine_sweep(source, target, low, high, lev, tens):
    def turn(x):
        fx_up, fx_down = lev[0, x], lev[0, x - 1]
        fy, fz = lev[1, x], lev[2, x]
        here = [source[c, x] for c in range(3)]
        flux = [
            tens[6 + c, x]
            + inflow(here[c], source[c, x + 1], source[c, x - 1], fx_up, fx_down, fy, fz)
            for c in range(3)
        ]
        step = apply_sym([lev[3 + k, x] for k in range(6)], flux)
        for c in range(3):
            target[c, x] = (1.0 - damping) * here[c] + step[c]

    loop(low, high, turn)


def widen_kernel(layers, par, own, xa, xb, out):
    shape = (8, 128)
    low_of, high_of = sides(par, 0, shape)
    for f in range(own.shape[0]):
        for k in range(layers):
            out[f, k] = low_of(xa[f, 8 - layers + k], xb[f, 8 - layers + k])
            out[f, layers + 8 + k] = high_of(xa[f, k], xb[f, k])
        for k in range(8):
            out[f, layers + k] = own[f, k]


def stack_rows(par, own, ya, yb, out, fields):
    low_of, high_of = sides(par, 1, (8, 128))

    def turn(x):
        for f in range(fields):
            a, b = ya[f, x], yb[f, x]
            out[f, x, 0:8] = low_of(a, b)
            out[f, x, 8:16] = own[f, x]
            out[f, x, 16:24] = high_of(a, b)

    loop(0, own.shape[1], turn)


def pre_kernel(first, *refs):
    if first:
        par, own, ya, yb, flow_out, msg, lev, tens, u0, u1, w, even, odd, sums = refs
    else:
        par, own, ya, yb, tens, flow_out, msg, lev, u0, u1, w, even, odd, sums = refs
    shape = (ROWS, 128)
    lane = iota(shape, 1)
    last, start = lane == 127, lane == 0
    stack_rows(par, own, ya, yb, u0, own.shape[0])

    def z_slope(v):
        return jnp.where(last, 0.0, roll(v, -1, 1)) - jnp.where(start, 0.0, roll(v, 1, 1))

    def y_slope(v):
        return roll(v, -1, 0) - roll(v, 1, 0)

    if first:

        def tensor_turn(x):
            mean = 0.5 * (u0[3, x] + u0[4, x])
            sx = 0.25 * ((u0[3, x + 1] + u0[4, x + 1]) - (u0[3, x - 1] + u0[4, x - 1]))
            sy = 0.5 * y_slope(mean)
            sz = 0.5 * z_slope(mean)
            change = u0[4, x] - u0[3, x]
            scale = 1.0 / (sx * sx + sy * sy + sz * sz + floor_grad)
            gx, gy, gz = scale * sx, scale * sy, scale * sz
            for k, v in enumerate((gx * sx, gx * sy, gx * sz, gy * sy, gy * sz, gz * sz)):
                tens[k, x] = v
            for k, v in enumerate((gx, gy, gz)):
                tens[6 + k, x] = -v * change

        loop(2, 18, tensor_turn)

    row = iota(shape, 0) + (par[1] * 8 - 8)
    inside_y = (row >= 0) & (row < NY)

    def weight_turn(x):
        total = jnp.ones(shape, jnp.float32)
        for c in range(3):
            v = u0[c, x]
            for slope in (u0[c, x + 1] - u0[c, x - 1], y_slope(v), z_slope(v)):
                total = total + slope * slope
        place = x + (par[0] * 8 - 6)
        keep = jnp.where((place >= 0) & (place < NX), 1.0, 0.0)
        w[x] = jnp.where(inside_y, lax.rsqrt(total), 0.0) * keep

    loop(1, 19, weight_turn)

    def face_turn(x):
        v = w[x]
        lev[0, x] = face(v, w[x + 1], smooth_weight)
        lev[1, x] = face(v, roll(v, -1, 0), smooth_weight)
        lev[2, x] = jnp.where(last, 0.0, face(v, roll(v, -1, 1), smooth_weight))

    loop(1, 18, face_turn)

    def inverse_turn(x):
        total = total_of(lev[0, x], lev[0, x - 1], lev[1, x], lev[2, x])
        for k, v in enumerate(inverse_sym([tens[k, x] for k in range(6)], total)):
            lev[3 + k, x] = v

    loop(2, 18, inverse_turn)
    bufs = (u0, u1)
    for n in range(SWEEPS):
        fine_sweep(bufs[n % 2], bufs[(n + 1) % 2], 2 + n, 18 - n, lev, tens)

    def rest_at(x):
        fx_up, fx_down = lev[0, x], lev[0, x - 1]
        fy, fz = lev[1, x], lev[2, x]
        total = total_of(fx_up, fx_down, fy, fz)
        here = [u0[c, x] for c in range(3)]
        moved = apply_sym([tens[k, x] for k in range(6)], here)
        return [
            (
                tens[6 + c, x]
                + inflow(here[c], u0[c, x + 1], u0[c, x - 1], fx_up, fx_down, fy, fz)
                - moved[c]
                - total * here[c]
            )[8:16]
            for c in range(3)
        ]

    def rest_turn(m):
        x = 6 + 2 * m
        rest = [a + b for a, b in zip(rest_at(x), rest_at(x + 1))]
        pair = w[x] + w[x + 1]
        fields = rest + [pair[8:16], roll(pair, 2, 0)[8:16], pair[16:24]]
        if first:
            fields += [tens[k, x, 8:16] + tens[k, x + 1, 8:16] for k in range(6)]
        for k, v in enumerate(fields):
            stage = odd if k % 2 else even
            stage[pl.ds(pl.multiple_of((k // 2) * 32 + m * 8, 8), 8), :] = v

    loop(0, 4, rest_turn)
    for c in range(3):
        for k in range(8):
            flow_out[c, k] = u0[c, 6 + k, 8:16]
    square = (128, 128)
    into = iota(square, 0) // 2
    low = jnp.where(into == iota(square, 1), 0.125, 0.0)
    high = jnp.where(into + 64 == iota(square, 1), 0.125, 0.0)
    sums[...] = dot(even[...], low) + dot(odd[...], high)
    pairs = even.shape[0] // 32
    size = msg.shape[1]
    at = 0
    for p in range(pairs):
        if p == 2:
            v = sums[pl.ds(64, 4, stride=8), :] + sums[pl.ds(65, 4, stride=8), :]
            for s in range(8):
                msg[s, size - 8 : size - 4] = v
                msg[s, size - 4 : size] = v
            continue
        v = sums[pl.ds(p * 32, 16, stride=2), :] + sums[pl.ds(p * 32 + 1, 16, stride=2), :]
        for s in range(8):
            msg[s, at : at + 16] = v
        at += 16


def wide_layers(par, own, xa, xb, place):
    low_of, high_of = sides(par, 0, (8, 128))
    for c in range(3):
        for k in range(4):
            place(c, k, low_of(xa[c, 4 + k], xb[c, 4 + k]))
            place(c, 12 + k, high_of(xa[c, k], xb[c, k]))
        for k in range(8):
            place(c, 4 + k, own[c, k])


def send_flow(par, flow, fa, fb, to_a, to_b):
    first_of, second_of = sides(par, 1, (4, 128))

    def place(c, k, v):
        to_a[c, k] = first_of(v[0:4], v[4:8])
        to_b[c, k] = second_of(v[0:4], v[4:8])

    wide_layers(par, flow, fa, fb, place)


def mid_sweep(source, target, mfx, mlev):
    def turn(x):
        fx_up, fx_down = mfx[x + 1], mfx[x]
        fy, fz = mlev[0, x], mlev[1, x]
        here = [source[c, x + 1] for c in range(3)]
        flux = [
            mlev[8 + c, x]
            + inflow(here[c], source[c, x + 2], source[c, x], fx_up, fx_down, fy, fz)
            for c in range(3)
        ]
        step = apply_sym([mlev[2 + k, x] for k in range(6)], flux)
        for c in range(3):
            target[c, x + 1] = (1.0 - damping) * here[c] + step[c]

    loop(0, 16, turn, unroll=2)
    seam(target)


def seam(field):
    for c in range(3):
        field[c, 0] = roll(field[c, 16], 64, 1)
        field[c, 17] = roll(field[c, 1], 64, 1)


def mid_kernel(first, *refs):
    if first:
        par, own, ya, yb, flow, fa, fb, msg, to_a, to_b, mfx, mlev, err, mtens, u1, w, stage = refs
    else:
        par, own, ya, yb, flow, fa, fb, mtens, msg, to_a, to_b, mfx, mlev, err, u1, w, stage = refs
    send_flow(par, flow, fa, fb, to_a, to_b)
    shape = (MROWS, 128)
    lane = iota(shape, 1)
    left = iota((8, 128), 1) < 64
    low_of, high_of = sides(par, 1, (8, 128))
    size = own.shape[1]
    zero4 = jnp.zeros((4, 128), jnp.float32)

    def split(a, b, which):
        if which:
            return jnp.where(left, roll(a, 64, 1), b)
        return jnp.where(left, a, roll(b, 64, 1))

    def fields_of(out, slot, pair, which):
        def turn(a):
            for kk in range(2):
                rows = slice(pair * 16 + kk * 8, pair * 16 + kk * 8 + 8)
                la, lb = low_of(ya[a, rows], yb[a, rows]), low_of(ya[a + 4, rows], yb[a + 4, rows])
                ha, hb = high_of(ya[a, rows], yb[a, rows]), high_of(ya[a + 4, rows], yb[a + 4, rows])
                for base, va, vb in ((1, la, lb), (5, own[a, rows], own[a + 4, rows]), (9, ha, hb)):
                    v = split(va, vb, which)
                    for k in range(2):
                        x = a * 4 + kk * 2 + k
                        if slot is None:
                            out[x, base : base + 4] = v[4 * k : 4 * k + 4]
                        else:
                            out[slot, x, base : base + 4] = v[4 * k : 4 * k + 4]

        loop(0, 4, turn)

    def clear_turn(x):
        for ref in (w,):
            ref[x, 0:1] = zero4[0:1]
            ref[x, 13:16] = zero4[0:3]
        for k in range(3):
            mlev[8 + k, x, 0:1] = zero4[0:1]
            mlev[8 + k, x, 13:16] = zero4[0:3]
        if first:
            for k in range(6):
                mtens[k, x, 0:1] = zero4[0:1]
                mtens[k, x, 13:16] = zero4[0:3]

    loop(0, 16, clear_turn)
    fields_of(mlev, 8, 0, 0)
    fields_of(mlev, 9, 0, 1)
    fields_of(mlev, 10, 1, 0)
    fields_of(w, None, 1, 1)
    if first:
        for k in range(6):
            fields_of(mtens, k, 2 + k // 2, k % 2)
    outer = slice(size - 8, size)
    for a in range(4):
        la, lb = low_of(ya[a, outer], yb[a, outer]), low_of(ya[a + 4, outer], yb[a + 4, outer])
        ha, hb = high_of(ya[a, outer], yb[a, outer]), high_of(ya[a + 4, outer], yb[a + 4, outer])
        lo, hi = split(la, lb, 0), split(ha, hb, 1)
        for k in range(4):
            w[a * 4 + k, 0:1] = lo[k : k + 1]
            w[a * 4 + k, 13:14] = hi[k : k + 1]

    scale = smooth_weight / 4.0
    stop = (lane == 63) | (lane == 127)

    def face_turn(x):
        v = w[x]
        mlev[0, x] = face(v, roll(v, -1, 0), scale)
        mlev[1, x] = jnp.where(stop, 0.0, face(v, roll(v, -1, 1), scale))

    loop(0, 16, face_turn)

    def across_turn(x):
        mfx[x + 1] = face(w[x], w[x + 1], scale)

    loop(0, 15, across_turn)
    seam_face = jnp.where(lane < 64, face(w[15], roll(w[0], 64, 1), scale), 0.0)
    mfx[16] = seam_face
    mfx[0] = roll(seam_face, 64, 1)

    def inverse_turn(x):
        total = total_of(mfx[x + 1], mfx[x], mlev[0, x], mlev[1, x])
        inv = inverse_sym([mtens[k, x] for k in range(6)], total)
        for k in range(6):
            mlev[2 + k, x] = inv[k]
        begin = apply_sym(inv, [mlev[8 + c, x] for c in range(3)])
        for c in range(3):
            u1[c, x + 1] = begin[c]

    loop(0, 16, inverse_turn)
    seam(u1)
    bufs = (u1, err)
    for n in range(SWEEPS - 1):
        mid_sweep(bufs[n % 2], bufs[(n + 1) % 2], mfx, mlev)
    count = stage.shape[0] // 4
    stage[...] = jnp.zeros(stage.shape, jnp.float32)

    def rest_turn(a):
        sums = [jnp.zeros(shape, jnp.float32) for _ in range(9 if first else 3)]
        for k in range(4):
            x = a * 4 + k
            fx_up, fx_down = mfx[x + 1], mfx[x]
            fy, fz = mlev[0, x], mlev[1, x]
            total = total_of(fx_up, fx_down, fy, fz)
            here = [err[c, x + 1] for c in range(3)]
            moved = apply_sym([mtens[k, x] for k in range(6)], here)
            for c in range(3):
                sums[c] = sums[c] + (
                    mlev[8 + c, x]
                    + inflow(here[c], err[c, x + 2], err[c, x], fx_up, fx_down, fy, fz)
                    - moved[c]
                    - total * here[c]
                )
            if first:
                for q in range(6):
                    sums[3 + q] = sums[3 + q] + mtens[q, x]
        for q, v in enumerate(sums):
            stage[pl.ds(a * count + q, 1), :] = jnp.sum(v[5:9], axis=0, keepdims=True)

    loop(0, 4, rest_turn)
    for c in range(3):
        for x in range(16):
            v = err[c, x + 1, 5:9]
            to_a[3 + c, x] = v
            to_b[3 + c, x] = v
    square = (128, 128)
    z, to = iota(square, 0), iota(square, 1)
    gather = jnp.where((z // 64 == to // 64) & ((z % 64) // 4 == to % 64), 1.0 / 64.0, 0.0)
    mixed = dot(stage[...], gather)
    value = mixed[0:count]
    for a in range(1, 4):
        value = value + roll(mixed[a * count : (a + 1) * count], 16 * a, 1)
    for s in range(32):
        msg[s] = value


def coarse_kernel(first, *refs):
    if first:
        par, whole, mfx, mlev, err, ea, eb, out, cinv, u0, u1, lifted = refs
    else:
        par, whole, mfx, mlev, err, ea, eb, cinv, out, u0, u1, lifted = refs
    count = whole.shape[0] // 32
    grid = (32, 128)
    row, lane = iota(grid, 0), iota(grid, 1)
    cx, cz = lane // 16, lane % 16
    scale = smooth_weight / 64.0
    one = lambda cond: jnp.where(cond, scale, 0.0)
    ups = (one(cx < 7), one(cx > 0), one(row < 31), one(row > 0), one(cz < 15), one(cz > 0))
    total = ups[0] + ups[1] + ups[2] + ups[3] + ups[4] + ups[5]
    if first:
        inv = inverse_sym([whole[pl.ds(3 + k, 32, stride=count), :] for k in range(6)], total)
        for k in range(6):
            cinv[k] = inv[k]
    inv = [cinv[k] for k in range(6)]
    source = [whole[pl.ds(c, 32, stride=count), :] for c in range(3)]

    def turn(index, now):
        flux = []
        for c in range(3):
            v = now[c]
            flux.append(
                source[c]
                + ups[0] * roll(v, -16, 1)
                + ups[1] * roll(v, 16, 1)
                + ups[2] * roll(v, -1, 0)
                + ups[3] * roll(v, 1, 0)
                + ups[4] * roll(v, -1, 1)
                + ups[5] * roll(v, 1, 1)
            )
        step = apply_sym(inv, flux)
        return tuple((1.0 - damping) * now[c] + step[c] for c in range(3))

    correction = lax.fori_loop(0, COARSE_SWEEPS - 1, turn, tuple(apply_sym(inv, source)))

    shape = (MROWS, 32)
    place = (iota(shape, 0) + (par[1] * 4 - 5)).astype(jnp.float32) * 0.25 - 0.375
    along = hat(place - iota(shape, 1).astype(jnp.float32))
    rows = jnp.concatenate([dot(along, correction[c]) for c in range(3)], axis=0)
    square = (128, 128)
    src, to = iota(square, 0), iota(square, 1)
    depth = hat((to % 64).astype(jnp.float32) * 0.25 - 0.375 - (src % 16).astype(jnp.float32))
    for a in range(4):
        spread = jnp.where(src // 16 == a + 4 * (to // 64), depth, 0.0)
        lifted[a + 1] = dot(rows, spread)
    halves = iota((3 * MROWS, 128), 1) < 64
    lifted[0] = jnp.where(halves, 0.0, roll(lifted[4], 64, 1))
    lifted[5] = jnp.where(halves, roll(lifted[1], 64, 1), 0.0)

    low_of, high_of = sides(par, 1, (4, 128))
    zero = jnp.zeros((MROWS, 128), jnp.float32)
    for x in range(16):
        a, d = x // 4, x % 4
        t = (d + 0.5) / 4 - 0.5
        other = a if t < 0 else a + 2
        added = (1.0 - abs(t)) * lifted[a + 1] + abs(t) * lifted[other]
        for c in range(3):
            u0[c, x + 1] = zero
            u0[c, x + 1, 1:5] = low_of(ea[3 + c, x], eb[3 + c, x])
            u0[c, x + 1, 5:9] = err[c, x + 1, 5:9]
            u0[c, x + 1, 9:13] = high_of(ea[3 + c, x], eb[3 + c, x])
            u0[c, x + 1] = u0[c, x + 1] + added[c * MROWS : (c + 1) * MROWS]
    seam(u0)
    bufs = (u0, u1)
    for n in range(SWEEPS):
        mid_sweep(bufs[n % 2], bufs[(n + 1) % 2], mfx, mlev)

    left = iota((4, 128), 1) < 64
    for b in range(3):
        block = par[0] + (b - 1)
        there = jnp.where((block >= 0) & (block < 8), 1.0, 0.0)
        block = jnp.clip(block, 0, 7)
        upper = (jnp.zeros((4, 128), jnp.int32) + block // 4) == 1
        for k in range(4):
            x = (block % 4) * 4 + k + 1
            v = [u0[c, x, 5:9] for c in range(3)]
            v = [(a, roll(a, 64, 1)) for a in v]
            to_left = [jnp.where(upper, turned, a) for a, turned in v]
            to_right = [jnp.where(upper, a, turned) for a, turned in v]
            out[0, b * 4 + k] = jnp.where(left, to_left[0], to_right[1]) * there
            out[1, b * 4 + k] = jnp.where(left, to_left[2], 0.0) * there


def post_kernel(par, flow, fa, fb, ya, yb, mine, ea, eb, lev, tens, out, u0, u1, mixed, lifted, tall):
    low_of, high_of = sides(par, 1, (4, 128))
    zero = jnp.zeros((4, 128), jnp.float32)

    def place(c, k, v):
        u0[c, 2 + k, 8:16] = v

    wide_layers(par, flow, fa, fb, place)

    def edge_turn(k):
        for c in range(3):
            u0[c, 2 + k, 0:4] = zero
            u0[c, 2 + k, 4:8] = low_of(ya[c, k], yb[c, k])
            u0[c, 2 + k, 16:20] = high_of(ya[c, k], yb[c, k])
            u0[c, 2 + k, 20:24] = zero

    loop(0, 16, edge_turn)
    for x in range(12):
        for p in range(2):
            v = [low_of(ea[p, x], eb[p, x]), mine[p, x], high_of(ea[p, x], eb[p, x])]
            for q in range(3):
                mixed[2 * p, x, 4 * q : 4 * q + 4] = v[q]
            mixed[2 * p, x, 12:16] = zero
    square = (128, 128)
    src, to = iota(square, 0), iota(square, 1)
    place = to.astype(jnp.float32) * 0.5 - 0.25
    depth = hat(place - (src % 64).astype(jnp.float32))
    low = jnp.where(src < 64, depth, 0.0)
    high = jnp.where(src < 64, 0.0, depth)
    for c in range(3):
        v = mixed[2 * (c // 2)].reshape(12 * 16, 128)
        lifted[c] = dot(v, high if c == 1 else low).reshape(12, 16, 128)

    def tall_turn(x):
        for c in range(3):
            v = lifted[c, x]
            tall[c, x, pl.ds(0, 12, stride=2), :] = (0.75 * v + 0.25 * roll(v, 1, 0))[0:12]
            tall[c, x, pl.ds(1, 12, stride=2), :] = (0.75 * v + 0.25 * roll(v, -1, 0))[0:12]

    loop(0, 12, tall_turn)

    def add_turn(m):
        for c in range(3):
            a, b, d = tall[c, m - 1], tall[c, m], tall[c, m + 1]
            x = 2 * m - 2
            u0[c, x] = u0[c, x] + (0.75 * b + 0.25 * a)
            u0[c, x + 1] = u0[c, x + 1] + (0.75 * b + 0.25 * d)

    loop(2, 10, add_turn)
    bufs = (u0, u1)
    for n in range(SWEEPS):
        fine_sweep(bufs[n % 2], bufs[(n + 1) % 2], 3 + n, 17 - n, lev, tens)
    for c in range(3):
        for k in range(8):
            out[c, k] = u0[c, 6 + k, 8:16]


def f32(*shape):
    return jax.ShapeDtypeStruct(shape, jnp.float32)


def call(kernel, outs, scratch, args):
    specs = [pl.BlockSpec(memory_space=pltpu.SMEM)]
    specs += [pl.BlockSpec(memory_space=pltpu.VMEM)] * (len(args) - 1)
    return pl.pallas_call(
        kernel,
        in_specs=specs,
        out_specs=[pl.BlockSpec(memory_space=pltpu.VMEM)] * len(outs),
        out_shape=[f32(*shape) for shape in outs],
        scratch_shapes=[pltpu.VMEM(shape, jnp.float32) for shape in scratch],
        compiler_params=pltpu.CompilerParams(vmem_limit_bytes=20 * 2**20),
        cost_estimate=pl.CostEstimate(flops=20_000_000, bytes_accessed=1_000_000, transcendentals=0),
    )(*args)


def pairs_of(size, start):
    pairs = []
    for k in range(start, size - 1, 2):
        pairs += [(k, k + 1), (k + 1, k)]
    return pairs


def across(field, axes, start):
    return lax.ppermute(field, axes, pairs_of(lax.axis_size(axes), start))


def beside(field, axes):
    return [across(field, axes, 0), across(field, axes, 1)]


def shared(message, axes):
    return lax.all_to_all(message, axes, 0, 0, tiled=True)


def body(first_image, second_image, start_flow):
    par = jnp.stack([lax.axis_index(GX), lax.axis_index(GY)]).astype(jnp.int32)
    block = jnp.concatenate([start_flow, first_image[None], second_image[None]])
    flow = start_flow
    tens = mtens = cinv = None
    fine_shape, mid_shape = (WIDE, ROWS, 128), (16, MROWS, 128)
    for cycle in range(CYCLES):
        first = cycle == 0
        sent = block if first else flow
        fields = sent.shape[0]
        args = [par, sent, *beside(sent, GX)]
        (wide,) = call(functools.partial(widen_kernel, 6), [(fields, WIDE, 8, 128)], [], args)
        size = 88 if first else 40
        stage = (6 if first else 3) * 32
        outs = [(3, 8, 8, 128), (8, size, 128), (9, *fine_shape)]
        scratch = [(fields, *fine_shape), (3, *fine_shape), fine_shape, (stage, 128), (stage, 128), (stage, 128)]
        args = [par, wide, *beside(wide, GY)]
        pre = functools.partial(pre_kernel, first)
        if first:
            flow, message, lev, tens = call(pre, [*outs, (9, *fine_shape)], scratch, args)
        else:
            flow, message, lev = call(pre, outs, scratch, [*args, tens])
        layers = beside(flow, GX)
        mids = shared(message, GX)
        args = [par, mids, *beside(mids, GY), flow, *layers]
        count = 16 if first else 8
        sides_shape = (6, 16, 4, 128)
        outs = [(32, count, 128), sides_shape, sides_shape, (17, MROWS, 128), (11, *mid_shape), (3, 18, MROWS, 128)]
        scratch = [(3, 18, MROWS, 128), mid_shape, (4 * count, 128)]
        mid = functools.partial(mid_kernel, first)
        if first:
            coarse, to_a, to_b, mfx, mlev, err, mtens = call(mid, [*outs, (6, *mid_shape)], scratch, args)
        else:
            coarse, to_a, to_b, mfx, mlev, err = call(mid, outs, scratch, [*args, mtens])
        edges = [across(to_a, GY, 0), across(to_b, GY, 1)]
        whole = shared(coarse, GY).reshape(32 * count, 128)
        args = [par, whole, mfx, mlev, err, *edges]
        outs = [(2, 12, 4, 128)]
        scratch = [(3, 18, MROWS, 128), (3, 18, MROWS, 128), (6, 3 * MROWS, 128)]
        low = functools.partial(coarse_kernel, first)
        if first:
            error, cinv = call(low, [*outs, (6, 32, 128)], scratch, args)
        else:
            (error,) = call(low, outs, scratch, [*args, cinv])
        args = [par, flow, *layers, *edges, error, *beside(error, GY), lev, tens]
        scratch = [(3, *fine_shape), (3, *fine_shape), (3, 12, 16, 128), (3, 12, 16, 128), (3, 12, 24, 128)]
        (flow,) = call(post_kernel, [(3, 8, 8, 128)], scratch, args)
    return flow


def solution(mesh):
    finer = Mesh(mesh.devices.reshape(4, 2, 8, 4), ("gx_0", "gx_1", "gy_0", "gy_1"))
    return jax.shard_map(
        body,
        mesh=finer,
        in_specs=(P(GX, GY, None), P(GX, GY, None), P(None, GX, GY, None)),
        out_specs=P(None, GX, GY, None),
        check_vma=False,
    )
```

profile of v0, /device:TPU:122, one launch (start us, length us, event | category | flops | bytes accessed | tf_op | source)
XLA Modules:
  0.0 233.3 jit_solution(7766500195418254320)
XLA Ops:
  8.2 4.7 %collective-permute-start.3 = (f32[5,20,8,128]{3,2,1,0:T(8,128)S(1)}, f32[5,20,8,128]{3,2,1,0:T(8,128)S(1)}, u32[]{:S(2)}, u32[]{:S(2)}) collective-permute-start(f32[5,20,8,128]{3,2,1,0:T(8,128)S(1)} %shard_map.37.refs_1_), channel_id=1, source_target_pairs={{1,2},{2,1},{3,4},{4,3},{5,6},{6,5},{7,8},{8,7},{9,10},{10,9},{11,... | collective-permute-start | bytes 1228808 | tf_op jit(solution)/shard_map/ppermute | solution.py:613
  13.0 11.9 %collective-permute-done.3.refs_3_ = f32[5,20,8,128]{3,2,1,0:T(8,128)S(1)} collective-permute-done((f32[5,20,8,128]{3,2,1,0:T(8,128)S(1)}, f32[5,20,8,128]{3,2,1,0:T(8,128)S(1)}, u32[]{:S(2)}, u32[]{:S(2)}) %collective-permute-start.3) | collective-permute-done | bytes 409632 | tf_op jit(solution)/shard_map/ppermute | solution.py:613
  24.9 12.6 %shard_map.38 = (f32[3,8,8,128]{3,2,1,0:T(8,128)S(1)}, f32[8,88,128]{2,1,0:T(8,128)S(1)}, f32[9,20,24,128]{3,2,1,0:T(8,128)S(1)}, f32[9,20,24,128]{3,2,1,0:T(8,128)S(1)}) custom-call(s32[2]{0:T(128)S(1)} %pad_add_fusion.par.refs_0_, f32[5,20,8,128]{3,2,1,0:T(8,128)S(1)} %shard_map.37.refs_1_, f32[5,20,8,128]{3,2,1,0:T(8,128)S(1)} %collective-permute-done.2.refs_2_, ...), custom_call_target="tpu_custom_call" | custom-call | flops 20000000 | bytes 1000000 | tf_op jit(solution)/shard_map/pallas_call | solution.py:594
  38.8 11.7 %all_to_all.20.refs_1_ = f32[8,88,128]{2,1,0:T(8,128)S(1)} all-to-all(f32[8,88,128]{2,1,0:T(8,128)S(1)} %get-tuple-element.28), channel_id=1, replica_groups=mesh['gx_0'=4,'gx_1'=2,'gy_0'=8,'gy_1'=4] {'gx_0','gx_1'}, dimensions={0} | all-to-all | bytes 720896 | tf_op jit(solution)/shard_map/all_to_all | solution.py:621
  50.5 4.7 %collective-permute-start.7 = (f32[8,88,128]{2,1,0:T(8,128)S(1)}, f32[8,88,128]{2,1,0:T(8,128)S(1)}, u32[]{:S(2)}, u32[]{:S(2)}) collective-permute-start(f32[8,88,128]{2,1,0:T(8,128)S(1)} %all_to_all.20.refs_1_), channel_id=1, source_target_pairs={{1,2},{2,1},{3,4},{4,3},{5,6},{6,5},{7,8},{8,7},{9,10},{10,9},{11,... | collective-permute-start | bytes 1081352 | tf_op jit(solution)/shard_map/ppermute | solution.py:613
  61.3 4.5 %collective-permute-done.7.refs_3_ = f32[8,88,128]{2,1,0:T(8,128)S(1)} collective-permute-done((f32[8,88,128]{2,1,0:T(8,128)S(1)}, f32[8,88,128]{2,1,0:T(8,128)S(1)}, u32[]{:S(2)}, u32[]{:S(2)}) %collective-permute-start.7) | collective-permute-done | bytes 360480 | tf_op jit(solution)/shard_map/ppermute | solution.py:613
  65.8 11.1 %shard_map.39 = (f32[32,16,128]{2,1,0:T(8,128)}, f32[6,16,4,128]{3,2,1,0:T(4,128)}, f32[6,16,4,128]{3,2,1,0:T(4,128)S(1)}, f32[17,16,128]{2,1,0:T(8,128)S(1)}, f...) custom-call(s32[2]{0:T(128)S(1)} %pad_add_fusion.par.refs_0_, ...), custom_call_target="tpu_custom_call" | custom-call | flops 20000000 | bytes 1000000 | tf_op jit(solution)/shard_map/pallas_call | solution.py:594
  80.2 7.5 %all-to-all-start.1 = ((f32[32,16,128]{2,1,0:T(8,128)}), f32[32,16,128]{2,1,0:T(8,128)S(1)}, u32[]{:S(2)}, u32[]{:S(2)}) async-start(f32[32,16,128]{2,1,0:T(8,128)} %get-tuple-element.31), calls=%async_computation.1 | async-start | bytes 524288 | tf_op jit(solution)/shard_map/all_to_all | solution.py:621
  88.6 5.2 %collective-permute-start.9 = (f32[6,16,4,128]{3,2,1,0:T(4,128)}, f32[6,16,4,128]{3,2,1,0:T(4,128)S(1)}, u32[]{:S(2)}, u32[]{:S(2)}) collective-permute-start(f32[6,16,4,128]{3,2,1,0:T(4,128)} %copy-done.18), channel_id=1, source_target_pairs={{1,2},{2,1},{3,4},{4,3},{5,6},{6,5},{7,8},{8,7},{9,10},{10,9},{11,... | collective-permute-start | bytes 589832 | tf_op jit(solution)/shard_map/ppermute | solution.py:613
  102.1 6.3 %shard_map.40 = (f32[2,12,4,128]{3,2,1,0:T(4,128)S(1)}, f32[6,32,128]{2,1,0:T(8,128)S(1)}) custom-call(s32[2]{0:T(128)S(1)} %pad_add_fusion.par.refs_0_, f32[512,128]{1,0:T(8,128)S(1)} %bitcast.6, f32[17,16,128]{2,1,0:T(8,128)S(1)} %copy-done.13, f32[11,16,16,128]{3,2,1,0:T(8,128)S(1)} %copy-done.5, f32[3,18,16,128]{3,2,1,0:T(8,128)S(1)} %get-tuple-element.34.refs_4_, ...), custom_call_target="tpu_custom_call" | custom-call | flops 20000000 | bytes 1000000 | tf_op jit(solution)/shard_map/pallas_call | solution.py:594
  108.5 5.2 %collective-permute-start.11 = (f32[2,12,4,128]{3,2,1,0:T(4,128)S(1)}, f32[2,12,4,128]{3,2,1,0:T(4,128)S(1)}, u32[]{:S(2)}, u32[]{:S(2)}) collective-permute-start(f32[2,12,4,128]{3,2,1,0:T(4,128)S(1)} %get-tuple-element.35.mine), channel_id=1, source_target_pairs={{1,2},{2,1},{3,4},{4,3},{5,6},{6,5},{7,8},{8,7},{9,10},{10,9},{11,... | collective-permute-start | bytes 147464 | tf_op jit(solution)/shard_map/ppermute | solution.py:613
  117.8 5.7 %shard_map.41.own = f32[3,8,8,128]{3,2,1,0:T(8,128)S(1)} custom-call(s32[2]{0:T(128)S(1)} %pad_add_fusion.par.refs_0_, f32[3,8,8,128]{3,2,1,0:T(8,128)S(1)} %get-tuple-element.27.refs_4_.flow, f32[3,8,8,128]{3,2,1,0:T(8,128)S(1)} %copy-done.11, f32[3,8,8,128]{3,2,1,0:T(8,128)S(1)} %collective-permute-done.5.refs_6_.fb, ...), custom_call_target="tpu_custom_call" | custom-call | flops 20000000 | bytes 1000000 | tf_op jit(solution)/shard_map/pallas_call | solution.py:594
  130.2 5.1 %collective-permute-start.15 = (f32[3,20,8,128]{3,2,1,0:T(8,128)S(1)}, f32[3,20,8,128]{3,2,1,0:T(8,128)S(1)}, u32[]{:S(2)}, u32[]{:S(2)}) collective-permute-start(f32[3,20,8,128]{3,2,1,0:T(8,128)S(1)} %shard_map.42.refs_1_), channel_id=1, source_target_pairs={{1,2},{2,1},{3,4},{4,3},{5,6},{6,5},{7,8},{8,7},{9,10},{10,9},{11,... | collective-permute-start | bytes 737288 | tf_op jit(solution)/shard_map/ppermute | solution.py:613
  135.4 6.5 %collective-permute-done.15.refs_3_ = f32[3,20,8,128]{3,2,1,0:T(8,128)S(1)} collective-permute-done((f32[3,20,8,128]{3,2,1,0:T(8,128)S(1)}, f32[3,20,8,128]{3,2,1,0:T(8,128)S(1)}, u32[]{:S(2)}, u32[]{:S(2)}) %collective-permute-start.15) | collective-permute-done | bytes 245792 | tf_op jit(solution)/shard_map/ppermute | solution.py:613
  142.0 10.9 %shard_map.43 = (f32[3,8,8,128]{3,2,1,0:T(8,128)S(1)}, f32[8,40,128]{2,1,0:T(8,128)S(1)}, f32[9,20,24,128]{3,2,1,0:T(8,128)S(1)}) custom-call(s32[2]{0:T(128)S(1)} %pad_add_fusion.par.refs_0_, f32[3,20,8,128]{3,2,1,0:T(8,128)S(1)} %shard_map.42.refs_1_, f32[3,20,8,128]{3,2,1,0:T(8,128)S(1)} %collective-permute-done.14.refs_2_, ...), custom_call_target="tpu_custom_call" | custom-call | flops 20000000 | bytes 1000000 | tf_op jit(solution)/shard_map/pallas_call | solution.py:594
  154.2 9.9 %all_to_all.21.refs_1_ = f32[8,40,128]{2,1,0:T(8,128)S(1)} all-to-all(f32[8,40,128]{2,1,0:T(8,128)S(1)} %get-tuple-element.39), channel_id=1, replica_groups=mesh['gx_0'=4,'gx_1'=2,'gy_0'=8,'gy_1'=4] {'gx_0','gx_1'}, dimensions={0} | all-to-all | bytes 327680 | tf_op jit(solution)/shard_map/all_to_all | solution.py:621
  164.1 5.1 %collective-permute-start.19 = (f32[8,40,128]{2,1,0:T(8,128)S(1)}, f32[8,40,128]{2,1,0:T(8,128)S(1)}, u32[]{:S(2)}, u32[]{:S(2)}) collective-permute-start(f32[8,40,128]{2,1,0:T(8,128)S(1)} %all_to_all.21.refs_1_), channel_id=1, source_target_pairs={{1,2},{2,1},{3,4},{4,3},{5,6},{6,5},{7,8},{8,7},{9,10},{10,9},{11,... | collective-permute-start | bytes 491528 | tf_op jit(solution)/shard_map/ppermute | solution.py:613
  175.3 9.2 %shard_map.44 = (f32[32,8,128]{2,1,0:T(8,128)}, f32[6,16,4,128]{3,2,1,0:T(4,128)}, f32[6,16,4,128]{3,2,1,0:T(4,128)S(1)}, f32[17,16,128]{2,1,0:T(8,128)S(1)}, f3...) custom-call(s32[2]{0:T(128)S(1)} %pad_add_fusion.par.refs_0_, f32[8,40,128]{2,1,0:T(8,128)S(1)} %all_to_all.21.refs_1_, ...), custom_call_target="tpu_custom_call" | custom-call | flops 20000000 | bytes 1000000 | tf_op jit(solution)/shard_map/pallas_call | solution.py:594
  186.9 8.8 %all-to-all-start.3 = ((f32[32,8,128]{2,1,0:T(8,128)}), f32[32,8,128]{2,1,0:T(8,128)S(1)}, u32[]{:S(2)}, u32[]{:S(2)}) async-start(f32[32,8,128]{2,1,0:T(8,128)} %get-tuple-element.43), calls=%async_computation.3 | async-start | bytes 262144 | tf_op jit(solution)/shard_map/all_to_all | solution.py:621
  196.9 5.2 %collective-permute-start.21 = (f32[6,16,4,128]{3,2,1,0:T(4,128)}, f32[6,16,4,128]{3,2,1,0:T(4,128)S(1)}, u32[]{:S(2)}, u32[]{:S(2)}) collective-permute-start(f32[6,16,4,128]{3,2,1,0:T(4,128)} %copy-done.19), channel_id=1, source_target_pairs={{1,2},{2,1},{3,4},{4,3},{5,6},{6,5},{7,8},{8,7},{9,10},{10,9},{11,... | collective-permute-start | bytes 589832 | tf_op jit(solution)/shard_map/ppermute | solution.py:613
  202.9 5.1 %collective-permute-done.21.refs_6_.yb = f32[6,16,4,128]{3,2,1,0:T(4,128)S(1)} collective-permute-done((f32[6,16,4,128]{3,2,1,0:T(4,128)}, f32[6,16,4,128]{3,2,1,0:T(4,128)S(1)}, u32[]{:S(2)}, u32[]{:S(2)}) %collective-permute-start.21) | collective-permute-done | bytes 196640 | tf_op jit(solution)/shard_map/ppermute | solution.py:613
  211.3 6.3 %shard_map.45.mine = f32[2,12,4,128]{3,2,1,0:T(4,128)S(1)} custom-call(s32[2]{0:T(128)S(1)} %pad_add_fusion.par.refs_0_, f32[256,128]{1,0:T(8,128)S(1)} %bitcast.7, f32[17,16,128]{2,1,0:T(8,128)S(1)} %copy-done.15, f32[11,16,16,128]{3,2,1,0:T(8,128)S(1)} %copy-done.7, f32[3,18,16,128]{3,2,1,0:T(8,128)S(1)} %get-tuple-element.46.refs_4_, ...), custom_call_target="tpu_custom_call" | custom-call | flops 20000000 | bytes 1000000 | tf_op jit(solution)/shard_map/pallas_call | solution.py:594
  217.5 5.2 %collective-permute-start.23 = (f32[2,12,4,128]{3,2,1,0:T(4,128)S(1)}, f32[2,12,4,128]{3,2,1,0:T(4,128)S(1)}, u32[]{:S(2)}, u32[]{:S(2)}) collective-permute-start(f32[2,12,4,128]{3,2,1,0:T(4,128)S(1)} %shard_map.45.mine), channel_id=1, source_target_pairs={{1,2},{2,1},{3,4},{4,3},{5,6},{6,5},{7,8},{8,7},{9,10},{10,9},{11,... | collective-permute-start | bytes 147464 | tf_op jit(solution)/shard_map/ppermute | solution.py:613
  226.9 6.3 %shard_map.46 = f32[3,8,8,128]{3,2,1,0:T(8,128)} custom-call(s32[2]{0:T(128)S(1)} %pad_add_fusion.par.refs_0_, f32[3,8,8,128]{3,2,1,0:T(8,128)S(1)} %get-tuple-element.38.refs_4_.flow, f32[3,8,8,128]{3,2,1,0:T(8,128)S(1)} %collective-permute-done.16.refs_5_.fa, f32[3,8,8,128]{3,2,1,0:T(8,128)S(1)} %collective-permute-done.17.refs_6_.fb, ...), custom_call_target="tpu_custom_call" | custom-call | flops 20000000 | bytes 1000000 | tf_op jit(solution)/shard_map/pallas_call | solution.py:594
  (82 shorter events, 58.4 us)
Async XLA Ops:
  0.9 6.6 %collective-permute-start.1 = (f32[5,8,8,128]{3,2,1,0:T(8,128)S(1)}, f32[5,8,8,128]{3,2,1,0:T(8,128)S(1)}, u32[]{:S(2)}, u32[]{:S(2)}) collective-permute-start(f32[5,8,8,128]{3,2,1,0:T(8,128)S(1)} %pad_maximum_fusion.own), channel_id=1, source_target_pairs={{32,64},{64,32},{96,128},{128,96},{160,192},{192,160},{33,65},{65,... | collective-permute-start | bytes 491528 | tf_op jit(solution)/shard_map/ppermute | solution.py:613
  2.9 4.7 %collective-permute-start = (f32[5,8,8,128]{3,2,1,0:T(8,128)S(1)}, f32[5,8,8,128]{3,2,1,0:T(8,128)S(1)}, u32[]{:S(2)}, u32[]{:S(2)}) collective-permute-start(f32[5,8,8,128]{3,2,1,0:T(8,128)S(1)} %pad_maximum_fusion.own), channel_id=1, source_target_pairs={{0,32},{32,0},{64,96},{96,64},{128,160},{160,128},{192,224},{224,1... | collective-permute-start | bytes 491528 | tf_op jit(solution)/shard_map/ppermute | solution.py:613
  8.2 16.7 %collective-permute-start.3 = (f32[5,20,8,128]{3,2,1,0:T(8,128)S(1)}, f32[5,20,8,128]{3,2,1,0:T(8,128)S(1)}, u32[]{:S(2)}, u32[]{:S(2)}) collective-permute-start(f32[5,20,8,128]{3,2,1,0:T(8,128)S(1)} %shard_map.37.refs_1_), channel_id=1, source_target_pairs={{1,2},{2,1},{3,4},{4,3},{5,6},{6,5},{7,8},{8,7},{9,10},{10,9},{11,... | collective-permute-start | bytes 1228808 | tf_op jit(solution)/shard_map/ppermute | solution.py:613
  12.9 12.0 %collective-permute-start.2 = (f32[5,20,8,128]{3,2,1,0:T(8,128)S(1)}, f32[5,20,8,128]{3,2,1,0:T(8,128)S(1)}, u32[]{:S(2)}, u32[]{:S(2)}) collective-permute-start(f32[5,20,8,128]{3,2,1,0:T(8,128)S(1)} %shard_map.37.refs_1_), channel_id=1, source_target_pairs={{0,1},{1,0},{2,3},{3,2},{4,5},{5,4},{6,7},{7,6},{8,9},{9,8},{10,11... | collective-permute-start | bytes 1228808 | tf_op jit(solution)/shard_map/ppermute | solution.py:613
  50.5 15.2 %collective-permute-start.7 = (f32[8,88,128]{2,1,0:T(8,128)S(1)}, f32[8,88,128]{2,1,0:T(8,128)S(1)}, u32[]{:S(2)}, u32[]{:S(2)}) collective-permute-start(f32[8,88,128]{2,1,0:T(8,128)S(1)} %all_to_all.20.refs_1_), channel_id=1, source_target_pairs={{1,2},{2,1},{3,4},{4,3},{5,6},{6,5},{7,8},{8,7},{9,10},{10,9},{11,... | collective-permute-start | bytes 1081352 | tf_op jit(solution)/shard_map/ppermute | solution.py:613
  55.2 10.5 %collective-permute-start.6 = (f32[8,88,128]{2,1,0:T(8,128)S(1)}, f32[8,88,128]{2,1,0:T(8,128)S(1)}, u32[]{:S(2)}, u32[]{:S(2)}) collective-permute-start(f32[8,88,128]{2,1,0:T(8,128)S(1)} %all_to_all.20.refs_1_), channel_id=1, source_target_pairs={{0,1},{1,0},{2,3},{3,2},{4,5},{5,4},{6,7},{7,6},{8,9},{9,8},{10,11... | collective-permute-start | bytes 1081352 | tf_op jit(solution)/shard_map/ppermute | solution.py:613
  55.3 5.9 %collective-permute-start.5 = (f32[3,8,8,128]{3,2,1,0:T(8,128)S(1)}, f32[3,8,8,128]{3,2,1,0:T(8,128)S(1)}, u32[]{:S(2)}, u32[]{:S(2)}) collective-permute-start(f32[3,8,8,128]{3,2,1,0:T(8,128)S(1)} %get-tuple-element.27.refs_4_.flow), channel_id=1, source_target_pairs={{32,64},{64,32},{96,128},{128,96},{160,192},{192,160},{33,65},{65,... | collective-permute-start | bytes 294920 | tf_op jit(solution)/shard_map/ppermute | solution.py:613
  80.2 19.5 %all-to-all-start.1 = ((f32[32,16,128]{2,1,0:T(8,128)}), f32[32,16,128]{2,1,0:T(8,128)S(1)}, u32[]{:S(2)}, u32[]{:S(2)}) async-start(f32[32,16,128]{2,1,0:T(8,128)} %get-tuple-element.31), calls=%async_computation.1 | async-start | bytes 524288 | tf_op jit(solution)/shard_map/all_to_all | solution.py:621
  87.7 7.6 %collective-permute-start.8 = (f32[6,16,4,128]{3,2,1,0:T(4,128)}, f32[6,16,4,128]{3,2,1,0:T(4,128)S(1)}, u32[]{:S(2)}, u32[]{:S(2)}) collective-permute-start(f32[6,16,4,128]{3,2,1,0:T(4,128)} %get-tuple-element.29), channel_id=1, source_target_pairs={{0,1},{1,0},{2,3},{3,2},{4,5},{5,4},{6,7},{7,6},{8,9},{9,8},{10,11... | collective-permute-start | bytes 589832 | tf_op jit(solution)/shard_map/ppermute | solution.py:613
  88.6 11.1 %collective-permute-start.9 = (f32[6,16,4,128]{3,2,1,0:T(4,128)}, f32[6,16,4,128]{3,2,1,0:T(4,128)S(1)}, u32[]{:S(2)}, u32[]{:S(2)}) collective-permute-start(f32[6,16,4,128]{3,2,1,0:T(4,128)} %copy-done.18), channel_id=1, source_target_pairs={{1,2},{2,1},{3,4},{4,3},{5,6},{6,5},{7,8},{8,7},{9,10},{10,9},{11,... | collective-permute-start | bytes 589832 | tf_op jit(solution)/shard_map/ppermute | solution.py:613
  108.5 9.3 %collective-permute-start.11 = (f32[2,12,4,128]{3,2,1,0:T(4,128)S(1)}, f32[2,12,4,128]{3,2,1,0:T(4,128)S(1)}, u32[]{:S(2)}, u32[]{:S(2)}) collective-permute-start(f32[2,12,4,128]{3,2,1,0:T(4,128)S(1)} %get-tuple-element.35.mine), channel_id=1, source_target_pairs={{1,2},{2,1},{3,4},{4,3},{5,6},{6,5},{7,8},{8,7},{9,10},{10,9},{11,... | collective-permute-start | bytes 147464 | tf_op jit(solution)/shard_map/ppermute | solution.py:613
  113.7 4.2 %collective-permute-start.10 = (f32[2,12,4,128]{3,2,1,0:T(4,128)S(1)}, f32[2,12,4,128]{3,2,1,0:T(4,128)S(1)}, u32[]{:S(2)}, u32[]{:S(2)}) collective-permute-start(f32[2,12,4,128]{3,2,1,0:T(4,128)S(1)} %get-tuple-element.35.mine), channel_id=1, source_target_pairs={{0,1},{1,0},{2,3},{3,2},{4,5},{5,4},{6,7},{7,6},{8,9},{9,8},{10,11... | collective-permute-start | bytes 147464 | tf_op jit(solution)/shard_map/ppermute | solution.py:613
  123.6 6.1 %collective-permute-start.13 = (f32[3,8,8,128]{3,2,1,0:T(8,128)S(1)}, f32[3,8,8,128]{3,2,1,0:T(8,128)S(1)}, u32[]{:S(2)}, u32[]{:S(2)}) collective-permute-start(f32[3,8,8,128]{3,2,1,0:T(8,128)S(1)} %shard_map.41.own), channel_id=1, source_target_pairs={{32,64},{64,32},{96,128},{128,96},{160,192},{192,160},{33,65},{65,... | collective-permute-start | bytes 294920 | tf_op jit(solution)/shard_map/ppermute | solution.py:613
  125.6 4.0 %collective-permute-start.12 = (f32[3,8,8,128]{3,2,1,0:T(8,128)S(1)}, f32[3,8,8,128]{3,2,1,0:T(8,128)S(1)}, u32[]{:S(2)}, u32[]{:S(2)}) collective-permute-start(f32[3,8,8,128]{3,2,1,0:T(8,128)S(1)} %shard_map.41.own), channel_id=1, source_target_pairs={{0,32},{32,0},{64,96},{96,64},{128,160},{160,128},{192,224},{224,1... | collective-permute-start | bytes 294920 | tf_op jit(solution)/shard_map/ppermute | solution.py:613
  130.2 11.8 %collective-permute-start.15 = (f32[3,20,8,128]{3,2,1,0:T(8,128)S(1)}, f32[3,20,8,128]{3,2,1,0:T(8,128)S(1)}, u32[]{:S(2)}, u32[]{:S(2)}) collective-permute-start(f32[3,20,8,128]{3,2,1,0:T(8,128)S(1)} %shard_map.42.refs_1_), channel_id=1, source_target_pairs={{1,2},{2,1},{3,4},{4,3},{5,6},{6,5},{7,8},{8,7},{9,10},{10,9},{11,... | collective-permute-start | bytes 737288 | tf_op jit(solution)/shard_map/ppermute | solution.py:613
  135.3 6.6 %collective-permute-start.14 = (f32[3,20,8,128]{3,2,1,0:T(8,128)S(1)}, f32[3,20,8,128]{3,2,1,0:T(8,128)S(1)}, u32[]{:S(2)}, u32[]{:S(2)}) collective-permute-start(f32[3,20,8,128]{3,2,1,0:T(8,128)S(1)} %shard_map.42.refs_1_), channel_id=1, source_target_pairs={{0,1},{1,0},{2,3},{3,2},{4,5},{5,4},{6,7},{7,6},{8,9},{9,8},{10,11... | collective-permute-start | bytes 737288 | tf_op jit(solution)/shard_map/ppermute | solution.py:613
  164.1 11.2 %collective-permute-start.19 = (f32[8,40,128]{2,1,0:T(8,128)S(1)}, f32[8,40,128]{2,1,0:T(8,128)S(1)}, u32[]{:S(2)}, u32[]{:S(2)}) collective-permute-start(f32[8,40,128]{2,1,0:T(8,128)S(1)} %all_to_all.21.refs_1_), channel_id=1, source_target_pairs={{1,2},{2,1},{3,4},{4,3},{5,6},{6,5},{7,8},{8,7},{9,10},{10,9},{11,... | collective-permute-start | bytes 491528 | tf_op jit(solution)/shard_map/ppermute | solution.py:613
  169.2 6.0 %collective-permute-start.18 = (f32[8,40,128]{2,1,0:T(8,128)S(1)}, f32[8,40,128]{2,1,0:T(8,128)S(1)}, u32[]{:S(2)}, u32[]{:S(2)}) collective-permute-start(f32[8,40,128]{2,1,0:T(8,128)S(1)} %all_to_all.21.refs_1_), channel_id=1, source_target_pairs={{0,1},{1,0},{2,3},{3,2},{4,5},{5,4},{6,7},{7,6},{8,9},{9,8},{10,11... | collective-permute-start | bytes 491528 | tf_op jit(solution)/shard_map/ppermute | solution.py:613
  169.3 5.9 %collective-permute-start.17 = (f32[3,8,8,128]{3,2,1,0:T(8,128)S(1)}, f32[3,8,8,128]{3,2,1,0:T(8,128)S(1)}, u32[]{:S(2)}, u32[]{:S(2)}) collective-permute-start(f32[3,8,8,128]{3,2,1,0:T(8,128)S(1)} %get-tuple-element.38.refs_4_.flow), channel_id=1, source_target_pairs={{32,64},{64,32},{96,128},{128,96},{160,192},{192,160},{33,65},{65,... | collective-permute-start | bytes 294920 | tf_op jit(solution)/shard_map/ppermute | solution.py:613
  186.9 21.0 %all-to-all-start.3 = ((f32[32,8,128]{2,1,0:T(8,128)}), f32[32,8,128]{2,1,0:T(8,128)S(1)}, u32[]{:S(2)}, u32[]{:S(2)}) async-start(f32[32,8,128]{2,1,0:T(8,128)} %get-tuple-element.43), calls=%async_computation.3 | async-start | bytes 262144 | tf_op jit(solution)/shard_map/all_to_all | solution.py:621
  195.8 7.1 %collective-permute-start.20 = (f32[6,16,4,128]{3,2,1,0:T(4,128)}, f32[6,16,4,128]{3,2,1,0:T(4,128)S(1)}, u32[]{:S(2)}, u32[]{:S(2)}) collective-permute-start(f32[6,16,4,128]{3,2,1,0:T(4,128)} %get-tuple-element.41), channel_id=1, source_target_pairs={{0,1},{1,0},{2,3},{3,2},{4,5},{5,4},{6,7},{7,6},{8,9},{9,8},{10,11... | collective-permute-start | bytes 589832 | tf_op jit(solution)/shard_map/ppermute | solution.py:613
  196.9 11.1 %collective-permute-start.21 = (f32[6,16,4,128]{3,2,1,0:T(4,128)}, f32[6,16,4,128]{3,2,1,0:T(4,128)S(1)}, u32[]{:S(2)}, u32[]{:S(2)}) collective-permute-start(f32[6,16,4,128]{3,2,1,0:T(4,128)} %copy-done.19), channel_id=1, source_target_pairs={{1,2},{2,1},{3,4},{4,3},{5,6},{6,5},{7,8},{8,7},{9,10},{10,9},{11,... | collective-permute-start | bytes 589832 | tf_op jit(solution)/shard_map/ppermute | solution.py:613
  217.5 9.3 %collective-permute-start.23 = (f32[2,12,4,128]{3,2,1,0:T(4,128)S(1)}, f32[2,12,4,128]{3,2,1,0:T(4,128)S(1)}, u32[]{:S(2)}, u32[]{:S(2)}) collective-permute-start(f32[2,12,4,128]{3,2,1,0:T(4,128)S(1)} %shard_map.45.mine), channel_id=1, source_target_pairs={{1,2},{2,1},{3,4},{4,3},{5,6},{6,5},{7,8},{8,7},{9,10},{10,9},{11,... | collective-permute-start | bytes 147464 | tf_op jit(solution)/shard_map/ppermute | solution.py:613
  222.7 4.2 %collective-permute-start.22 = (f32[2,12,4,128]{3,2,1,0:T(4,128)S(1)}, f32[2,12,4,128]{3,2,1,0:T(4,128)S(1)}, u32[]{:S(2)}, u32[]{:S(2)}) collective-permute-start(f32[2,12,4,128]{3,2,1,0:T(4,128)S(1)} %shard_map.45.mine), channel_id=1, source_target_pairs={{0,1},{1,0},{2,3},{3,2},{4,5},{5,4},{6,7},{7,6},{8,9},{9,8},{10,11... | collective-permute-start | bytes 147464 | tf_op jit(solution)/shard_map/ppermute | solution.py:613
  (22 other events, 156.6 us)
where the time goes:
time: 235 us; the launch traced here: 233 us
  starting transfers between devices  70.3 us (30%)
  Pallas kernels  69.4 us (30%)
  waiting for transfers between devices  56.3 us (24%)
  blocking collectives  21.6 us (9%)
  local copies, waits for them, and re-layouts  14.3 us (6%)
    pallas_call x10, Pallas kernels, call(): pl.pallas_call(kernel, in_specs=specs, out_specs=[pl.BlockSpec(memory_spa...  69.4 us
    ppermute x24, waiting for transfers between devices, across(): return lax.ppermute(field, axes, pairs_of(lax.axis_size(axes), start))  56.3 us
    ppermute x24, starting transfers between devices, across(): return lax.ppermute(field, axes, pairs_of(lax.axis_size(axes), start))  54 us
    all_to_all x2, blocking collectives, shared(): return lax.all_to_all(message, axes, 0, 0, tiled=True)  21.6 us
    all_to_all x2, starting transfers between devices, shared(): return lax.all_to_all(message, axes, 0, 0, tiled=True)  16.3 us
    unnamed x40, local copies, waits for them, and re-layouts  14.3 us
  transfers between devices with their start and end apart: 26, of which 15 were waited for; matrix products, arithmetic and copies ran while one was open for 0% of the time, Pallas kernels for 0%

commit v1 on v0

--- a/solution.py
+++ b/solution.py
@@ -79,12 +79,16 @@
     return fx_up + fx_down + fy + roll(fy, 1, 0) + fz + roll(fz, 1, 1)
 
 
-def loop(low, high, turn, unroll=1):
-    def step(index, carry):
+def loop(low, high, turn):
+    for index in range(low, high):
         turn(index)
-        return carry
-
-    lax.fori_loop(low, high, step, 0, unroll=unroll)
+
+
+def moved(pairs, sems):
+    copies = [pltpu.make_async_copy(a, b, sems.at[k]) for k, (a, b) in enumerate(pairs)]
+    for copy in copies:
+        copy.start()
+    return copies
 
 
 def sides(par, which, shape):
@@ -143,9 +147,10 @@
 
 def pre_kernel(first, *refs):
     if first:
-        par, own, ya, yb, flow_out, msg, lev, tens, u0, u1, w, even, odd, sums = refs
+        par, own, ya, yb, flow_out, msg, lev_far, tens_far, lev, tens, u0, u1, w, even, odd, sums, sems = refs
     else:
-        par, own, ya, yb, tens, flow_out, msg, lev, u0, u1, w, even, odd, sums = refs
+        par, own, ya, yb, tens_far, flow_out, msg, lev_far, lev, tens, u0, u1, w, even, odd, sums, sems = refs
+        (tens_copy,) = moved([(tens_far, tens)], sems)
     shape = (ROWS, 128)
     lane = iota(shape, 1)
     last, start = lane == 127, lane == 0
@@ -197,12 +202,17 @@
 
     loop(1, 18, face_turn)
 
+    if not first:
+        tens_copy.wait()
+
     def inverse_turn(x):
         total = total_of(lev[0, x], lev[0, x - 1], lev[1, x], lev[2, x])
         for k, v in enumerate(inverse_sym([tens[k, x] for k in range(6)], total)):
             lev[3 + k, x] = v
 
     loop(2, 18, inverse_turn)
+    far = [(lev, lev_far), (tens, tens_far)] if first else [(lev, lev_far)]
+    copies = moved(far, sems)
     bufs = (u0, u1)
     for n in range(SWEEPS):
         fine_sweep(bufs[n % 2], bufs[(n + 1) % 2], 2 + n, 18 - n, lev, tens)
@@ -232,7 +242,8 @@
             fields += [tens[k, x, 8:16] + tens[k, x + 1, 8:16] for k in range(6)]
         for k, v in enumerate(fields):
             stage = odd if k % 2 else even
-            stage[pl.ds(pl.multiple_of((k // 2) * 32 + m * 8, 8), 8), :] = v
+            at = (k // 2) * 32 + m * 8
+            stage[at : at + 8] = v
 
     loop(0, 4, rest_turn)
     for c in range(3):
@@ -257,6 +268,8 @@
         for s in range(8):
             msg[s, at : at + 16] = v
         at += 16
+    for copy in copies:
+        copy.wait()
 
 
 def wide_layers(par, own, xa, xb, place):
@@ -293,7 +306,7 @@
         for c in range(3):
             target[c, x + 1] = (1.0 - damping) * here[c] + step[c]
 
-    loop(0, 16, turn, unroll=2)
+    loop(0, 16, turn)
     seam(target)
 
 
@@ -305,9 +318,12 @@
 
 def mid_kernel(first, *refs):
     if first:
-        par, own, ya, yb, flow, fa, fb, msg, to_a, to_b, mfx, mlev, err, mtens, u1, w, stage = refs
+        par, own, ya, yb, flow, fa, fb, msg, to_a, to_b, *refs = refs
+        mfx_far, mlev_far, err_far, mtens_far, mfx, mlev, err, mtens, u1, w, stage, sems = refs
     else:
-        par, own, ya, yb, flow, fa, fb, mtens, msg, to_a, to_b, mfx, mlev, err, u1, w, stage = refs
+        par, own, ya, yb, flow, fa, fb, mtens_far, msg, to_a, to_b, *refs = refs
+        mfx_far, mlev_far, err_far, mfx, mlev, err, mtens, u1, w, stage, sems = refs
+        (mtens_copy,) = moved([(mtens_far, mtens)], sems)
     send_flow(par, flow, fa, fb, to_a, to_b)
     shape = (MROWS, 128)
     lane = iota(shape, 1)
@@ -385,6 +401,9 @@
     mfx[16] = seam_face
     mfx[0] = roll(seam_face, 64, 1)
 
+    if not first:
+        mtens_copy.wait()
+
     def inverse_turn(x):
         total = total_of(mfx[x + 1], mfx[x], mlev[0, x], mlev[1, x])
         inv = inverse_sym([mtens[k, x] for k in range(6)], total)
@@ -396,9 +415,12 @@
 
     loop(0, 16, inverse_turn)
     seam(u1)
+    far = [(mfx, mfx_far), (mlev, mlev_far)]
+    copies = moved(far + [(mtens, mtens_far)] if first else far, sems)
     bufs = (u1, err)
     for n in range(SWEEPS - 1):
         mid_sweep(bufs[n % 2], bufs[(n + 1) % 2], mfx, mlev)
+    (err_copy,) = moved([(err, err_far)], sems.at[3:4])
     count = stage.shape[0] // 4
     stage[...] = jnp.zeros(stage.shape, jnp.float32)
 
@@ -422,7 +444,7 @@
                 for q in range(6):
                     sums[3 + q] = sums[3 + q] + mtens[q, x]
         for q, v in enumerate(sums):
-            stage[pl.ds(a * count + q, 1), :] = jnp.sum(v[5:9], axis=0, keepdims=True)
+            stage[a * count + q : a * count + q + 1] = jnp.sum(v[5:9], axis=0, keepdims=True)
 
     loop(0, 4, rest_turn)
     for c in range(3):
@@ -439,13 +461,16 @@
         value = value + roll(mixed[a * count : (a + 1) * count], 16 * a, 1)
     for s in range(32):
         msg[s] = value
+    for copy in [*copies, err_copy]:
+        copy.wait()
 
 
 def coarse_kernel(first, *refs):
     if first:
-        par, whole, mfx, mlev, err, ea, eb, out, cinv, u0, u1, lifted = refs
+        par, whole, mfx_far, mlev_far, err_far, ea, eb, out, cinv_far, mfx, mlev, err, cinv, u0, u1, lifted, sems = refs
     else:
-        par, whole, mfx, mlev, err, ea, eb, cinv, out, u0, u1, lifted = refs
+        par, whole, mfx_far, mlev_far, err_far, ea, eb, cinv, out, mfx, mlev, err, u0, u1, lifted, sems = refs
+    copies = moved([(mfx_far, mfx), (mlev_far, mlev), (err_far, err)], sems)
     count = whole.shape[0] // 32
     grid = (32, 128)
     row, lane = iota(grid, 0), iota(grid, 1)
@@ -458,6 +483,7 @@
         inv = inverse_sym([whole[pl.ds(3 + k, 32, stride=count), :] for k in range(6)], total)
         for k in range(6):
             cinv[k] = inv[k]
+        copies += moved([(cinv, cinv_far)], sems.at[3:4])
     inv = [cinv[k] for k in range(6)]
     source = [whole[pl.ds(c, 32, stride=count), :] for c in range(3)]
 
@@ -493,6 +519,8 @@
     lifted[0] = jnp.where(halves, 0.0, roll(lifted[4], 64, 1))
     lifted[5] = jnp.where(halves, roll(lifted[1], 64, 1), 0.0)
 
+    for copy in copies:
+        copy.wait()
     low_of, high_of = sides(par, 1, (4, 128))
     zero = jnp.zeros((MROWS, 128), jnp.float32)
     for x in range(16):
@@ -527,7 +555,8 @@
             out[1, b * 4 + k] = jnp.where(left, to_left[2], 0.0) * there
 
 
-def post_kernel(par, flow, fa, fb, ya, yb, mine, ea, eb, lev, tens, out, u0, u1, mixed, lifted, tall):
+def post_kernel(par, flow, fa, fb, ya, yb, mine, ea, eb, lev_far, tens_far, out, lev, tens, u0, u1, mixed, lifted, tall, sems):
+    copies = moved([(lev_far, lev), (tens_far.at[6:9], tens.at[6:9])], sems)
     low_of, high_of = sides(par, 1, (4, 128))
     zero = jnp.zeros((4, 128), jnp.float32)
 
@@ -576,6 +605,8 @@
             u0[c, x + 1] = u0[c, x + 1] + (0.75 * b + 0.25 * d)
 
     loop(2, 10, add_turn)
+    for copy in copies:
+        copy.wait()
     bufs = (u0, u1)
     for n in range(SWEEPS):
         fine_sweep(bufs[n % 2], bufs[(n + 1) % 2], 3 + n, 17 - n, lev, tens)
@@ -588,16 +619,21 @@
     return jax.ShapeDtypeStruct(shape, jnp.float32)
 
 
-def call(kernel, outs, scratch, args):
+def call(kernel, outs, scratch, args, far_in=(), far_out=(), sems=0):
+    near, far = pl.BlockSpec(memory_space=pltpu.VMEM), pl.BlockSpec(memory_space=pltpu.HBM)
+    args = [pltpu.with_memory_space_constraint(v, pltpu.HBM) if k in far_in else v for k, v in enumerate(args)]
     specs = [pl.BlockSpec(memory_space=pltpu.SMEM)]
-    specs += [pl.BlockSpec(memory_space=pltpu.VMEM)] * (len(args) - 1)
+    specs += [far if k in far_in else near for k in range(1, len(args))]
+    scratch_shapes = [pltpu.VMEM(shape, jnp.float32) for shape in scratch]
+    if sems:
+        scratch_shapes.append(pltpu.SemaphoreType.DMA((sems,)))
     return pl.pallas_call(
         kernel,
         in_specs=specs,
-        out_specs=[pl.BlockSpec(memory_space=pltpu.VMEM)] * len(outs),
-        out_shape=[f32(*shape) for shape in outs],
-        scratch_shapes=[pltpu.VMEM(shape, jnp.float32) for shape in scratch],
-        compiler_params=pltpu.CompilerParams(vmem_limit_bytes=20 * 2**20),
+        out_specs=[far if k in far_out else near for k in range(len(outs))],
+        out_shape=[pltpu.HBM(shape, jnp.float32) if k in far_out else f32(*shape) for k, shape in enumerate(outs)],
+        scratch_shapes=scratch_shapes,
+        compiler_params=pltpu.CompilerParams(vmem_limit_bytes=24 * 2**20),
         cost_estimate=pl.CostEstimate(flops=20_000_000, bytes_accessed=1_000_000, transcendentals=0),
     )(*args)
 
@@ -636,38 +672,44 @@
         size = 88 if first else 40
         stage = (6 if first else 3) * 32
         outs = [(3, 8, 8, 128), (8, size, 128), (9, *fine_shape)]
-        scratch = [(fields, *fine_shape), (3, *fine_shape), fine_shape, (stage, 128), (stage, 128), (stage, 128)]
+        scratch = [(9, *fine_shape), (9, *fine_shape), (fields, *fine_shape), (3, *fine_shape), fine_shape]
+        scratch += [(stage, 128)] * 3
         args = [par, wide, *beside(wide, GY)]
         pre = functools.partial(pre_kernel, first)
         if first:
-            flow, message, lev, tens = call(pre, [*outs, (9, *fine_shape)], scratch, args)
+            flow, message, lev, tens = call(pre, [*outs, (9, *fine_shape)], scratch, args, (), (2, 3), 2)
         else:
-            flow, message, lev = call(pre, outs, scratch, [*args, tens])
+            flow, message, lev = call(pre, outs, scratch, [*args, tens], (4,), (2,), 2)
         layers = beside(flow, GX)
         mids = shared(message, GX)
         args = [par, mids, *beside(mids, GY), flow, *layers]
         count = 16 if first else 8
         sides_shape = (6, 16, 4, 128)
-        outs = [(32, count, 128), sides_shape, sides_shape, (17, MROWS, 128), (11, *mid_shape), (3, 18, MROWS, 128)]
-        scratch = [(3, 18, MROWS, 128), mid_shape, (4 * count, 128)]
+        saved = [(17, MROWS, 128), (11, *mid_shape), (3, 18, MROWS, 128)]
+        outs = [(32, count, 128), sides_shape, sides_shape, *saved]
+        scratch = [*saved, (6, *mid_shape), (3, 18, MROWS, 128), mid_shape, (4 * count, 128)]
         mid = functools.partial(mid_kernel, first)
         if first:
-            coarse, to_a, to_b, mfx, mlev, err, mtens = call(mid, [*outs, (6, *mid_shape)], scratch, args)
+            coarse, to_a, to_b, mfx, mlev, err, mtens = call(
+                mid, [*outs, (6, *mid_shape)], scratch, args, (), (3, 4, 5, 6), 4
+            )
         else:
-            coarse, to_a, to_b, mfx, mlev, err = call(mid, outs, scratch, [*args, mtens])
+            coarse, to_a, to_b, mfx, mlev, err = call(mid, outs, scratch, [*args, mtens], (7,), (3, 4, 5), 4)
         edges = [across(to_a, GY, 0), across(to_b, GY, 1)]
         whole = shared(coarse, GY).reshape(32 * count, 128)
         args = [par, whole, mfx, mlev, err, *edges]
         outs = [(2, 12, 4, 128)]
         scratch = [(3, 18, MROWS, 128), (3, 18, MROWS, 128), (6, 3 * MROWS, 128)]
+        inverse = (6, 32, 128)
         low = functools.partial(coarse_kernel, first)
         if first:
-            error, cinv = call(low, [*outs, (6, 32, 128)], scratch, args)
+            error, cinv = call(low, [*outs, inverse], [*saved, inverse, *scratch], args, (2, 3, 4), (1,), 4)
         else:
-            (error,) = call(low, outs, scratch, [*args, cinv])
+            (error,) = call(low, outs, [*saved, *scratch], [*args, cinv], (2, 3, 4), (), 4)
         args = [par, flow, *layers, *edges, error, *beside(error, GY), lev, tens]
-        scratch = [(3, *fine_shape), (3, *fine_shape), (3, 12, 16, 128), (3, 12, 16, 128), (3, 12, 24, 128)]
-        (flow,) = call(post_kernel, [(3, 8, 8, 128)], scratch, args)
+        scratch = [(9, *fine_shape), (9, *fine_shape), (3, *fine_shape), (3, *fine_shape)]
+        scratch += [(3, 12, 16, 128), (3, 12, 16, 128), (3, 12, 24, 128)]
+        (flow,) = call(post_kernel, [(3, 8, 8, 128)], scratch, args, (9, 10), (), 2)
     return flow
 
 

time: 235 us -> 188 us (0.80)
  Pallas kernels: 69.4 us -> 37.6 us
  local copies, waits for them, and re-layouts: 14.3 us -> 0.01 us
    pallas_call x10, Pallas kernels: 69.4 us -> 37.6 us  [call(): pl.pallas_call(kernel, in_specs=specs, out_specs=[far if k in far_out els...]
    unnamed x40 -> x2, local copies, waits for them, and re-layouts: 14.3 us -> 0.01 us
where the time goes in v1:
time: 188 us; the launch traced here: 187 us
  starting transfers between devices  70.1 us (37%)
  waiting for transfers between devices  55.9 us (30%)
  Pallas kernels  37.6 us (20%)
  blocking collectives  21.6 us (11%)
    ppermute x24, waiting for transfers between devices, across(): return lax.ppermute(field, axes, pairs_of(lax.axis_size(axes), start))  55.9 us
    ppermute x24, starting transfers between devices, across(): return lax.ppermute(field, axes, pairs_of(lax.axis_size(axes), start))  53.8 us
    pallas_call x10, Pallas kernels, call(): pl.pallas_call(kernel, in_specs=specs, out_specs=[far if k in far_out els...  37.6 us
    all_to_all x2, blocking collectives, shared(): return lax.all_to_all(message, axes, 0, 0, tiled=True)  21.6 us
    all_to_all x2, starting transfers between devices, shared(): return lax.all_to_all(message, axes, 0, 0, tiled=True)  16.3 us
  transfers between devices with their start and end apart: 26, of which 15 were waited for; matrix products, arithmetic and copies ran while one was open for 0% of the time, Pallas kernels for 0%

profile of v1, /device:TPU:122, one launch (start us, length us, event | category | flops | bytes accessed | tf_op | source)
XLA Modules:
  0.0 186.7 jit_solution(15878512189088489365)
XLA Ops:
  8.2 4.7 %collective-permute-start.3 = (f32[5,20,8,128]{3,2,1,0:T(8,128)S(1)}, f32[5,20,8,128]{3,2,1,0:T(8,128)S(1)}, u32[]{:S(2)}, u32[]{:S(2)}) collective-permute-start(f32[5,20,8,128]{3,2,1,0:T(8,128)S(1)} %shard_map.37.refs_1_), channel_id=1, source_target_pairs={{1,2},{2,1},{3,4},{4,3},{5,6},{6,5},{7,8},{8,7},{9,10},{10,9},{11,... | collective-permute-start | bytes 1228808 | tf_op jit(solution)/shard_map/ppermute | solution.py:649
  13.0 11.9 %collective-permute-done.3.refs_3_ = f32[5,20,8,128]{3,2,1,0:T(8,128)S(1)} collective-permute-done((f32[5,20,8,128]{3,2,1,0:T(8,128)S(1)}, f32[5,20,8,128]{3,2,1,0:T(8,128)S(1)}, u32[]{:S(2)}, u32[]{:S(2)}) %collective-permute-start.3) | collective-permute-done | bytes 409632 | tf_op jit(solution)/shard_map/ppermute | solution.py:649
  24.9 5.3 %shard_map.38 = (f32[3,8,8,128]{3,2,1,0:T(8,128)S(1)}, f32[8,88,128]{2,1,0:T(8,128)S(1)}, f32[9,20,24,128]{3,2,1,0:T(8,128)}, f32[9,20,24,128]{3,2,1,0:T(8,128)}) custom-call(s32[2]{0:T(128)S(1)} %pad_add_fusion.par.refs_0_, f32[5,20,8,128]{3,2,1,0:T(8,128)S(1)} %shard_map.37.refs_1_, f32[5,20,8,128]{3,2,1,0:T(8,128)S(1)} %collective-permute-done.2.refs_2_, ...), custom_call_target="tpu_custom_call" | custom-call | flops 20000000 | bytes 1000000 | tf_op jit(solution)/shard_map/pallas_call | solution.py:630
  30.2 11.7 %all_to_all.20.refs_1_ = f32[8,88,128]{2,1,0:T(8,128)S(1)} all-to-all(f32[8,88,128]{2,1,0:T(8,128)S(1)} %get-tuple-element.28), channel_id=1, replica_groups=mesh['gx_0'=4,'gx_1'=2,'gy_0'=8,'gy_1'=4] {'gx_0','gx_1'}, dimensions={0} | all-to-all | bytes 720896 | tf_op jit(solution)/shard_map/all_to_all | solution.py:657
  41.9 4.7 %collective-permute-start.7 = (f32[8,88,128]{2,1,0:T(8,128)S(1)}, f32[8,88,128]{2,1,0:T(8,128)S(1)}, u32[]{:S(2)}, u32[]{:S(2)}) collective-permute-start(f32[8,88,128]{2,1,0:T(8,128)S(1)} %all_to_all.20.refs_1_), channel_id=1, source_target_pairs={{1,2},{2,1},{3,4},{4,3},{5,6},{6,5},{7,8},{8,7},{9,10},{10,9},{11,... | collective-permute-start | bytes 1081352 | tf_op jit(solution)/shard_map/ppermute | solution.py:649
  52.7 4.5 %collective-permute-done.7.refs_3_ = f32[8,88,128]{2,1,0:T(8,128)S(1)} collective-permute-done((f32[8,88,128]{2,1,0:T(8,128)S(1)}, f32[8,88,128]{2,1,0:T(8,128)S(1)}, u32[]{:S(2)}, u32[]{:S(2)}) %collective-permute-start.7) | collective-permute-done | bytes 360480 | tf_op jit(solution)/shard_map/ppermute | solution.py:649
  61.1 7.5 %all-to-all-start.1 = ((f32[32,16,128]{2,1,0:T(8,128)}), f32[32,16,128]{2,1,0:T(8,128)S(1)}, u32[]{:S(2)}, u32[]{:S(2)}) async-start(f32[32,16,128]{2,1,0:T(8,128)} %get-tuple-element.31), calls=%async_computation.1 | async-start | bytes 524288 | tf_op jit(solution)/shard_map/all_to_all | solution.py:657
  69.6 5.2 %collective-permute-start.9 = (f32[6,16,4,128]{3,2,1,0:T(4,128)S(1)}, f32[6,16,4,128]{3,2,1,0:T(4,128)S(1)}, u32[]{:S(2)}, u32[]{:S(2)}) collective-permute-start(f32[6,16,4,128]{3,2,1,0:T(4,128)S(1)} %get-tuple-element.30), channel_id=1, source_target_pairs={{1,2},{2,1},{3,4},{4,3},{5,6},{6,5},{7,8},{8,7},{9,10},{10,9},{11,... | collective-permute-start | bytes 589832 | tf_op jit(solution)/shard_map/ppermute | solution.py:649
  76.3 4.2 %collective-permute-done.9.refs_6_.yb = f32[6,16,4,128]{3,2,1,0:T(4,128)S(1)} collective-permute-done((f32[6,16,4,128]{3,2,1,0:T(4,128)S(1)}, f32[6,16,4,128]{3,2,1,0:T(4,128)S(1)}, u32[]{:S(2)}, u32[]{:S(2)}) %collective-permute-start.9) | collective-permute-done | bytes 196640 | tf_op jit(solution)/shard_map/ppermute | solution.py:649
  80.5 4.1 %shard_map.40 = (f32[2,12,4,128]{3,2,1,0:T(4,128)S(1)}, f32[6,32,128]{2,1,0:T(8,128)}) custom-call(s32[2]{0:T(128)S(1)} %pad_add_fusion.par.refs_0_, f32[512,128]{1,0:T(8,128)S(1)} %bitcast.6, f32[17,16,128]{2,1,0:T(8,128)} %get-tuple-element.32.refs_2_, f32[11,16,16,128]{3,2,1,0:T(8,128)} %get-tuple-element.33.refs_3_, ...), custom_call_target="tpu_custom_call" | custom-call | flops 20000000 | bytes 1000000 | tf_op jit(solution)/shard_map/pallas_call | solution.py:630
  84.7 5.1 %collective-permute-start.11 = (f32[2,12,4,128]{3,2,1,0:T(4,128)S(1)}, f32[2,12,4,128]{3,2,1,0:T(4,128)S(1)}, u32[]{:S(2)}, u32[]{:S(2)}) collective-permute-start(f32[2,12,4,128]{3,2,1,0:T(4,128)S(1)} %get-tuple-element.35.mine), channel_id=1, source_target_pairs={{1,2},{2,1},{3,4},{4,3},{5,6},{6,5},{7,8},{8,7},{9,10},{10,9},{11,... | collective-permute-start | bytes 147464 | tf_op jit(solution)/shard_map/ppermute | solution.py:649
  104.4 5.1 %collective-permute-start.15 = (f32[3,20,8,128]{3,2,1,0:T(8,128)S(1)}, f32[3,20,8,128]{3,2,1,0:T(8,128)S(1)}, u32[]{:S(2)}, u32[]{:S(2)}) collective-permute-start(f32[3,20,8,128]{3,2,1,0:T(8,128)S(1)} %shard_map.42.refs_1_), channel_id=1, source_target_pairs={{1,2},{2,1},{3,4},{4,3},{5,6},{6,5},{7,8},{8,7},{9,10},{10,9},{11,... | collective-permute-start | bytes 737288 | tf_op jit(solution)/shard_map/ppermute | solution.py:649
  109.5 6.7 %collective-permute-done.15.refs_3_ = f32[3,20,8,128]{3,2,1,0:T(8,128)S(1)} collective-permute-done((f32[3,20,8,128]{3,2,1,0:T(8,128)S(1)}, f32[3,20,8,128]{3,2,1,0:T(8,128)S(1)}, u32[]{:S(2)}, u32[]{:S(2)}) %collective-permute-start.15) | collective-permute-done | bytes 245792 | tf_op jit(solution)/shard_map/ppermute | solution.py:649
  116.3 5.8 %shard_map.43 = (f32[3,8,8,128]{3,2,1,0:T(8,128)S(1)}, f32[8,40,128]{2,1,0:T(8,128)S(1)}, f32[9,20,24,128]{3,2,1,0:T(8,128)}) custom-call(s32[2]{0:T(128)S(1)} %pad_add_fusion.par.refs_0_, f32[3,20,8,128]{3,2,1,0:T(8,128)S(1)} %shard_map.42.refs_1_, f32[3,20,8,128]{3,2,1,0:T(8,128)S(1)} %collective-permute-done.14.refs_2_, ...), custom_call_target="tpu_custom_call" | custom-call | flops 20000000 | bytes 1000000 | tf_op jit(solution)/shard_map/pallas_call | solution.py:630
  122.0 9.9 %all_to_all.21.refs_1_ = f32[8,40,128]{2,1,0:T(8,128)S(1)} all-to-all(f32[8,40,128]{2,1,0:T(8,128)S(1)} %get-tuple-element.39), channel_id=1, replica_groups=mesh['gx_0'=4,'gx_1'=2,'gy_0'=8,'gy_1'=4] {'gx_0','gx_1'}, dimensions={0} | all-to-all | bytes 327680 | tf_op jit(solution)/shard_map/all_to_all | solution.py:657
  131.9 4.9 %collective-permute-start.19 = (f32[8,40,128]{2,1,0:T(8,128)S(1)}, f32[8,40,128]{2,1,0:T(8,128)S(1)}, u32[]{:S(2)}, u32[]{:S(2)}) collective-permute-start(f32[8,40,128]{2,1,0:T(8,128)S(1)} %all_to_all.21.refs_1_), channel_id=1, source_target_pairs={{1,2},{2,1},{3,4},{4,3},{5,6},{6,5},{7,8},{8,7},{9,10},{10,9},{11,... | collective-permute-start | bytes 491528 | tf_op jit(solution)/shard_map/ppermute | solution.py:649
  142.9 5.3 %shard_map.44 = (f32[32,8,128]{2,1,0:T(8,128)}, f32[6,16,4,128]{3,2,1,0:T(4,128)S(1)}, f32[6,16,4,128]{3,2,1,0:T(4,128)S(1)}, f32[17,16,128]{2,1,0:T(8,128)}, f3...) custom-call(s32[2]{0:T(128)S(1)} %pad_add_fusion.par.refs_0_, f32[8,40,128]{2,1,0:T(8,128)S(1)} %all_to_all.21.refs_1_, ...), custom_call_target="tpu_custom_call" | custom-call | flops 20000000 | bytes 1000000 | tf_op jit(solution)/shard_map/pallas_call | solution.py:630
  148.2 8.8 %all-to-all-start.3 = ((f32[32,8,128]{2,1,0:T(8,128)}), f32[32,8,128]{2,1,0:T(8,128)S(1)}, u32[]{:S(2)}, u32[]{:S(2)}) async-start(f32[32,8,128]{2,1,0:T(8,128)} %get-tuple-element.43), calls=%async_computation.3 | async-start | bytes 262144 | tf_op jit(solution)/shard_map/all_to_all | solution.py:657
  158.0 5.4 %collective-permute-start.21 = (f32[6,16,4,128]{3,2,1,0:T(4,128)S(1)}, f32[6,16,4,128]{3,2,1,0:T(4,128)S(1)}, u32[]{:S(2)}, u32[]{:S(2)}) collective-permute-start(f32[6,16,4,128]{3,2,1,0:T(4,128)S(1)} %get-tuple-element.42), channel_id=1, source_target_pairs={{1,2},{2,1},{3,4},{4,3},{5,6},{6,5},{7,8},{8,7},{9,10},{10,9},{11,... | collective-permute-start | bytes 589832 | tf_op jit(solution)/shard_map/ppermute | solution.py:649
  163.8 5.0 %collective-permute-done.21.refs_6_.yb = f32[6,16,4,128]{3,2,1,0:T(4,128)S(1)} collective-permute-done((f32[6,16,4,128]{3,2,1,0:T(4,128)S(1)}, f32[6,16,4,128]{3,2,1,0:T(4,128)S(1)}, u32[]{:S(2)}, u32[]{:S(2)}) %collective-permute-start.21) | collective-permute-done | bytes 196640 | tf_op jit(solution)/shard_map/ppermute | solution.py:649
  168.8 4.1 %shard_map.45.mine = f32[2,12,4,128]{3,2,1,0:T(4,128)S(1)} custom-call(s32[2]{0:T(128)S(1)} %pad_add_fusion.par.refs_0_, f32[256,128]{1,0:T(8,128)S(1)} %bitcast.7, f32[17,16,128]{2,1,0:T(8,128)} %get-tuple-element.44.refs_2_, f32[11,16,16,128]{3,2,1,0:T(8,128)} %get-tuple-element.45.refs_3_, f32[3,18,16,128]{3,2,1,0:T(8,128)} %get-tuple-element.46.refs_4_, ...), custom_call_target="tpu_custom_call" | custom-call | flops 20000000 | bytes 1000000 | tf_op jit(solution)/shard_map/pallas_call | solution.py:630
  172.9 5.2 %collective-permute-start.23 = (f32[2,12,4,128]{3,2,1,0:T(4,128)S(1)}, f32[2,12,4,128]{3,2,1,0:T(4,128)S(1)}, u32[]{:S(2)}, u32[]{:S(2)}) collective-permute-start(f32[2,12,4,128]{3,2,1,0:T(4,128)S(1)} %shard_map.45.mine), channel_id=1, source_target_pairs={{1,2},{2,1},{3,4},{4,3},{5,6},{6,5},{7,8},{8,7},{9,10},{10,9},{11,... | collective-permute-start | bytes 147464 | tf_op jit(solution)/shard_map/ppermute | solution.py:649
  178.2 4.0 %collective-permute-done.23.eb = f32[2,12,4,128]{3,2,1,0:T(4,128)S(1)} collective-permute-done((f32[2,12,4,128]{3,2,1,0:T(4,128)S(1)}, f32[2,12,4,128]{3,2,1,0:T(4,128)S(1)}, u32[]{:S(2)}, u32[]{:S(2)}) %collective-permute-start.23) | collective-permute-done | bytes 49184 | tf_op jit(solution)/shard_map/ppermute | solution.py:649
  182.3 4.3 %shard_map.46 = f32[3,8,8,128]{3,2,1,0:T(8,128)} custom-call(s32[2]{0:T(128)S(1)} %pad_add_fusion.par.refs_0_, f32[3,8,8,128]{3,2,1,0:T(8,128)S(1)} %get-tuple-element.38.refs_4_.flow, f32[3,8,8,128]{3,2,1,0:T(8,128)S(1)} %collective-permute-done.16.refs_5_.fa, f32[3,8,8,128]{3,2,1,0:T(8,128)S(1)} %collective-permute-done.17.refs_6_.fb, ...), custom_call_target="tpu_custom_call" | custom-call | flops 20000000 | bytes 1000000 | tf_op jit(solution)/shard_map/pallas_call | solution.py:630
  (44 shorter events, 42.9 us)
Async XLA Ops:
  0.9 6.6 %collective-permute-start.1 = (f32[5,8,8,128]{3,2,1,0:T(8,128)S(1)}, f32[5,8,8,128]{3,2,1,0:T(8,128)S(1)}, u32[]{:S(2)}, u32[]{:S(2)}) collective-permute-start(f32[5,8,8,128]{3,2,1,0:T(8,128)S(1)} %pad_maximum_fusion.own), channel_id=1, source_target_pairs={{32,64},{64,32},{96,128},{128,96},{160,192},{192,160},{33,65},{65,... | collective-permute-start | bytes 491528 | tf_op jit(solution)/shard_map/ppermute | solution.py:649
  2.9 4.7 %collective-permute-start = (f32[5,8,8,128]{3,2,1,0:T(8,128)S(1)}, f32[5,8,8,128]{3,2,1,0:T(8,128)S(1)}, u32[]{:S(2)}, u32[]{:S(2)}) collective-permute-start(f32[5,8,8,128]{3,2,1,0:T(8,128)S(1)} %pad_maximum_fusion.own), channel_id=1, source_target_pairs={{0,32},{32,0},{64,96},{96,64},{128,160},{160,128},{192,224},{224,1... | collective-permute-start | bytes 491528 | tf_op jit(solution)/shard_map/ppermute | solution.py:649
  8.2 16.7 %collective-permute-start.3 = (f32[5,20,8,128]{3,2,1,0:T(8,128)S(1)}, f32[5,20,8,128]{3,2,1,0:T(8,128)S(1)}, u32[]{:S(2)}, u32[]{:S(2)}) collective-permute-start(f32[5,20,8,128]{3,2,1,0:T(8,128)S(1)} %shard_map.37.refs_1_), channel_id=1, source_target_pairs={{1,2},{2,1},{3,4},{4,3},{5,6},{6,5},{7,8},{8,7},{9,10},{10,9},{11,... | collective-permute-start | bytes 1228808 | tf_op jit(solution)/shard_map/ppermute | solution.py:649
  12.9 12.0 %collective-permute-start.2 = (f32[5,20,8,128]{3,2,1,0:T(8,128)S(1)}, f32[5,20,8,128]{3,2,1,0:T(8,128)S(1)}, u32[]{:S(2)}, u32[]{:S(2)}) collective-permute-start(f32[5,20,8,128]{3,2,1,0:T(8,128)S(1)} %shard_map.37.refs_1_), channel_id=1, source_target_pairs={{0,1},{1,0},{2,3},{3,2},{4,5},{5,4},{6,7},{7,6},{8,9},{9,8},{10,11... | collective-permute-start | bytes 1228808 | tf_op jit(solution)/shard_map/ppermute | solution.py:649
  41.9 15.2 %collective-permute-start.7 = (f32[8,88,128]{2,1,0:T(8,128)S(1)}, f32[8,88,128]{2,1,0:T(8,128)S(1)}, u32[]{:S(2)}, u32[]{:S(2)}) collective-permute-start(f32[8,88,128]{2,1,0:T(8,128)S(1)} %all_to_all.20.refs_1_), channel_id=1, source_target_pairs={{1,2},{2,1},{3,4},{4,3},{5,6},{6,5},{7,8},{8,7},{9,10},{10,9},{11,... | collective-permute-start | bytes 1081352 | tf_op jit(solution)/shard_map/ppermute | solution.py:649
  46.6 10.5 %collective-permute-start.6 = (f32[8,88,128]{2,1,0:T(8,128)S(1)}, f32[8,88,128]{2,1,0:T(8,128)S(1)}, u32[]{:S(2)}, u32[]{:S(2)}) collective-permute-start(f32[8,88,128]{2,1,0:T(8,128)S(1)} %all_to_all.20.refs_1_), channel_id=1, source_target_pairs={{0,1},{1,0},{2,3},{3,2},{4,5},{5,4},{6,7},{7,6},{8,9},{9,8},{10,11... | collective-permute-start | bytes 1081352 | tf_op jit(solution)/shard_map/ppermute | solution.py:649
  46.7 5.9 %collective-permute-start.5 = (f32[3,8,8,128]{3,2,1,0:T(8,128)S(1)}, f32[3,8,8,128]{3,2,1,0:T(8,128)S(1)}, u32[]{:S(2)}, u32[]{:S(2)}) collective-permute-start(f32[3,8,8,128]{3,2,1,0:T(8,128)S(1)} %get-tuple-element.27.refs_4_.flow), channel_id=1, source_target_pairs={{32,64},{64,32},{96,128},{128,96},{160,192},{192,160},{33,65},{65,... | collective-permute-start | bytes 294920 | tf_op jit(solution)/shard_map/ppermute | solution.py:649
  61.1 19.4 %all-to-all-start.1 = ((f32[32,16,128]{2,1,0:T(8,128)}), f32[32,16,128]{2,1,0:T(8,128)S(1)}, u32[]{:S(2)}, u32[]{:S(2)}) async-start(f32[32,16,128]{2,1,0:T(8,128)} %get-tuple-element.31), calls=%async_computation.1 | async-start | bytes 524288 | tf_op jit(solution)/shard_map/all_to_all | solution.py:657
  68.7 7.6 %collective-permute-start.8 = (f32[6,16,4,128]{3,2,1,0:T(4,128)S(1)}, f32[6,16,4,128]{3,2,1,0:T(4,128)S(1)}, u32[]{:S(2)}, u32[]{:S(2)}) collective-permute-start(f32[6,16,4,128]{3,2,1,0:T(4,128)S(1)} %get-tuple-element.29), channel_id=1, source_target_pairs={{0,1},{1,0},{2,3},{3,2},{4,5},{5,4},{6,7},{7,6},{8,9},{9,8},{10,11... | collective-permute-start | bytes 589832 | tf_op jit(solution)/shard_map/ppermute | solution.py:649
  69.6 10.9 %collective-permute-start.9 = (f32[6,16,4,128]{3,2,1,0:T(4,128)S(1)}, f32[6,16,4,128]{3,2,1,0:T(4,128)S(1)}, u32[]{:S(2)}, u32[]{:S(2)}) collective-permute-start(f32[6,16,4,128]{3,2,1,0:T(4,128)S(1)} %get-tuple-element.30), channel_id=1, source_target_pairs={{1,2},{2,1},{3,4},{4,3},{5,6},{6,5},{7,8},{8,7},{9,10},{10,9},{11,... | collective-permute-start | bytes 589832 | tf_op jit(solution)/shard_map/ppermute | solution.py:649
  84.7 9.3 %collective-permute-start.11 = (f32[2,12,4,128]{3,2,1,0:T(4,128)S(1)}, f32[2,12,4,128]{3,2,1,0:T(4,128)S(1)}, u32[]{:S(2)}, u32[]{:S(2)}) collective-permute-start(f32[2,12,4,128]{3,2,1,0:T(4,128)S(1)} %get-tuple-element.35.mine), channel_id=1, source_target_pairs={{1,2},{2,1},{3,4},{4,3},{5,6},{6,5},{7,8},{8,7},{9,10},{10,9},{11,... | collective-permute-start | bytes 147464 | tf_op jit(solution)/shard_map/ppermute | solution.py:649
  89.8 4.4 %collective-permute-start.10 = (f32[2,12,4,128]{3,2,1,0:T(4,128)S(1)}, f32[2,12,4,128]{3,2,1,0:T(4,128)S(1)}, u32[]{:S(2)}, u32[]{:S(2)}) collective-permute-start(f32[2,12,4,128]{3,2,1,0:T(4,128)S(1)} %get-tuple-element.35.mine), channel_id=1, source_target_pairs={{0,1},{1,0},{2,3},{3,2},{4,5},{5,4},{6,7},{7,6},{8,9},{9,8},{10,11... | collective-permute-start | bytes 147464 | tf_op jit(solution)/shard_map/ppermute | solution.py:649
  97.8 5.9 %collective-permute-start.13 = (f32[3,8,8,128]{3,2,1,0:T(8,128)S(1)}, f32[3,8,8,128]{3,2,1,0:T(8,128)S(1)}, u32[]{:S(2)}, u32[]{:S(2)}) collective-permute-start(f32[3,8,8,128]{3,2,1,0:T(8,128)S(1)} %shard_map.41.own), channel_id=1, source_target_pairs={{32,64},{64,32},{96,128},{128,96},{160,192},{192,160},{33,65},{65,... | collective-permute-start | bytes 294920 | tf_op jit(solution)/shard_map/ppermute | solution.py:649
  99.8 4.0 %collective-permute-start.12 = (f32[3,8,8,128]{3,2,1,0:T(8,128)S(1)}, f32[3,8,8,128]{3,2,1,0:T(8,128)S(1)}, u32[]{:S(2)}, u32[]{:S(2)}) collective-permute-start(f32[3,8,8,128]{3,2,1,0:T(8,128)S(1)} %shard_map.41.own), channel_id=1, source_target_pairs={{0,32},{32,0},{64,96},{96,64},{128,160},{160,128},{192,224},{224,1... | collective-permute-start | bytes 294920 | tf_op jit(solution)/shard_map/ppermute | solution.py:649
  104.4 11.9 %collective-permute-start.15 = (f32[3,20,8,128]{3,2,1,0:T(8,128)S(1)}, f32[3,20,8,128]{3,2,1,0:T(8,128)S(1)}, u32[]{:S(2)}, u32[]{:S(2)}) collective-permute-start(f32[3,20,8,128]{3,2,1,0:T(8,128)S(1)} %shard_map.42.refs_1_), channel_id=1, source_target_pairs={{1,2},{2,1},{3,4},{4,3},{5,6},{6,5},{7,8},{8,7},{9,10},{10,9},{11,... | collective-permute-start | bytes 737288 | tf_op jit(solution)/shard_map/ppermute | solution.py:649
  109.5 6.8 %collective-permute-start.14 = (f32[3,20,8,128]{3,2,1,0:T(8,128)S(1)}, f32[3,20,8,128]{3,2,1,0:T(8,128)S(1)}, u32[]{:S(2)}, u32[]{:S(2)}) collective-permute-start(f32[3,20,8,128]{3,2,1,0:T(8,128)S(1)} %shard_map.42.refs_1_), channel_id=1, source_target_pairs={{0,1},{1,0},{2,3},{3,2},{4,5},{5,4},{6,7},{7,6},{8,9},{9,8},{10,11... | collective-permute-start | bytes 737288 | tf_op jit(solution)/shard_map/ppermute | solution.py:649
  131.9 11.0 %collective-permute-start.19 = (f32[8,40,128]{2,1,0:T(8,128)S(1)}, f32[8,40,128]{2,1,0:T(8,128)S(1)}, u32[]{:S(2)}, u32[]{:S(2)}) collective-permute-start(f32[8,40,128]{2,1,0:T(8,128)S(1)} %all_to_all.21.refs_1_), channel_id=1, source_target_pairs={{1,2},{2,1},{3,4},{4,3},{5,6},{6,5},{7,8},{8,7},{9,10},{10,9},{11,... | collective-permute-start | bytes 491528 | tf_op jit(solution)/shard_map/ppermute | solution.py:649
  136.8 6.0 %collective-permute-start.18 = (f32[8,40,128]{2,1,0:T(8,128)S(1)}, f32[8,40,128]{2,1,0:T(8,128)S(1)}, u32[]{:S(2)}, u32[]{:S(2)}) collective-permute-start(f32[8,40,128]{2,1,0:T(8,128)S(1)} %all_to_all.21.refs_1_), channel_id=1, source_target_pairs={{0,1},{1,0},{2,3},{3,2},{4,5},{5,4},{6,7},{7,6},{8,9},{9,8},{10,11... | collective-permute-start | bytes 491528 | tf_op jit(solution)/shard_map/ppermute | solution.py:649
  136.9 5.9 %collective-permute-start.17 = (f32[3,8,8,128]{3,2,1,0:T(8,128)S(1)}, f32[3,8,8,128]{3,2,1,0:T(8,128)S(1)}, u32[]{:S(2)}, u32[]{:S(2)}) collective-permute-start(f32[3,8,8,128]{3,2,1,0:T(8,128)S(1)} %get-tuple-element.38.refs_4_.flow), channel_id=1, source_target_pairs={{32,64},{64,32},{96,128},{128,96},{160,192},{192,160},{33,65},{65,... | collective-permute-start | bytes 294920 | tf_op jit(solution)/shard_map/ppermute | solution.py:649
  148.2 20.6 %all-to-all-start.3 = ((f32[32,8,128]{2,1,0:T(8,128)}), f32[32,8,128]{2,1,0:T(8,128)S(1)}, u32[]{:S(2)}, u32[]{:S(2)}) async-start(f32[32,8,128]{2,1,0:T(8,128)} %get-tuple-element.43), calls=%async_computation.3 | async-start | bytes 262144 | tf_op jit(solution)/shard_map/all_to_all | solution.py:657
  157.0 6.8 %collective-permute-start.20 = (f32[6,16,4,128]{3,2,1,0:T(4,128)S(1)}, f32[6,16,4,128]{3,2,1,0:T(4,128)S(1)}, u32[]{:S(2)}, u32[]{:S(2)}) collective-permute-start(f32[6,16,4,128]{3,2,1,0:T(4,128)S(1)} %get-tuple-element.41), channel_id=1, source_target_pairs={{0,1},{1,0},{2,3},{3,2},{4,5},{5,4},{6,7},{7,6},{8,9},{9,8},{10,11... | collective-permute-start | bytes 589832 | tf_op jit(solution)/shard_map/ppermute | solution.py:649
  158.0 10.9 %collective-permute-start.21 = (f32[6,16,4,128]{3,2,1,0:T(4,128)S(1)}, f32[6,16,4,128]{3,2,1,0:T(4,128)S(1)}, u32[]{:S(2)}, u32[]{:S(2)}) collective-permute-start(f32[6,16,4,128]{3,2,1,0:T(4,128)S(1)} %get-tuple-element.42), channel_id=1, source_target_pairs={{1,2},{2,1},{3,4},{4,3},{5,6},{6,5},{7,8},{8,7},{9,10},{10,9},{11,... | collective-permute-start | bytes 589832 | tf_op jit(solution)/shard_map/ppermute | solution.py:649
  172.9 9.3 %collective-permute-start.23 = (f32[2,12,4,128]{3,2,1,0:T(4,128)S(1)}, f32[2,12,4,128]{3,2,1,0:T(4,128)S(1)}, u32[]{:S(2)}, u32[]{:S(2)}) collective-permute-start(f32[2,12,4,128]{3,2,1,0:T(4,128)S(1)} %shard_map.45.mine), channel_id=1, source_target_pairs={{1,2},{2,1},{3,4},{4,3},{5,6},{6,5},{7,8},{8,7},{9,10},{10,9},{11,... | collective-permute-start | bytes 147464 | tf_op jit(solution)/shard_map/ppermute | solution.py:649
  178.1 4.2 %collective-permute-start.22 = (f32[2,12,4,128]{3,2,1,0:T(4,128)S(1)}, f32[2,12,4,128]{3,2,1,0:T(4,128)S(1)}, u32[]{:S(2)}, u32[]{:S(2)}) collective-permute-start(f32[2,12,4,128]{3,2,1,0:T(4,128)S(1)} %shard_map.45.mine), channel_id=1, source_target_pairs={{0,1},{1,0},{2,3},{3,2},{4,5},{5,4},{6,7},{7,6},{8,9},{9,8},{10,11... | collective-permute-start | bytes 147464 | tf_op jit(solution)/shard_map/ppermute | solution.py:649
  (3 other events, 71.7 us)

commit v2 on v1

--- a/solution.py
+++ b/solution.py
@@ -121,28 +121,39 @@
     loop(low, high, turn)
 
 
-def widen_kernel(layers, par, own, xa, xb, out):
-    shape = (8, 128)
-    low_of, high_of = sides(par, 0, shape)
+def widen_kernel(par, own, xa, xb, wide, to_a, to_b):
+    low_of, high_of = sides(par, 0, (8, 128))
+    first_of, second_of = sides(par, 1, (4, 128))
     for f in range(own.shape[0]):
-        for k in range(layers):
-            out[f, k] = low_of(xa[f, 8 - layers + k], xb[f, 8 - layers + k])
-            out[f, layers + 8 + k] = high_of(xa[f, k], xb[f, k])
-        for k in range(8):
-            out[f, layers + k] = own[f, k]
-
-
-def stack_rows(par, own, ya, yb, out, fields):
-    low_of, high_of = sides(par, 1, (8, 128))
-
-    def turn(x):
-        for f in range(fields):
-            a, b = ya[f, x], yb[f, x]
-            out[f, x, 0:8] = low_of(a, b)
+        for x in range(WIDE):
+            if x < 6:
+                v = low_of(xa[f, 2 + x], xb[f, 2 + x])
+            elif x < 14:
+                v = own[f, x - 6]
+            else:
+                v = high_of(xa[f, x - 14], xb[f, x - 14])
+            wide[f, x] = v
+            below, above = v[0:4], v[4:8]
+            if 1 <= x < 19:
+                to_a[f, x - 1] = first_of(below, above)
+                to_b[f, x - 1] = second_of(below, above)
+            if 5 <= x < 15:
+                to_a[f, 13 + x] = first_of(above, below)
+                to_b[f, 13 + x] = second_of(above, below)
+
+
+def stack_rows(par, own, ya, yb, out):
+    low_of, high_of = sides(par, 1, (4, 128))
+    zero = jnp.zeros((4, 128), jnp.float32)
+    for f in range(own.shape[0]):
+        for x in range(WIDE):
             out[f, x, 8:16] = own[f, x]
-            out[f, x, 16:24] = high_of(a, b)
-
-    loop(0, own.shape[1], turn)
+            near = (ya[f, x - 1], yb[f, x - 1]) if 1 <= x < 19 else (zero, zero)
+            far = (ya[f, 13 + x], yb[f, 13 + x]) if 5 <= x < 15 else (zero, zero)
+            out[f, x, 0:4] = low_of(*far)
+            out[f, x, 4:8] = low_of(*near)
+            out[f, x, 16:20] = high_of(*near)
+            out[f, x, 20:24] = high_of(*far)
 
 
 def pre_kernel(first, *refs):
@@ -150,11 +161,12 @@
         par, own, ya, yb, flow_out, msg, lev_far, tens_far, lev, tens, u0, u1, w, even, odd, sums, sems = refs
     else:
         par, own, ya, yb, tens_far, flow_out, msg, lev_far, lev, tens, u0, u1, w, even, odd, sums, sems = refs
-        (tens_copy,) = moved([(tens_far, tens)], sems)
+        parts = [(tens_far.at[k, 2:18], tens.at[k, 2:18]) for k in (slice(0, 6), slice(6, 9))]
+        tens_copy, source_copy = moved(parts, sems)
     shape = (ROWS, 128)
     lane = iota(shape, 1)
     last, start = lane == 127, lane == 0
-    stack_rows(par, own, ya, yb, u0, own.shape[0])
+    stack_rows(par, own, ya, yb, u0)
 
     def z_slope(v):
         return jnp.where(last, 0.0, roll(v, -1, 1)) - jnp.where(start, 0.0, roll(v, 1, 1))
@@ -211,6 +223,8 @@
             lev[3 + k, x] = v
 
     loop(2, 18, inverse_turn)
+    if not first:
+        source_copy.wait()
     far = [(lev, lev_far), (tens, tens_far)] if first else [(lev, lev_far)]
     copies = moved(far, sems)
     bufs = (u0, u1)
@@ -459,6 +473,7 @@
     value = mixed[0:count]
     for a in range(1, 4):
         value = value + roll(mixed[a * count : (a + 1) * count], 16 * a, 1)
+    value = value[0 : msg.shape[1]]
     for s in range(32):
         msg[s] = value
     for copy in [*copies, err_copy]:
@@ -556,7 +571,9 @@
 
 
 def post_kernel(par, flow, fa, fb, ya, yb, mine, ea, eb, lev_far, tens_far, out, lev, tens, u0, u1, mixed, lifted, tall, sems):
-    copies = moved([(lev_far, lev), (tens_far.at[6:9], tens.at[6:9])], sems)
+    copies = moved(
+        [(lev_far.at[:, 2:17], lev.at[:, 2:17]), (tens_far.at[6:9, 3:17], tens.at[6:9, 3:17])], sems
+    )
     low_of, high_of = sides(par, 1, (4, 128))
     zero = jnp.zeros((4, 128), jnp.float32)
 
@@ -668,13 +685,14 @@
         sent = block if first else flow
         fields = sent.shape[0]
         args = [par, sent, *beside(sent, GX)]
-        (wide,) = call(functools.partial(widen_kernel, 6), [(fields, WIDE, 8, 128)], [], args)
+        outs = [(fields, WIDE, 8, 128), (fields, 28, 4, 128), (fields, 28, 4, 128)]
+        wide, to_a, to_b = call(widen_kernel, outs, [], args)
         size = 88 if first else 40
         stage = (6 if first else 3) * 32
         outs = [(3, 8, 8, 128), (8, size, 128), (9, *fine_shape)]
         scratch = [(9, *fine_shape), (9, *fine_shape), (fields, *fine_shape), (3, *fine_shape), fine_shape]
         scratch += [(stage, 128)] * 3
-        args = [par, wide, *beside(wide, GY)]
+        args = [par, wide, across(to_a, GY, 0), across(to_b, GY, 1)]
         pre = functools.partial(pre_kernel, first)
         if first:
             flow, message, lev, tens = call(pre, [*outs, (9, *fine_shape)], scratch, args, (), (2, 3), 2)
@@ -683,11 +701,11 @@
         layers = beside(flow, GX)
         mids = shared(message, GX)
         args = [par, mids, *beside(mids, GY), flow, *layers]
-        count = 16 if first else 8
+        count, padded = (12, 16) if first else (4, 8)
         sides_shape = (6, 16, 4, 128)
         saved = [(17, MROWS, 128), (11, *mid_shape), (3, 18, MROWS, 128)]
         outs = [(32, count, 128), sides_shape, sides_shape, *saved]
-        scratch = [*saved, (6, *mid_shape), (3, 18, MROWS, 128), mid_shape, (4 * count, 128)]
+        scratch = [*saved, (6, *mid_shape), (3, 18, MROWS, 128), mid_shape, (4 * padded, 128)]
         mid = functools.partial(mid_kernel, first)
         if first:
             coarse, to_a, to_b, mfx, mlev, err, mtens = call(

time: 188 us -> 186 us (0.989)
  the two profiles are of different devices: /device:TPU:122 before, /device:TPU:32 now
where the time goes in v2:
time: 186 us; the launch traced here: 185 us
  starting transfers between devices  57.7 us (31%)
  blocking collectives  45 us (24%)
  waiting for transfers between devices  44.3 us (24%)
  Pallas kernels  36.6 us (20%)
    ppermute x24, starting transfers between devices, across(): return lax.ppermute(field, axes, pairs_of(lax.axis_size(axes), start))  46.5 us
    all_to_all x3, blocking collectives, shared(): return lax.all_to_all(message, axes, 0, 0, tiled=True)  45 us
    ppermute x24, waiting for transfers between devices, across(): return lax.ppermute(field, axes, pairs_of(lax.axis_size(axes), start))  38.6 us
    pallas_call x10, Pallas kernels, call(): pl.pallas_call(kernel, in_specs=specs, out_specs=[far if k in far_out els...  36.6 us
    all_to_all x1, starting transfers between devices, shared(): return lax.all_to_all(message, axes, 0, 0, tiled=True)  11.2 us
    all_to_all x1, waiting for transfers between devices, shared(): return lax.all_to_all(message, axes, 0, 0, tiled=True)  5.75 us
  transfers between devices with their start and end apart: 25, of which 15 were waited for; matrix products, arithmetic and copies ran while one was open for 0% of the time, Pallas kernels for 0%

profile of v2, /device:TPU:32, one launch (start us, length us, event | category | flops | bytes accessed | tf_op | source)
XLA Modules:
  0.0 185.1 jit_solution(17645475691751589733)
XLA Ops:
  7.9 3.6 %collective-permute-start.3 = (f32[5,28,4,128]{3,2,1,0:T(4,128)S(1)}, f32[5,28,4,128]{3,2,1,0:T(4,128)S(1)}, u32[]{:S(2)}, u32[]{:S(2)}) collective-permute-start(f32[5,28,4,128]{3,2,1,0:T(4,128)S(1)} %get-tuple-element.35), channel_id=1, source_target_pairs={{1,2},{2,1},{3,4},{4,3},{5,6},{6,5},{7,8},{8,7},{9,10},{10,9},{11,... | collective-permute-start | bytes 860168 | tf_op jit(solution)/shard_map/ppermute | solution.py:666
  15.1 5.8 %collective-permute-done.3.refs_3_ = f32[5,28,4,128]{3,2,1,0:T(4,128)S(1)} collective-permute-done((f32[5,28,4,128]{3,2,1,0:T(4,128)S(1)}, f32[5,28,4,128]{3,2,1,0:T(4,128)S(1)}, u32[]{:S(2)}, u32[]{:S(2)}) %collective-permute-start.3) | collective-permute-done | bytes 286752 | tf_op jit(solution)/shard_map/ppermute | solution.py:666
  20.9 5.5 %shard_map.38 = (f32[3,8,8,128]{3,2,1,0:T(8,128)S(1)}, f32[8,88,128]{2,1,0:T(8,128)S(1)}, f32[9,20,24,128]{3,2,1,0:T(8,128)}, f32[9,20,24,128]{3,2,1,0:T(8,128)}) custom-call(s32[2]{0:T(128)S(1)} %pad_add_fusion.par.refs_0_, f32[5,20,8,128]{3,2,1,0:T(8,128)S(1)} %get-tuple-element.33.refs_1_, f32[5,28,4,128]{3,2,1,0:T(4,128)S(1)} %collective-permute-done.2.refs_2_, ...), custom_call_target="tpu_custom_call" | custom-call | flops 20000000 | bytes 1000000 | tf_op jit(solution)/shard_map/pallas_call | solution.py:647
  26.4 14.2 %all_to_all.20.refs_1_ = f32[8,88,128]{2,1,0:T(8,128)S(1)} all-to-all(f32[8,88,128]{2,1,0:T(8,128)S(1)} %get-tuple-element.37), channel_id=1, replica_groups=mesh['gx_0'=4,'gx_1'=2,'gy_0'=8,'gy_1'=4] {'gx_0','gx_1'}, dimensions={0} | all-to-all | bytes 720896 | tf_op jit(solution)/shard_map/all_to_all | solution.py:674
  40.6 3.6 %collective-permute-start.7 = (f32[8,88,128]{2,1,0:T(8,128)S(1)}, f32[8,88,128]{2,1,0:T(8,128)S(1)}, u32[]{:S(2)}, u32[]{:S(2)}) collective-permute-start(f32[8,88,128]{2,1,0:T(8,128)S(1)} %all_to_all.20.refs_1_), channel_id=1, source_target_pairs={{1,2},{2,1},{3,4},{4,3},{5,6},{6,5},{7,8},{8,7},{9,10},{10,9},{11,... | collective-permute-start | bytes 1081352 | tf_op jit(solution)/shard_map/ppermute | solution.py:666
  48.0 6.6 %collective-permute-done.7.refs_3_ = f32[8,88,128]{2,1,0:T(8,128)S(1)} collective-permute-done((f32[8,88,128]{2,1,0:T(8,128)S(1)}, f32[8,88,128]{2,1,0:T(8,128)S(1)}, u32[]{:S(2)}, u32[]{:S(2)}) %collective-permute-start.7) | collective-permute-done | bytes 360480 | tf_op jit(solution)/shard_map/ppermute | solution.py:666
  54.6 4.0 %shard_map.39 = (f32[32,12,128]{2,1,0:T(8,128)}, f32[6,16,4,128]{3,2,1,0:T(4,128)S(1)}, f32[6,16,4,128]{3,2,1,0:T(4,128)S(1)}, f32[17,16,128]{2,1,0:T(8,128)}, f...) custom-call(s32[2]{0:T(128)S(1)} %pad_add_fusion.par.refs_0_, ...), custom_call_target="tpu_custom_call" | custom-call | flops 20000000 | bytes 1000000 | tf_op jit(solution)/shard_map/pallas_call | solution.py:647
  58.6 11.2 %all-to-all-start.1 = ((f32[32,12,128]{2,1,0:T(8,128)}), f32[32,12,128]{2,1,0:T(8,128)S(1)}, u32[]{:S(2)}, u32[]{:S(2)}) async-start(f32[32,12,128]{2,1,0:T(8,128)} %get-tuple-element.40), calls=%async_computation.1 | async-start | bytes 524288 | tf_op jit(solution)/shard_map/all_to_all | solution.py:674
  71.3 4.0 %collective-permute-start.9 = (f32[6,16,4,128]{3,2,1,0:T(4,128)S(1)}, f32[6,16,4,128]{3,2,1,0:T(4,128)S(1)}, u32[]{:S(2)}, u32[]{:S(2)}) collective-permute-start(f32[6,16,4,128]{3,2,1,0:T(4,128)S(1)} %get-tuple-element.39), channel_id=1, source_target_pairs={{1,2},{2,1},{3,4},{4,3},{5,6},{6,5},{7,8},{8,7},{9,10},{10,9},{11,... | collective-permute-start | bytes 589832 | tf_op jit(solution)/shard_map/ppermute | solution.py:666
  75.3 5.8 %all-to-all-done.1 = f32[32,12,128]{2,1,0:T(8,128)S(1)} async-done(((f32[32,12,128]{2,1,0:T(8,128)}), f32[32,12,128]{2,1,0:T(8,128)S(1)}, u32[]{:S(2)}, u32[]{:S(2)}) %all-to-all-start.1) | async-done | bytes 196640 | tf_op jit(solution)/shard_map/all_to_all | solution.py:674
  82.5 4.1 %shard_map.40 = (f32[2,12,4,128]{3,2,1,0:T(4,128)S(1)}, f32[6,32,128]{2,1,0:T(8,128)}) custom-call(s32[2]{0:T(128)S(1)} %pad_add_fusion.par.refs_0_, f32[384,128]{1,0:T(8,128)S(1)} %reshape.6.refs_1_, f32[17,16,128]{2,1,0:T(8,128)} %get-tuple-element.41.refs_2_, f32[11,16,16,128]{3,2,1,0:T(8,128)} %get-tuple-element.42.refs_3_, ...), custom_call_target="tpu_custom_call" | custom-call | flops 20000000 | bytes 1000000 | tf_op jit(solution)/shard_map/pallas_call | solution.py:647
  90.0 4.7 %collective-permute-done.11.eb = f32[2,12,4,128]{3,2,1,0:T(4,128)S(1)} collective-permute-done((f32[2,12,4,128]{3,2,1,0:T(4,128)S(1)}, f32[2,12,4,128]{3,2,1,0:T(4,128)S(1)}, u32[]{:S(2)}, u32[]{:S(2)}) %collective-permute-start.11) | collective-permute-done | bytes 49184 | tf_op jit(solution)/shard_map/ppermute | solution.py:666
  102.6 4.2 %collective-permute-start.15 = (f32[3,28,4,128]{3,2,1,0:T(4,128)S(1)}, f32[3,28,4,128]{3,2,1,0:T(4,128)S(1)}, u32[]{:S(2)}, u32[]{:S(2)}) collective-permute-start(f32[3,28,4,128]{3,2,1,0:T(4,128)S(1)} %get-tuple-element.49), channel_id=1, source_target_pairs={{1,2},{2,1},{3,4},{4,3},{5,6},{6,5},{7,8},{8,7},{9,10},{10,9},{11,... | collective-permute-start | bytes 516104 | tf_op jit(solution)/shard_map/ppermute | solution.py:666
  109.5 4.0 %collective-permute-done.15.refs_3_ = f32[3,28,4,128]{3,2,1,0:T(4,128)S(1)} collective-permute-done((f32[3,28,4,128]{3,2,1,0:T(4,128)S(1)}, f32[3,28,4,128]{3,2,1,0:T(4,128)S(1)}, u32[]{:S(2)}, u32[]{:S(2)}) %collective-permute-start.15) | collective-permute-done | bytes 172064 | tf_op jit(solution)/shard_map/ppermute | solution.py:666
  113.5 5.4 %shard_map.43 = (f32[3,8,8,128]{3,2,1,0:T(8,128)S(1)}, f32[8,40,128]{2,1,0:T(8,128)S(1)}, f32[9,20,24,128]{3,2,1,0:T(8,128)}) custom-call(s32[2]{0:T(128)S(1)} %pad_add_fusion.par.refs_0_, f32[3,20,8,128]{3,2,1,0:T(8,128)S(1)} %get-tuple-element.47.refs_1_, f32[3,28,4,128]{3,2,1,0:T(4,128)S(1)} %collective-permute-done.14.refs_2_, ...), custom_call_target="tpu_custom_call" | custom-call | flops 20000000 | bytes 1000000 | tf_op jit(solution)/shard_map/pallas_call | solution.py:647
  119.0 10.2 %all_to_all.21.refs_1_ = f32[8,40,128]{2,1,0:T(8,128)S(1)} all-to-all(f32[8,40,128]{2,1,0:T(8,128)S(1)} %get-tuple-element.51), channel_id=1, replica_groups=mesh['gx_0'=4,'gx_1'=2,'gy_0'=8,'gy_1'=4] {'gx_0','gx_1'}, dimensions={0} | all-to-all | bytes 327680 | tf_op jit(solution)/shard_map/all_to_all | solution.py:674
  129.2 4.2 %collective-permute-start.19 = (f32[8,40,128]{2,1,0:T(8,128)S(1)}, f32[8,40,128]{2,1,0:T(8,128)S(1)}, u32[]{:S(2)}, u32[]{:S(2)}) collective-permute-start(f32[8,40,128]{2,1,0:T(8,128)S(1)} %all_to_all.21.refs_1_), channel_id=1, source_target_pairs={{1,2},{2,1},{3,4},{4,3},{5,6},{6,5},{7,8},{8,7},{9,10},{10,9},{11,... | collective-permute-start | bytes 491528 | tf_op jit(solution)/shard_map/ppermute | solution.py:666
  138.9 4.6 %shard_map.44 = (f32[32,4,128]{2,1,0:T(4,128)S(1)}, f32[6,16,4,128]{3,2,1,0:T(4,128)S(1)}, f32[6,16,4,128]{3,2,1,0:T(4,128)S(1)}, f32[17,16,128]{2,1,0:T(8,128)}...) custom-call(s32[2]{0:T(128)S(1)} %pad_add_fusion.par.refs_0_, f32[8,40,128]{2,1,0:T(8,128)S(1)} %all_to_all.21.refs_1_, ...), custom_call_target="tpu_custom_call" | custom-call | flops 20000000 | bytes 1000000 | tf_op jit(solution)/shard_map/pallas_call | solution.py:647
  143.9 3.9 %collective-permute-start.21 = (f32[6,16,4,128]{3,2,1,0:T(4,128)S(1)}, f32[6,16,4,128]{3,2,1,0:T(4,128)S(1)}, u32[]{:S(2)}, u32[]{:S(2)}) collective-permute-start(f32[6,16,4,128]{3,2,1,0:T(4,128)S(1)} %get-tuple-element.54), channel_id=1, source_target_pairs={{1,2},{2,1},{3,4},{4,3},{5,6},{6,5},{7,8},{8,7},{9,10},{10,9},{11,... | collective-permute-start | bytes 589832 | tf_op jit(solution)/shard_map/ppermute | solution.py:666
  147.8 20.7 %all_to_all.22 = f32[32,4,128]{2,1,0:T(4,128)S(1)} all-to-all(f32[32,4,128]{2,1,0:T(4,128)S(1)} %get-tuple-element.55), channel_id=1, replica_groups=mesh['gx_0'=4,'gx_1'=2,'gy_0'=8,'gy_1'=4] {'gy_0','gy_1'}, dimensions={0} | all-to-all | bytes 131072 | tf_op jit(solution)/shard_map/all_to_all | solution.py:674
  168.5 4.1 %shard_map.45.mine = f32[2,12,4,128]{3,2,1,0:T(4,128)S(1)} custom-call(s32[2]{0:T(128)S(1)} %pad_add_fusion.par.refs_0_, f32[128,128]{1,0:T(8,128)S(1)} %bitcast.5, f32[17,16,128]{2,1,0:T(8,128)} %get-tuple-element.56.refs_2_, f32[11,16,16,128]{3,2,1,0:T(8,128)} %get-tuple-element.57.refs_3_, f32[3,18,16,128]{3,2,1,0:T(8,128)} %get-tuple-element.58.refs_4_, ...), custom_call_target="tpu_custom_call" | custom-call | flops 20000000 | bytes 1000000 | tf_op jit(solution)/shard_map/pallas_call | solution.py:647
  172.6 4.0 %collective-permute-start.23 = (f32[2,12,4,128]{3,2,1,0:T(4,128)S(1)}, f32[2,12,4,128]{3,2,1,0:T(4,128)S(1)}, u32[]{:S(2)}, u32[]{:S(2)}) collective-permute-start(f32[2,12,4,128]{3,2,1,0:T(4,128)S(1)} %shard_map.45.mine), channel_id=1, source_target_pairs={{1,2},{2,1},{3,4},{4,3},{5,6},{6,5},{7,8},{8,7},{9,10},{10,9},{11,... | collective-permute-start | bytes 147464 | tf_op jit(solution)/shard_map/ppermute | solution.py:666
  176.7 4.0 %collective-permute-done.23.eb = f32[2,12,4,128]{3,2,1,0:T(4,128)S(1)} collective-permute-done((f32[2,12,4,128]{3,2,1,0:T(4,128)S(1)}, f32[2,12,4,128]{3,2,1,0:T(4,128)S(1)}, u32[]{:S(2)}, u32[]{:S(2)}) %collective-permute-start.23) | collective-permute-done | bytes 49184 | tf_op jit(solution)/shard_map/ppermute | solution.py:666
  180.8 4.1 %shard_map.46 = f32[3,8,8,128]{3,2,1,0:T(8,128)} custom-call(s32[2]{0:T(128)S(1)} %pad_add_fusion.par.refs_0_, f32[3,8,8,128]{3,2,1,0:T(8,128)S(1)} %get-tuple-element.50.refs_4_.flow, f32[3,8,8,128]{3,2,1,0:T(8,128)S(1)} %collective-permute-done.16.refs_5_.fa, f32[3,8,8,128]{3,2,1,0:T(8,128)S(1)} %collective-permute-done.17.refs_6_.fb, ...), custom_call_target="tpu_custom_call" | custom-call | flops 20000000 | bytes 1000000 | tf_op jit(solution)/shard_map/pallas_call | solution.py:647
  (44 shorter events, 38.1 us)
Async XLA Ops:
  0.9 3.7 %collective-permute-start.1 = (f32[5,8,8,128]{3,2,1,0:T(8,128)S(1)}, f32[5,8,8,128]{3,2,1,0:T(8,128)S(1)}, u32[]{:S(2)}, u32[]{:S(2)}) collective-permute-start(f32[5,8,8,128]{3,2,1,0:T(8,128)S(1)} %pad_maximum_fusion.own), channel_id=1, source_target_pairs={{32,64},{64,32},{96,128},{128,96},{160,192},{192,160},{33,65},{65,... | collective-permute-start | bytes 491528 | tf_op jit(solution)/shard_map/ppermute | solution.py:666
  1.6 4.0 %collective-permute-start = (f32[5,8,8,128]{3,2,1,0:T(8,128)S(1)}, f32[5,8,8,128]{3,2,1,0:T(8,128)S(1)}, u32[]{:S(2)}, u32[]{:S(2)}) collective-permute-start(f32[5,8,8,128]{3,2,1,0:T(8,128)S(1)} %pad_maximum_fusion.own), channel_id=1, source_target_pairs={{0,32},{32,0},{64,96},{96,64},{128,160},{160,128},{192,224},{224,1... | collective-permute-start | bytes 491528 | tf_op jit(solution)/shard_map/ppermute | solution.py:666
  6.2 8.9 %collective-permute-start.2 = (f32[5,28,4,128]{3,2,1,0:T(4,128)S(1)}, f32[5,28,4,128]{3,2,1,0:T(4,128)S(1)}, u32[]{:S(2)}, u32[]{:S(2)}) collective-permute-start(f32[5,28,4,128]{3,2,1,0:T(4,128)S(1)} %get-tuple-element.34), channel_id=1, source_target_pairs={{0,1},{1,0},{2,3},{3,2},{4,5},{5,4},{6,7},{7,6},{8,9},{9,8},{10,11... | collective-permute-start | bytes 860168 | tf_op jit(solution)/shard_map/ppermute | solution.py:666
  7.9 13.1 %collective-permute-start.3 = (f32[5,28,4,128]{3,2,1,0:T(4,128)S(1)}, f32[5,28,4,128]{3,2,1,0:T(4,128)S(1)}, u32[]{:S(2)}, u32[]{:S(2)}) collective-permute-start(f32[5,28,4,128]{3,2,1,0:T(4,128)S(1)} %get-tuple-element.35), channel_id=1, source_target_pairs={{1,2},{2,1},{3,4},{4,3},{5,6},{6,5},{7,8},{8,7},{9,10},{10,9},{11,... | collective-permute-start | bytes 860168 | tf_op jit(solution)/shard_map/ppermute | solution.py:666
  40.6 14.0 %collective-permute-start.7 = (f32[8,88,128]{2,1,0:T(8,128)S(1)}, f32[8,88,128]{2,1,0:T(8,128)S(1)}, u32[]{:S(2)}, u32[]{:S(2)}) collective-permute-start(f32[8,88,128]{2,1,0:T(8,128)S(1)} %all_to_all.20.refs_1_), channel_id=1, source_target_pairs={{1,2},{2,1},{3,4},{4,3},{5,6},{6,5},{7,8},{8,7},{9,10},{10,9},{11,... | collective-permute-start | bytes 1081352 | tf_op jit(solution)/shard_map/ppermute | solution.py:666
  44.2 10.4 %collective-permute-start.6 = (f32[8,88,128]{2,1,0:T(8,128)S(1)}, f32[8,88,128]{2,1,0:T(8,128)S(1)}, u32[]{:S(2)}, u32[]{:S(2)}) collective-permute-start(f32[8,88,128]{2,1,0:T(8,128)S(1)} %all_to_all.20.refs_1_), channel_id=1, source_target_pairs={{0,1},{1,0},{2,3},{3,2},{4,5},{5,4},{6,7},{7,6},{8,9},{9,8},{10,11... | collective-permute-start | bytes 1081352 | tf_op jit(solution)/shard_map/ppermute | solution.py:666
  44.3 2.7 %collective-permute-start.5 = (f32[3,8,8,128]{3,2,1,0:T(8,128)S(1)}, f32[3,8,8,128]{3,2,1,0:T(8,128)S(1)}, u32[]{:S(2)}, u32[]{:S(2)}) collective-permute-start(f32[3,8,8,128]{3,2,1,0:T(8,128)S(1)} %get-tuple-element.36.refs_4_.flow), channel_id=1, source_target_pairs={{32,64},{64,32},{96,128},{128,96},{160,192},{192,160},{33,65},{65,... | collective-permute-start | bytes 294920 | tf_op jit(solution)/shard_map/ppermute | solution.py:666
  45.0 3.0 %collective-permute-start.4 = (f32[3,8,8,128]{3,2,1,0:T(8,128)S(1)}, f32[3,8,8,128]{3,2,1,0:T(8,128)S(1)}, u32[]{:S(2)}, u32[]{:S(2)}) collective-permute-start(f32[3,8,8,128]{3,2,1,0:T(8,128)S(1)} %get-tuple-element.36.refs_4_.flow), channel_id=1, source_target_pairs={{0,32},{32,0},{64,96},{96,64},{128,160},{160,128},{192,224},{224,1... | collective-permute-start | bytes 294920 | tf_op jit(solution)/shard_map/ppermute | solution.py:666
  58.6 22.4 %all-to-all-start.1 = ((f32[32,12,128]{2,1,0:T(8,128)}), f32[32,12,128]{2,1,0:T(8,128)S(1)}, u32[]{:S(2)}, u32[]{:S(2)}) async-start(f32[32,12,128]{2,1,0:T(8,128)} %get-tuple-element.40), calls=%async_computation.1 | async-start | bytes 524288 | tf_op jit(solution)/shard_map/all_to_all | solution.py:674
  69.8 11.3 %collective-permute-start.8 = (f32[6,16,4,128]{3,2,1,0:T(4,128)S(1)}, f32[6,16,4,128]{3,2,1,0:T(4,128)S(1)}, u32[]{:S(2)}, u32[]{:S(2)}) collective-permute-start(f32[6,16,4,128]{3,2,1,0:T(4,128)S(1)} %get-tuple-element.38), channel_id=1, source_target_pairs={{0,1},{1,0},{2,3},{3,2},{4,5},{5,4},{6,7},{7,6},{8,9},{9,8},{10,11... | collective-permute-start | bytes 589832 | tf_op jit(solution)/shard_map/ppermute | solution.py:666
  71.3 11.2 %collective-permute-start.9 = (f32[6,16,4,128]{3,2,1,0:T(4,128)S(1)}, f32[6,16,4,128]{3,2,1,0:T(4,128)S(1)}, u32[]{:S(2)}, u32[]{:S(2)}) collective-permute-start(f32[6,16,4,128]{3,2,1,0:T(4,128)S(1)} %get-tuple-element.39), channel_id=1, source_target_pairs={{1,2},{2,1},{3,4},{4,3},{5,6},{6,5},{7,8},{8,7},{9,10},{10,9},{11,... | collective-permute-start | bytes 589832 | tf_op jit(solution)/shard_map/ppermute | solution.py:666
  86.6 8.1 %collective-permute-start.11 = (f32[2,12,4,128]{3,2,1,0:T(4,128)S(1)}, f32[2,12,4,128]{3,2,1,0:T(4,128)S(1)}, u32[]{:S(2)}, u32[]{:S(2)}) collective-permute-start(f32[2,12,4,128]{3,2,1,0:T(4,128)S(1)} %get-tuple-element.44.mine), channel_id=1, source_target_pairs={{1,2},{2,1},{3,4},{4,3},{5,6},{6,5},{7,8},{8,7},{9,10},{10,9},{11,... | collective-permute-start | bytes 147464 | tf_op jit(solution)/shard_map/ppermute | solution.py:666
  89.8 4.9 %collective-permute-start.10 = (f32[2,12,4,128]{3,2,1,0:T(4,128)S(1)}, f32[2,12,4,128]{3,2,1,0:T(4,128)S(1)}, u32[]{:S(2)}, u32[]{:S(2)}) collective-permute-start(f32[2,12,4,128]{3,2,1,0:T(4,128)S(1)} %get-tuple-element.44.mine), channel_id=1, source_target_pairs={{0,1},{1,0},{2,3},{3,2},{4,5},{5,4},{6,7},{7,6},{8,9},{9,8},{10,11... | collective-permute-start | bytes 147464 | tf_op jit(solution)/shard_map/ppermute | solution.py:666
  98.9 3.0 %collective-permute-start.12 = (f32[3,8,8,128]{3,2,1,0:T(8,128)S(1)}, f32[3,8,8,128]{3,2,1,0:T(8,128)S(1)}, u32[]{:S(2)}, u32[]{:S(2)}) collective-permute-start(f32[3,8,8,128]{3,2,1,0:T(8,128)S(1)} %shard_map.41.own), channel_id=1, source_target_pairs={{0,32},{32,0},{64,96},{96,64},{128,160},{160,128},{192,224},{224,1... | collective-permute-start | bytes 294920 | tf_op jit(solution)/shard_map/ppermute | solution.py:666
  102.5 7.0 %collective-permute-start.14 = (f32[3,28,4,128]{3,2,1,0:T(4,128)S(1)}, f32[3,28,4,128]{3,2,1,0:T(4,128)S(1)}, u32[]{:S(2)}, u32[]{:S(2)}) collective-permute-start(f32[3,28,4,128]{3,2,1,0:T(4,128)S(1)} %get-tuple-element.48), channel_id=1, source_target_pairs={{0,1},{1,0},{2,3},{3,2},{4,5},{5,4},{6,7},{7,6},{8,9},{9,8},{10,11... | collective-permute-start | bytes 516104 | tf_op jit(solution)/shard_map/ppermute | solution.py:666
  102.6 11.0 %collective-permute-start.15 = (f32[3,28,4,128]{3,2,1,0:T(4,128)S(1)}, f32[3,28,4,128]{3,2,1,0:T(4,128)S(1)}, u32[]{:S(2)}, u32[]{:S(2)}) collective-permute-start(f32[3,28,4,128]{3,2,1,0:T(4,128)S(1)} %get-tuple-element.49), channel_id=1, source_target_pairs={{1,2},{2,1},{3,4},{4,3},{5,6},{6,5},{7,8},{8,7},{9,10},{10,9},{11,... | collective-permute-start | bytes 516104 | tf_op jit(solution)/shard_map/ppermute | solution.py:666
  129.2 9.7 %collective-permute-start.19 = (f32[8,40,128]{2,1,0:T(8,128)S(1)}, f32[8,40,128]{2,1,0:T(8,128)S(1)}, u32[]{:S(2)}, u32[]{:S(2)}) collective-permute-start(f32[8,40,128]{2,1,0:T(8,128)S(1)} %all_to_all.21.refs_1_), channel_id=1, source_target_pairs={{1,2},{2,1},{3,4},{4,3},{5,6},{6,5},{7,8},{8,7},{9,10},{10,9},{11,... | collective-permute-start | bytes 491528 | tf_op jit(solution)/shard_map/ppermute | solution.py:666
  133.4 5.5 %collective-permute-start.18 = (f32[8,40,128]{2,1,0:T(8,128)S(1)}, f32[8,40,128]{2,1,0:T(8,128)S(1)}, u32[]{:S(2)}, u32[]{:S(2)}) collective-permute-start(f32[8,40,128]{2,1,0:T(8,128)S(1)} %all_to_all.21.refs_1_), channel_id=1, source_target_pairs={{0,1},{1,0},{2,3},{3,2},{4,5},{5,4},{6,7},{7,6},{8,9},{9,8},{10,11... | collective-permute-start | bytes 491528 | tf_op jit(solution)/shard_map/ppermute | solution.py:666
  133.5 2.7 %collective-permute-start.17 = (f32[3,8,8,128]{3,2,1,0:T(8,128)S(1)}, f32[3,8,8,128]{3,2,1,0:T(8,128)S(1)}, u32[]{:S(2)}, u32[]{:S(2)}) collective-permute-start(f32[3,8,8,128]{3,2,1,0:T(8,128)S(1)} %get-tuple-element.50.refs_4_.flow), channel_id=1, source_target_pairs={{32,64},{64,32},{96,128},{128,96},{160,192},{192,160},{33,65},{65,... | collective-permute-start | bytes 294920 | tf_op jit(solution)/shard_map/ppermute | solution.py:666
  134.1 3.0 %collective-permute-start.16 = (f32[3,8,8,128]{3,2,1,0:T(8,128)S(1)}, f32[3,8,8,128]{3,2,1,0:T(8,128)S(1)}, u32[]{:S(2)}, u32[]{:S(2)}) collective-permute-start(f32[3,8,8,128]{3,2,1,0:T(8,128)S(1)} %get-tuple-element.50.refs_4_.flow), channel_id=1, source_target_pairs={{0,32},{32,0},{64,96},{96,64},{128,160},{160,128},{192,224},{224,1... | collective-permute-start | bytes 294920 | tf_op jit(solution)/shard_map/ppermute | solution.py:666
  143.5 25.0 %collective-permute-start.20 = (f32[6,16,4,128]{3,2,1,0:T(4,128)S(1)}, f32[6,16,4,128]{3,2,1,0:T(4,128)S(1)}, u32[]{:S(2)}, u32[]{:S(2)}) collective-permute-start(f32[6,16,4,128]{3,2,1,0:T(4,128)S(1)} %get-tuple-element.53), channel_id=1, source_target_pairs={{0,1},{1,0},{2,3},{3,2},{4,5},{5,4},{6,7},{7,6},{8,9},{9,8},{10,11... | collective-permute-start | bytes 589832 | tf_op jit(solution)/shard_map/ppermute | solution.py:666
  143.9 24.6 %collective-permute-start.21 = (f32[6,16,4,128]{3,2,1,0:T(4,128)S(1)}, f32[6,16,4,128]{3,2,1,0:T(4,128)S(1)}, u32[]{:S(2)}, u32[]{:S(2)}) collective-permute-start(f32[6,16,4,128]{3,2,1,0:T(4,128)S(1)} %get-tuple-element.54), channel_id=1, source_target_pairs={{1,2},{2,1},{3,4},{4,3},{5,6},{6,5},{7,8},{8,7},{9,10},{10,9},{11,... | collective-permute-start | bytes 589832 | tf_op jit(solution)/shard_map/ppermute | solution.py:666
  172.6 8.1 %collective-permute-start.23 = (f32[2,12,4,128]{3,2,1,0:T(4,128)S(1)}, f32[2,12,4,128]{3,2,1,0:T(4,128)S(1)}, u32[]{:S(2)}, u32[]{:S(2)}) collective-permute-start(f32[2,12,4,128]{3,2,1,0:T(4,128)S(1)} %shard_map.45.mine), channel_id=1, source_target_pairs={{1,2},{2,1},{3,4},{4,3},{5,6},{6,5},{7,8},{8,7},{9,10},{10,9},{11,... | collective-permute-start | bytes 147464 | tf_op jit(solution)/shard_map/ppermute | solution.py:666
  176.6 4.2 %collective-permute-start.22 = (f32[2,12,4,128]{3,2,1,0:T(4,128)S(1)}, f32[2,12,4,128]{3,2,1,0:T(4,128)S(1)}, u32[]{:S(2)}, u32[]{:S(2)}) collective-permute-start(f32[2,12,4,128]{3,2,1,0:T(4,128)S(1)} %shard_map.45.mine), channel_id=1, source_target_pairs={{0,1},{1,0},{2,3},{3,2},{4,5},{5,4},{6,7},{7,6},{8,9},{9,8},{10,11... | collective-permute-start | bytes 147464 | tf_op jit(solution)/shard_map/ppermute | solution.py:666
  (2 other events, 57.7 us)

commit v3 on v2

--- a/solution.py
+++ b/solution.py
@@ -21,6 +21,7 @@
 
 NX, NY = 64, 256
 ROWS = 24
+NEAR = slice(4, 20)
 WIDE = 20
 MROWS = 16
 
@@ -142,7 +143,7 @@
                 to_b[f, 13 + x] = second_of(above, below)
 
 
-def stack_rows(par, own, ya, yb, out):
+def stack_rows(par, own, ya, yb, out, close):
     low_of, high_of = sides(par, 1, (4, 128))
     zero = jnp.zeros((4, 128), jnp.float32)
     for f in range(own.shape[0]):
@@ -150,23 +151,27 @@
             out[f, x, 8:16] = own[f, x]
             near = (ya[f, x - 1], yb[f, x - 1]) if 1 <= x < 19 else (zero, zero)
             far = (ya[f, 13 + x], yb[f, 13 + x]) if 5 <= x < 15 else (zero, zero)
+            low, high = low_of(*near), high_of(*near)
             out[f, x, 0:4] = low_of(*far)
-            out[f, x, 4:8] = low_of(*near)
-            out[f, x, 16:20] = high_of(*near)
+            out[f, x, 4:8] = low
+            out[f, x, 16:20] = high
             out[f, x, 20:24] = high_of(*far)
+            if f < 3:
+                close[f, x, 0:4] = low
+                close[f, x, 4:12] = own[f, x]
+                close[f, x, 12:16] = high
 
 
 def pre_kernel(first, *refs):
     if first:
-        par, own, ya, yb, flow_out, msg, lev_far, tens_far, lev, tens, u0, u1, w, even, odd, sums, sems = refs
+        par, own, ya, yb, flow_out, msg, lev_far, tens_far, lev, tens, full, u0, u1, w, fy_low, even, odd, sums, sems = refs
     else:
-        par, own, ya, yb, tens_far, flow_out, msg, lev_far, lev, tens, u0, u1, w, even, odd, sums, sems = refs
-        parts = [(tens_far.at[k, 2:18], tens.at[k, 2:18]) for k in (slice(0, 6), slice(6, 9))]
-        tens_copy, source_copy = moved(parts, sems)
+        par, own, ya, yb, tens, flow_out, msg, lev_far, lev, full, u0, u1, w, fy_low, even, odd, sums, sems = refs
     shape = (ROWS, 128)
     lane = iota(shape, 1)
     last, start = lane == 127, lane == 0
-    stack_rows(par, own, ya, yb, u0)
+    stack_rows(par, own, ya, yb, full, u0)
+    near_last = iota((16, 128), 1) == 127
 
     def z_slope(v):
         return jnp.where(last, 0.0, roll(v, -1, 1)) - jnp.where(start, 0.0, roll(v, 1, 1))
@@ -177,17 +182,17 @@
     if first:
 
         def tensor_turn(x):
-            mean = 0.5 * (u0[3, x] + u0[4, x])
-            sx = 0.25 * ((u0[3, x + 1] + u0[4, x + 1]) - (u0[3, x - 1] + u0[4, x - 1]))
+            mean = 0.5 * (full[3, x] + full[4, x])
+            sx = 0.25 * ((full[3, x + 1] + full[4, x + 1]) - (full[3, x - 1] + full[4, x - 1]))
             sy = 0.5 * y_slope(mean)
             sz = 0.5 * z_slope(mean)
-            change = u0[4, x] - u0[3, x]
+            change = full[4, x] - full[3, x]
             scale = 1.0 / (sx * sx + sy * sy + sz * sz + floor_grad)
             gx, gy, gz = scale * sx, scale * sy, scale * sz
             for k, v in enumerate((gx * sx, gx * sy, gx * sz, gy * sy, gy * sz, gz * sz)):
-                tens[k, x] = v
+                tens[k, x] = v[NEAR]
             for k, v in enumerate((gx, gy, gz)):
-                tens[6 + k, x] = -v * change
+                tens[6 + k, x] = (-v * change)[NEAR]
 
         loop(2, 18, tensor_turn)
 
@@ -197,8 +202,8 @@
     def weight_turn(x):
         total = jnp.ones(shape, jnp.float32)
         for c in range(3):
-            v = u0[c, x]
-            for slope in (u0[c, x + 1] - u0[c, x - 1], y_slope(v), z_slope(v)):
+            v = full[c, x]
+            for slope in (full[c, x + 1] - full[c, x - 1], y_slope(v), z_slope(v)):
                 total = total + slope * slope
         place = x + (par[0] * 8 - 6)
         keep = jnp.where((place >= 0) & (place < NX), 1.0, 0.0)
@@ -208,27 +213,48 @@
 
     def face_turn(x):
         v = w[x]
-        lev[0, x] = face(v, w[x + 1], smooth_weight)
-        lev[1, x] = face(v, roll(v, -1, 0), smooth_weight)
-        lev[2, x] = jnp.where(last, 0.0, face(v, roll(v, -1, 1), smooth_weight))
+        near = v[NEAR]
+        lev[0, x] = face(near, w[x + 1][NEAR], smooth_weight)
+        if x > 1:
+            along = face(v, roll(v, -1, 0), smooth_weight)
+            lev[1, x] = along[NEAR]
+            fy_low[x] = along[3:19]
+            lev[2, x] = jnp.where(near_last, 0.0, face(near, roll(near, -1, 1), smooth_weight))
 
     loop(1, 18, face_turn)
 
-    if not first:
-        tens_copy.wait()
-
     def inverse_turn(x):
-        total = total_of(lev[0, x], lev[0, x - 1], lev[1, x], lev[2, x])
+        fz = lev[2, x]
+        total = lev[0, x] + lev[0, x - 1] + lev[1, x] + fy_low[x] + fz + roll(fz, 1, 1)
         for k, v in enumerate(inverse_sym([tens[k, x] for k in range(6)], total)):
             lev[3 + k, x] = v
 
     loop(2, 18, inverse_turn)
-    if not first:
-        source_copy.wait()
     far = [(lev, lev_far), (tens, tens_far)] if first else [(lev, lev_far)]
     copies = moved(far, sems)
     bufs = (u0, u1)
-    for n in range(SWEEPS):
+
+
+    def first_turn(x):
+        fx_up, fx_down = lev[0, x], lev[0, x - 1]
+        fy, fz = lev[1, x], lev[2, x]
+        here = [u0[c, x] for c in range(3)]
+        flux = [
+            tens[6 + c, x]
+            + fx_up * u0[c, x + 1]
+            + fx_down * u0[c, x - 1]
+            + fy * full[c, x, 5:21]
+            + fy_low[x] * full[c, x, 3:19]
+            + fz * roll(here[c], -1, 1)
+            + roll(fz * here[c], 1, 1)
+            for c in range(3)
+        ]
+        step = apply_sym([lev[3 + k, x] for k in range(6)], flux)
+        for c in range(3):
+            u1[c, x] = (1.0 - damping) * here[c] + step[c]
+
+    loop(2, 18, first_turn)
+    for n in range(1, SWEEPS):
         fine_sweep(bufs[n % 2], bufs[(n + 1) % 2], 2 + n, 18 - n, lev, tens)
 
     def rest_at(x):
@@ -243,7 +269,7 @@
                 + inflow(here[c], u0[c, x + 1], u0[c, x - 1], fx_up, fx_down, fy, fz)
                 - moved[c]
                 - total * here[c]
-            )[8:16]
+            )[4:12]
             for c in range(3)
         ]
 
@@ -253,7 +279,7 @@
         pair = w[x] + w[x + 1]
         fields = rest + [pair[8:16], roll(pair, 2, 0)[8:16], pair[16:24]]
         if first:
-            fields += [tens[k, x, 8:16] + tens[k, x + 1, 8:16] for k in range(6)]
+            fields += [tens[k, x, 4:12] + tens[k, x + 1, 4:12] for k in range(6)]
         for k, v in enumerate(fields):
             stage = odd if k % 2 else even
             at = (k // 2) * 32 + m * 8
@@ -262,7 +288,7 @@
     loop(0, 4, rest_turn)
     for c in range(3):
         for k in range(8):
-            flow_out[c, k] = u0[c, 6 + k, 8:16]
+            flow_out[c, k] = u0[c, 6 + k, 4:12]
     square = (128, 128)
     into = iota(square, 0) // 2
     low = jnp.where(into == iota(square, 1), 0.125, 0.0)
@@ -335,9 +361,8 @@
         par, own, ya, yb, flow, fa, fb, msg, to_a, to_b, *refs = refs
         mfx_far, mlev_far, err_far, mtens_far, mfx, mlev, err, mtens, u1, w, stage, sems = refs
     else:
-        par, own, ya, yb, flow, fa, fb, mtens_far, msg, to_a, to_b, *refs = refs
-        mfx_far, mlev_far, err_far, mfx, mlev, err, mtens, u1, w, stage, sems = refs
-        (mtens_copy,) = moved([(mtens_far, mtens)], sems)
+        par, own, ya, yb, flow, fa, fb, mtens, msg, to_a, to_b, *refs = refs
+        mfx_far, mlev_far, err_far, mfx, mlev, err, u1, w, stage, sems = refs
     send_flow(par, flow, fa, fb, to_a, to_b)
     shape = (MROWS, 128)
     lane = iota(shape, 1)
@@ -414,9 +439,6 @@
     seam_face = jnp.where(lane < 64, face(w[15], roll(w[0], 64, 1), scale), 0.0)
     mfx[16] = seam_face
     mfx[0] = roll(seam_face, 64, 1)
-
-    if not first:
-        mtens_copy.wait()
 
     def inverse_turn(x):
         total = total_of(mfx[x + 1], mfx[x], mlev[0, x], mlev[1, x])
@@ -578,16 +600,14 @@
     zero = jnp.zeros((4, 128), jnp.float32)
 
     def place(c, k, v):
-        u0[c, 2 + k, 8:16] = v
+        u0[c, 2 + k, 4:12] = v
 
     wide_layers(par, flow, fa, fb, place)
 
     def edge_turn(k):
         for c in range(3):
-            u0[c, 2 + k, 0:4] = zero
-            u0[c, 2 + k, 4:8] = low_of(ya[c, k], yb[c, k])
-            u0[c, 2 + k, 16:20] = high_of(ya[c, k], yb[c, k])
-            u0[c, 2 + k, 20:24] = zero
+            u0[c, 2 + k, 0:4] = low_of(ya[c, k], yb[c, k])
+            u0[c, 2 + k, 12:16] = high_of(ya[c, k], yb[c, k])
 
     loop(0, 16, edge_turn)
     for x in range(12):
@@ -609,10 +629,10 @@
     def tall_turn(x):
         for c in range(3):
             v = lifted[c, x]
-            tall[c, x, pl.ds(0, 12, stride=2), :] = (0.75 * v + 0.25 * roll(v, 1, 0))[0:12]
-            tall[c, x, pl.ds(1, 12, stride=2), :] = (0.75 * v + 0.25 * roll(v, -1, 0))[0:12]
-
-    loop(0, 12, tall_turn)
+            tall[c, x, pl.ds(0, 8, stride=2), :] = (0.75 * v + 0.25 * roll(v, 1, 0))[2:10]
+            tall[c, x, pl.ds(1, 8, stride=2), :] = (0.75 * v + 0.25 * roll(v, -1, 0))[2:10]
+
+    loop(1, 11, tall_turn)
 
     def add_turn(m):
         for c in range(3):
@@ -629,7 +649,7 @@
         fine_sweep(bufs[n % 2], bufs[(n + 1) % 2], 3 + n, 17 - n, lev, tens)
     for c in range(3):
         for k in range(8):
-            out[c, k] = u0[c, 6 + k, 8:16]
+            out[c, k] = u0[c, 6 + k, 4:12]
 
 
 def f32(*shape):
@@ -679,7 +699,7 @@
     block = jnp.concatenate([start_flow, first_image[None], second_image[None]])
     flow = start_flow
     tens = mtens = cinv = None
-    fine_shape, mid_shape = (WIDE, ROWS, 128), (16, MROWS, 128)
+    tall_shape, fine_shape, mid_shape = (WIDE, ROWS, 128), (WIDE, 16, 128), (16, MROWS, 128)
     for cycle in range(CYCLES):
         first = cycle == 0
         sent = block if first else flow
@@ -690,14 +710,15 @@
         size = 88 if first else 40
         stage = (6 if first else 3) * 32
         outs = [(3, 8, 8, 128), (8, size, 128), (9, *fine_shape)]
-        scratch = [(9, *fine_shape), (9, *fine_shape), (fields, *fine_shape), (3, *fine_shape), fine_shape]
+        scratch = [(9, *fine_shape)] * (2 if first else 1)
+        scratch += [(fields, *tall_shape), (3, *fine_shape), (3, *fine_shape), tall_shape, fine_shape]
         scratch += [(stage, 128)] * 3
         args = [par, wide, across(to_a, GY, 0), across(to_b, GY, 1)]
         pre = functools.partial(pre_kernel, first)
         if first:
             flow, message, lev, tens = call(pre, [*outs, (9, *fine_shape)], scratch, args, (), (2, 3), 2)
         else:
-            flow, message, lev = call(pre, outs, scratch, [*args, tens], (4,), (2,), 2)
+            flow, message, lev = call(pre, outs, scratch, [*args, tens], (), (2,), 2)
         layers = beside(flow, GX)
         mids = shared(message, GX)
         args = [par, mids, *beside(mids, GY), flow, *layers]
@@ -705,14 +726,14 @@
         sides_shape = (6, 16, 4, 128)
         saved = [(17, MROWS, 128), (11, *mid_shape), (3, 18, MROWS, 128)]
         outs = [(32, count, 128), sides_shape, sides_shape, *saved]
-        scratch = [*saved, (6, *mid_shape), (3, 18, MROWS, 128), mid_shape, (4 * padded, 128)]
+        scratch = [*saved, *([(6, *mid_shape)] if first else []), (3, 18, MROWS, 128), mid_shape, (4 * padded, 128)]
         mid = functools.partial(mid_kernel, first)
         if first:
             coarse, to_a, to_b, mfx, mlev, err, mtens = call(
                 mid, [*outs, (6, *mid_shape)], scratch, args, (), (3, 4, 5, 6), 4
             )
         else:
-            coarse, to_a, to_b, mfx, mlev, err = call(mid, outs, scratch, [*args, mtens], (7,), (3, 4, 5), 4)
+            coarse, to_a, to_b, mfx, mlev, err = call(mid, outs, scratch, [*args, mtens], (), (3, 4, 5), 4)
         edges = [across(to_a, GY, 0), across(to_b, GY, 1)]
         whole = shared(coarse, GY).reshape(32 * count, 128)
         args = [par, whole, mfx, mlev, err, *edges]
@@ -726,7 +747,7 @@
             (error,) = call(low, outs, [*saved, *scratch], [*args, cinv], (2, 3, 4), (), 4)
         args = [par, flow, *layers, *edges, error, *beside(error, GY), lev, tens]
         scratch = [(9, *fine_shape), (9, *fine_shape), (3, *fine_shape), (3, *fine_shape)]
-        scratch += [(3, 12, 16, 128), (3, 12, 16, 128), (3, 12, 24, 128)]
+        scratch += [(3, 12, 16, 128), (3, 12, 16, 128), (3, 12, 16, 128)]
         (flow,) = call(post_kernel, [(3, 8, 8, 128)], scratch, args, (9, 10), (), 2)
     return flow
 

time: 186 us -> 181 us (0.973)
  Pallas kernels: 36.6 us -> 31.8 us
    pallas_call x10, Pallas kernels: 36.6 us -> 31.8 us  [call(): pl.pallas_call(kernel, in_specs=specs, out_specs=[far if k in far_out els...]
where the time goes in v3:
time: 181 us
  starting transfers between devices  57.8 us (32%)
  blocking collectives  45.2 us (25%)
  waiting for transfers between devices  44.3 us (24%)
  Pallas kernels  31.8 us (18%)
    ppermute x24, starting transfers between devices, across(): return lax.ppermute(field, axes, pairs_of(lax.axis_size(axes), start))  46.7 us
    all_to_all x3, blocking collectives, shared(): return lax.all_to_all(message, axes, 0, 0, tiled=True)  45.2 us
    ppermute x24, waiting for transfers between devices, across(): return lax.ppermute(field, axes, pairs_of(lax.axis_size(axes), start))  38.6 us
    pallas_call x10, Pallas kernels, call(): pl.pallas_call(kernel, in_specs=specs, out_specs=[far if k in far_out els...  31.8 us
    all_to_all x1, starting transfers between devices, shared(): return lax.all_to_all(message, axes, 0, 0, tiled=True)  11.2 us
    all_to_all x1, waiting for transfers between devices, shared(): return lax.all_to_all(message, axes, 0, 0, tiled=True)  5.75 us
  transfers between devices with their start and end apart: 25, of which 15 were waited for; matrix products, arithmetic and copies ran while one was open for 0% of the time, Pallas kernels for 0%

profile of v3, /device:TPU:32, one launch (start us, length us, event | category | flops | bytes accessed | tf_op | source)
XLA Modules:
  0.0 180.6 jit_solution(15419901784812591787)
XLA Ops:
  7.9 3.6 %collective-permute-start.3 = (f32[5,28,4,128]{3,2,1,0:T(4,128)S(1)}, f32[5,28,4,128]{3,2,1,0:T(4,128)S(1)}, u32[]{:S(2)}, u32[]{:S(2)}) collective-permute-start(f32[5,28,4,128]{3,2,1,0:T(4,128)S(1)} %get-tuple-element.35), channel_id=1, source_target_pairs={{1,2},{2,1},{3,4},{4,3},{5,6},{6,5},{7,8},{8,7},{9,10},{10,9},{11,... | collective-permute-start | bytes 860168 | tf_op jit(solution)/shard_map/ppermute | solution.py:686
  11.5 3.6 %collective-permute-done.2.refs_2_ = f32[5,28,4,128]{3,2,1,0:T(4,128)S(1)} collective-permute-done((f32[5,28,4,128]{3,2,1,0:T(4,128)S(1)}, f32[5,28,4,128]{3,2,1,0:T(4,128)S(1)}, u32[]{:S(2)}, u32[]{:S(2)}) %collective-permute-start.2) | collective-permute-done | bytes 286752 | tf_op jit(solution)/shard_map/ppermute | solution.py:686
  15.1 5.8 %collective-permute-done.3.refs_3_ = f32[5,28,4,128]{3,2,1,0:T(4,128)S(1)} collective-permute-done((f32[5,28,4,128]{3,2,1,0:T(4,128)S(1)}, f32[5,28,4,128]{3,2,1,0:T(4,128)S(1)}, u32[]{:S(2)}, u32[]{:S(2)}) %collective-permute-start.3) | collective-permute-done | bytes 286752 | tf_op jit(solution)/shard_map/ppermute | solution.py:686
  20.9 4.5 %shard_map.38 = (f32[3,8,8,128]{3,2,1,0:T(8,128)S(1)}, f32[8,88,128]{2,1,0:T(8,128)S(1)}, f32[9,20,16,128]{3,2,1,0:T(8,128)}, f32[9,20,16,128]{3,2,1,0:T(8,128)}) custom-call(s32[2]{0:T(128)S(1)} %pad_add_fusion.par.refs_0_, f32[5,20,8,128]{3,2,1,0:T(8,128)S(1)} %get-tuple-element.33.refs_1_, f32[5,28,4,128]{3,2,1,0:T(4,128)S(1)} %collective-permute-done.2.refs_2_, ...), custom_call_target="tpu_custom_call" | custom-call | flops 20000000 | bytes 1000000 | tf_op jit(solution)/shard_map/pallas_call | solution.py:667
  25.5 14.2 %all_to_all.20.refs_1_ = f32[8,88,128]{2,1,0:T(8,128)S(1)} all-to-all(f32[8,88,128]{2,1,0:T(8,128)S(1)} %get-tuple-element.37), channel_id=1, replica_groups=mesh['gx_0'=4,'gx_1'=2,'gy_0'=8,'gy_1'=4] {'gx_0','gx_1'}, dimensions={0} | all-to-all | bytes 720896 | tf_op jit(solution)/shard_map/all_to_all | solution.py:694
  39.6 3.6 %collective-permute-start.7 = (f32[8,88,128]{2,1,0:T(8,128)S(1)}, f32[8,88,128]{2,1,0:T(8,128)S(1)}, u32[]{:S(2)}, u32[]{:S(2)}) collective-permute-start(f32[8,88,128]{2,1,0:T(8,128)S(1)} %all_to_all.20.refs_1_), channel_id=1, source_target_pairs={{1,2},{2,1},{3,4},{4,3},{5,6},{6,5},{7,8},{8,7},{9,10},{10,9},{11,... | collective-permute-start | bytes 1081352 | tf_op jit(solution)/shard_map/ppermute | solution.py:686
  47.0 6.6 %collective-permute-done.7.refs_3_ = f32[8,88,128]{2,1,0:T(8,128)S(1)} collective-permute-done((f32[8,88,128]{2,1,0:T(8,128)S(1)}, f32[8,88,128]{2,1,0:T(8,128)S(1)}, u32[]{:S(2)}, u32[]{:S(2)}) %collective-permute-start.7) | collective-permute-done | bytes 360480 | tf_op jit(solution)/shard_map/ppermute | solution.py:686
  53.6 4.0 %shard_map.39 = (f32[32,12,128]{2,1,0:T(8,128)}, f32[6,16,4,128]{3,2,1,0:T(4,128)S(1)}, f32[6,16,4,128]{3,2,1,0:T(4,128)S(1)}, f32[17,16,128]{2,1,0:T(8,128)}, f...) custom-call(s32[2]{0:T(128)S(1)} %pad_add_fusion.par.refs_0_, ...), custom_call_target="tpu_custom_call" | custom-call | flops 20000000 | bytes 1000000 | tf_op jit(solution)/shard_map/pallas_call | solution.py:667
  57.6 11.2 %all-to-all-start.1 = ((f32[32,12,128]{2,1,0:T(8,128)}), f32[32,12,128]{2,1,0:T(8,128)S(1)}, u32[]{:S(2)}, u32[]{:S(2)}) async-start(f32[32,12,128]{2,1,0:T(8,128)} %get-tuple-element.40), calls=%async_computation.1 | async-start | bytes 524288 | tf_op jit(solution)/shard_map/all_to_all | solution.py:694
  70.4 4.0 %collective-permute-start.9 = (f32[6,16,4,128]{3,2,1,0:T(4,128)S(1)}, f32[6,16,4,128]{3,2,1,0:T(4,128)S(1)}, u32[]{:S(2)}, u32[]{:S(2)}) collective-permute-start(f32[6,16,4,128]{3,2,1,0:T(4,128)S(1)} %get-tuple-element.39), channel_id=1, source_target_pairs={{1,2},{2,1},{3,4},{4,3},{5,6},{6,5},{7,8},{8,7},{9,10},{10,9},{11,... | collective-permute-start | bytes 589832 | tf_op jit(solution)/shard_map/ppermute | solution.py:686
  74.3 5.8 %all-to-all-done.1 = f32[32,12,128]{2,1,0:T(8,128)S(1)} async-done(((f32[32,12,128]{2,1,0:T(8,128)}), f32[32,12,128]{2,1,0:T(8,128)S(1)}, u32[]{:S(2)}, u32[]{:S(2)}) %all-to-all-start.1) | async-done | bytes 196640 | tf_op jit(solution)/shard_map/all_to_all | solution.py:694
  81.5 4.1 %shard_map.40 = (f32[2,12,4,128]{3,2,1,0:T(4,128)S(1)}, f32[6,32,128]{2,1,0:T(8,128)}) custom-call(s32[2]{0:T(128)S(1)} %pad_add_fusion.par.refs_0_, f32[384,128]{1,0:T(8,128)S(1)} %reshape.6.refs_1_, f32[17,16,128]{2,1,0:T(8,128)} %get-tuple-element.41.refs_2_, f32[11,16,16,128]{3,2,1,0:T(8,128)} %get-tuple-element.42.refs_3_, ...), custom_call_target="tpu_custom_call" | custom-call | flops 20000000 | bytes 1000000 | tf_op jit(solution)/shard_map/pallas_call | solution.py:667
  89.1 4.7 %collective-permute-done.11.eb = f32[2,12,4,128]{3,2,1,0:T(4,128)S(1)} collective-permute-done((f32[2,12,4,128]{3,2,1,0:T(4,128)S(1)}, f32[2,12,4,128]{3,2,1,0:T(4,128)S(1)}, u32[]{:S(2)}, u32[]{:S(2)}) %collective-permute-start.11) | collective-permute-done | bytes 49184 | tf_op jit(solution)/shard_map/ppermute | solution.py:686
  101.3 4.2 %collective-permute-start.15 = (f32[3,28,4,128]{3,2,1,0:T(4,128)S(1)}, f32[3,28,4,128]{3,2,1,0:T(4,128)S(1)}, u32[]{:S(2)}, u32[]{:S(2)}) collective-permute-start(f32[3,28,4,128]{3,2,1,0:T(4,128)S(1)} %get-tuple-element.49), channel_id=1, source_target_pairs={{1,2},{2,1},{3,4},{4,3},{5,6},{6,5},{7,8},{8,7},{9,10},{10,9},{11,... | collective-permute-start | bytes 516104 | tf_op jit(solution)/shard_map/ppermute | solution.py:686
  108.3 4.0 %collective-permute-done.15.refs_3_ = f32[3,28,4,128]{3,2,1,0:T(4,128)S(1)} collective-permute-done((f32[3,28,4,128]{3,2,1,0:T(4,128)S(1)}, f32[3,28,4,128]{3,2,1,0:T(4,128)S(1)}, u32[]{:S(2)}, u32[]{:S(2)}) %collective-permute-start.15) | collective-permute-done | bytes 172064 | tf_op jit(solution)/shard_map/ppermute | solution.py:686
  112.3 3.9 %shard_map.43 = (f32[3,8,8,128]{3,2,1,0:T(8,128)S(1)}, f32[8,40,128]{2,1,0:T(8,128)S(1)}, f32[9,20,16,128]{3,2,1,0:T(8,128)}) custom-call(s32[2]{0:T(128)S(1)} %pad_add_fusion.par.refs_0_, f32[3,20,8,128]{3,2,1,0:T(8,128)S(1)} %get-tuple-element.47.refs_1_, f32[3,28,4,128]{3,2,1,0:T(4,128)S(1)} %collective-permute-done.14.refs_2_, ...), custom_call_target="tpu_custom_call" | custom-call | flops 20000000 | bytes 1000000 | tf_op jit(solution)/shard_map/pallas_call | solution.py:667
  116.2 10.3 %all_to_all.21.refs_1_ = f32[8,40,128]{2,1,0:T(8,128)S(1)} all-to-all(f32[8,40,128]{2,1,0:T(8,128)S(1)} %get-tuple-element.51), channel_id=1, replica_groups=mesh['gx_0'=4,'gx_1'=2,'gy_0'=8,'gy_1'=4] {'gx_0','gx_1'}, dimensions={0} | all-to-all | bytes 327680 | tf_op jit(solution)/shard_map/all_to_all | solution.py:694
  126.5 4.2 %collective-permute-start.19 = (f32[8,40,128]{2,1,0:T(8,128)S(1)}, f32[8,40,128]{2,1,0:T(8,128)S(1)}, u32[]{:S(2)}, u32[]{:S(2)}) collective-permute-start(f32[8,40,128]{2,1,0:T(8,128)S(1)} %all_to_all.21.refs_1_), channel_id=1, source_target_pairs={{1,2},{2,1},{3,4},{4,3},{5,6},{6,5},{7,8},{8,7},{9,10},{10,9},{11,... | collective-permute-start | bytes 491528 | tf_op jit(solution)/shard_map/ppermute | solution.py:686
  139.8 3.9 %collective-permute-start.21 = (f32[6,16,4,128]{3,2,1,0:T(4,128)S(1)}, f32[6,16,4,128]{3,2,1,0:T(4,128)S(1)}, u32[]{:S(2)}, u32[]{:S(2)}) collective-permute-start(f32[6,16,4,128]{3,2,1,0:T(4,128)S(1)} %get-tuple-element.54), channel_id=1, source_target_pairs={{1,2},{2,1},{3,4},{4,3},{5,6},{6,5},{7,8},{8,7},{9,10},{10,9},{11,... | collective-permute-start | bytes 589832 | tf_op jit(solution)/shard_map/ppermute | solution.py:686
  143.7 20.7 %all_to_all.22 = f32[32,4,128]{2,1,0:T(4,128)S(1)} all-to-all(f32[32,4,128]{2,1,0:T(4,128)S(1)} %get-tuple-element.55), channel_id=1, replica_groups=mesh['gx_0'=4,'gx_1'=2,'gy_0'=8,'gy_1'=4] {'gy_0','gy_1'}, dimensions={0} | all-to-all | bytes 131072 | tf_op jit(solution)/shard_map/all_to_all | solution.py:694
  164.5 4.1 %shard_map.45.mine = f32[2,12,4,128]{3,2,1,0:T(4,128)S(1)} custom-call(s32[2]{0:T(128)S(1)} %pad_add_fusion.par.refs_0_, f32[128,128]{1,0:T(8,128)S(1)} %bitcast.5, f32[17,16,128]{2,1,0:T(8,128)} %get-tuple-element.56.refs_2_, f32[11,16,16,128]{3,2,1,0:T(8,128)} %get-tuple-element.57.refs_3_, f32[3,18,16,128]{3,2,1,0:T(8,128)} %get-tuple-element.58.refs_4_, ...), custom_call_target="tpu_custom_call" | custom-call | flops 20000000 | bytes 1000000 | tf_op jit(solution)/shard_map/pallas_call | solution.py:667
  168.6 4.0 %collective-permute-start.23 = (f32[2,12,4,128]{3,2,1,0:T(4,128)S(1)}, f32[2,12,4,128]{3,2,1,0:T(4,128)S(1)}, u32[]{:S(2)}, u32[]{:S(2)}) collective-permute-start(f32[2,12,4,128]{3,2,1,0:T(4,128)S(1)} %shard_map.45.mine), channel_id=1, source_target_pairs={{1,2},{2,1},{3,4},{4,3},{5,6},{6,5},{7,8},{8,7},{9,10},{10,9},{11,... | collective-permute-start | bytes 147464 | tf_op jit(solution)/shard_map/ppermute | solution.py:686
  172.6 4.0 %collective-permute-done.23.eb = f32[2,12,4,128]{3,2,1,0:T(4,128)S(1)} collective-permute-done((f32[2,12,4,128]{3,2,1,0:T(4,128)S(1)}, f32[2,12,4,128]{3,2,1,0:T(4,128)S(1)}, u32[]{:S(2)}, u32[]{:S(2)}) %collective-permute-start.23) | collective-permute-done | bytes 49184 | tf_op jit(solution)/shard_map/ppermute | solution.py:686
  176.7 3.7 %shard_map.46 = f32[3,8,8,128]{3,2,1,0:T(8,128)} custom-call(s32[2]{0:T(128)S(1)} %pad_add_fusion.par.refs_0_, f32[3,8,8,128]{3,2,1,0:T(8,128)S(1)} %get-tuple-element.50.refs_4_.flow, f32[3,8,8,128]{3,2,1,0:T(8,128)S(1)} %collective-permute-done.16.refs_5_.fa, f32[3,8,8,128]{3,2,1,0:T(8,128)S(1)} %collective-permute-done.17.refs_6_.fb, ...), custom_call_target="tpu_custom_call" | custom-call | flops 20000000 | bytes 1000000 | tf_op jit(solution)/shard_map/pallas_call | solution.py:667
  (48 shorter events, 37.5 us)
Async XLA Ops:
  0.9 3.7 %collective-permute-start.1 = (f32[5,8,8,128]{3,2,1,0:T(8,128)S(1)}, f32[5,8,8,128]{3,2,1,0:T(8,128)S(1)}, u32[]{:S(2)}, u32[]{:S(2)}) collective-permute-start(f32[5,8,8,128]{3,2,1,0:T(8,128)S(1)} %pad_maximum_fusion.own), channel_id=1, source_target_pairs={{32,64},{64,32},{96,128},{128,96},{160,192},{192,160},{33,65},{65,... | collective-permute-start | bytes 491528 | tf_op jit(solution)/shard_map/ppermute | solution.py:686
  1.6 4.0 %collective-permute-start = (f32[5,8,8,128]{3,2,1,0:T(8,128)S(1)}, f32[5,8,8,128]{3,2,1,0:T(8,128)S(1)}, u32[]{:S(2)}, u32[]{:S(2)}) collective-permute-start(f32[5,8,8,128]{3,2,1,0:T(8,128)S(1)} %pad_maximum_fusion.own), channel_id=1, source_target_pairs={{0,32},{32,0},{64,96},{96,64},{128,160},{160,128},{192,224},{224,1... | collective-permute-start | bytes 491528 | tf_op jit(solution)/shard_map/ppermute | solution.py:686
  6.2 8.9 %collective-permute-start.2 = (f32[5,28,4,128]{3,2,1,0:T(4,128)S(1)}, f32[5,28,4,128]{3,2,1,0:T(4,128)S(1)}, u32[]{:S(2)}, u32[]{:S(2)}) collective-permute-start(f32[5,28,4,128]{3,2,1,0:T(4,128)S(1)} %get-tuple-element.34), channel_id=1, source_target_pairs={{0,1},{1,0},{2,3},{3,2},{4,5},{5,4},{6,7},{7,6},{8,9},{9,8},{10,11... | collective-permute-start | bytes 860168 | tf_op jit(solution)/shard_map/ppermute | solution.py:686
  7.9 13.1 %collective-permute-start.3 = (f32[5,28,4,128]{3,2,1,0:T(4,128)S(1)}, f32[5,28,4,128]{3,2,1,0:T(4,128)S(1)}, u32[]{:S(2)}, u32[]{:S(2)}) collective-permute-start(f32[5,28,4,128]{3,2,1,0:T(4,128)S(1)} %get-tuple-element.35), channel_id=1, source_target_pairs={{1,2},{2,1},{3,4},{4,3},{5,6},{6,5},{7,8},{8,7},{9,10},{10,9},{11,... | collective-permute-start | bytes 860168 | tf_op jit(solution)/shard_map/ppermute | solution.py:686
  39.6 14.0 %collective-permute-start.7 = (f32[8,88,128]{2,1,0:T(8,128)S(1)}, f32[8,88,128]{2,1,0:T(8,128)S(1)}, u32[]{:S(2)}, u32[]{:S(2)}) collective-permute-start(f32[8,88,128]{2,1,0:T(8,128)S(1)} %all_to_all.20.refs_1_), channel_id=1, source_target_pairs={{1,2},{2,1},{3,4},{4,3},{5,6},{6,5},{7,8},{8,7},{9,10},{10,9},{11,... | collective-permute-start | bytes 1081352 | tf_op jit(solution)/shard_map/ppermute | solution.py:686
  43.3 10.4 %collective-permute-start.6 = (f32[8,88,128]{2,1,0:T(8,128)S(1)}, f32[8,88,128]{2,1,0:T(8,128)S(1)}, u32[]{:S(2)}, u32[]{:S(2)}) collective-permute-start(f32[8,88,128]{2,1,0:T(8,128)S(1)} %all_to_all.20.refs_1_), channel_id=1, source_target_pairs={{0,1},{1,0},{2,3},{3,2},{4,5},{5,4},{6,7},{7,6},{8,9},{9,8},{10,11... | collective-permute-start | bytes 1081352 | tf_op jit(solution)/shard_map/ppermute | solution.py:686
  43.4 2.7 %collective-permute-start.5 = (f32[3,8,8,128]{3,2,1,0:T(8,128)S(1)}, f32[3,8,8,128]{3,2,1,0:T(8,128)S(1)}, u32[]{:S(2)}, u32[]{:S(2)}) collective-permute-start(f32[3,8,8,128]{3,2,1,0:T(8,128)S(1)} %get-tuple-element.36.refs_4_.flow), channel_id=1, source_target_pairs={{32,64},{64,32},{96,128},{128,96},{160,192},{192,160},{33,65},{65,... | collective-permute-start | bytes 294920 | tf_op jit(solution)/shard_map/ppermute | solution.py:686
  44.0 3.0 %collective-permute-start.4 = (f32[3,8,8,128]{3,2,1,0:T(8,128)S(1)}, f32[3,8,8,128]{3,2,1,0:T(8,128)S(1)}, u32[]{:S(2)}, u32[]{:S(2)}) collective-permute-start(f32[3,8,8,128]{3,2,1,0:T(8,128)S(1)} %get-tuple-element.36.refs_4_.flow), channel_id=1, source_target_pairs={{0,32},{32,0},{64,96},{96,64},{128,160},{160,128},{192,224},{224,1... | collective-permute-start | bytes 294920 | tf_op jit(solution)/shard_map/ppermute | solution.py:686
  57.6 22.4 %all-to-all-start.1 = ((f32[32,12,128]{2,1,0:T(8,128)}), f32[32,12,128]{2,1,0:T(8,128)S(1)}, u32[]{:S(2)}, u32[]{:S(2)}) async-start(f32[32,12,128]{2,1,0:T(8,128)} %get-tuple-element.40), calls=%async_computation.1 | async-start | bytes 524288 | tf_op jit(solution)/shard_map/all_to_all | solution.py:694
  68.8 11.3 %collective-permute-start.8 = (f32[6,16,4,128]{3,2,1,0:T(4,128)S(1)}, f32[6,16,4,128]{3,2,1,0:T(4,128)S(1)}, u32[]{:S(2)}, u32[]{:S(2)}) collective-permute-start(f32[6,16,4,128]{3,2,1,0:T(4,128)S(1)} %get-tuple-element.38), channel_id=1, source_target_pairs={{0,1},{1,0},{2,3},{3,2},{4,5},{5,4},{6,7},{7,6},{8,9},{9,8},{10,11... | collective-permute-start | bytes 589832 | tf_op jit(solution)/shard_map/ppermute | solution.py:686
  70.4 11.2 %collective-permute-start.9 = (f32[6,16,4,128]{3,2,1,0:T(4,128)S(1)}, f32[6,16,4,128]{3,2,1,0:T(4,128)S(1)}, u32[]{:S(2)}, u32[]{:S(2)}) collective-permute-start(f32[6,16,4,128]{3,2,1,0:T(4,128)S(1)} %get-tuple-element.39), channel_id=1, source_target_pairs={{1,2},{2,1},{3,4},{4,3},{5,6},{6,5},{7,8},{8,7},{9,10},{10,9},{11,... | collective-permute-start | bytes 589832 | tf_op jit(solution)/shard_map/ppermute | solution.py:686
  85.7 8.1 %collective-permute-start.11 = (f32[2,12,4,128]{3,2,1,0:T(4,128)S(1)}, f32[2,12,4,128]{3,2,1,0:T(4,128)S(1)}, u32[]{:S(2)}, u32[]{:S(2)}) collective-permute-start(f32[2,12,4,128]{3,2,1,0:T(4,128)S(1)} %get-tuple-element.44.mine), channel_id=1, source_target_pairs={{1,2},{2,1},{3,4},{4,3},{5,6},{6,5},{7,8},{8,7},{9,10},{10,9},{11,... | collective-permute-start | bytes 147464 | tf_op jit(solution)/shard_map/ppermute | solution.py:686
  88.8 4.9 %collective-permute-start.10 = (f32[2,12,4,128]{3,2,1,0:T(4,128)S(1)}, f32[2,12,4,128]{3,2,1,0:T(4,128)S(1)}, u32[]{:S(2)}, u32[]{:S(2)}) collective-permute-start(f32[2,12,4,128]{3,2,1,0:T(4,128)S(1)} %get-tuple-element.44.mine), channel_id=1, source_target_pairs={{0,1},{1,0},{2,3},{3,2},{4,5},{5,4},{6,7},{7,6},{8,9},{9,8},{10,11... | collective-permute-start | bytes 147464 | tf_op jit(solution)/shard_map/ppermute | solution.py:686
  96.9 2.8 %collective-permute-start.13 = (f32[3,8,8,128]{3,2,1,0:T(8,128)S(1)}, f32[3,8,8,128]{3,2,1,0:T(8,128)S(1)}, u32[]{:S(2)}, u32[]{:S(2)}) collective-permute-start(f32[3,8,8,128]{3,2,1,0:T(8,128)S(1)} %shard_map.41.own), channel_id=1, source_target_pairs={{32,64},{64,32},{96,128},{128,96},{160,192},{192,160},{33,65},{65,... | collective-permute-start | bytes 294920 | tf_op jit(solution)/shard_map/ppermute | solution.py:686
  97.7 2.9 %collective-permute-start.12 = (f32[3,8,8,128]{3,2,1,0:T(8,128)S(1)}, f32[3,8,8,128]{3,2,1,0:T(8,128)S(1)}, u32[]{:S(2)}, u32[]{:S(2)}) collective-permute-start(f32[3,8,8,128]{3,2,1,0:T(8,128)S(1)} %shard_map.41.own), channel_id=1, source_target_pairs={{0,32},{32,0},{64,96},{96,64},{128,160},{160,128},{192,224},{224,1... | collective-permute-start | bytes 294920 | tf_op jit(solution)/shard_map/ppermute | solution.py:686
  101.2 7.0 %collective-permute-start.14 = (f32[3,28,4,128]{3,2,1,0:T(4,128)S(1)}, f32[3,28,4,128]{3,2,1,0:T(4,128)S(1)}, u32[]{:S(2)}, u32[]{:S(2)}) collective-permute-start(f32[3,28,4,128]{3,2,1,0:T(4,128)S(1)} %get-tuple-element.48), channel_id=1, source_target_pairs={{0,1},{1,0},{2,3},{3,2},{4,5},{5,4},{6,7},{7,6},{8,9},{9,8},{10,11... | collective-permute-start | bytes 516104 | tf_op jit(solution)/shard_map/ppermute | solution.py:686
  101.3 11.0 %collective-permute-start.15 = (f32[3,28,4,128]{3,2,1,0:T(4,128)S(1)}, f32[3,28,4,128]{3,2,1,0:T(4,128)S(1)}, u32[]{:S(2)}, u32[]{:S(2)}) collective-permute-start(f32[3,28,4,128]{3,2,1,0:T(4,128)S(1)} %get-tuple-element.49), channel_id=1, source_target_pairs={{1,2},{2,1},{3,4},{4,3},{5,6},{6,5},{7,8},{8,7},{9,10},{10,9},{11,... | collective-permute-start | bytes 516104 | tf_op jit(solution)/shard_map/ppermute | solution.py:686
  126.5 9.7 %collective-permute-start.19 = (f32[8,40,128]{2,1,0:T(8,128)S(1)}, f32[8,40,128]{2,1,0:T(8,128)S(1)}, u32[]{:S(2)}, u32[]{:S(2)}) collective-permute-start(f32[8,40,128]{2,1,0:T(8,128)S(1)} %all_to_all.21.refs_1_), channel_id=1, source_target_pairs={{1,2},{2,1},{3,4},{4,3},{5,6},{6,5},{7,8},{8,7},{9,10},{10,9},{11,... | collective-permute-start | bytes 491528 | tf_op jit(solution)/shard_map/ppermute | solution.py:686
  130.7 5.5 %collective-permute-start.18 = (f32[8,40,128]{2,1,0:T(8,128)S(1)}, f32[8,40,128]{2,1,0:T(8,128)S(1)}, u32[]{:S(2)}, u32[]{:S(2)}) collective-permute-start(f32[8,40,128]{2,1,0:T(8,128)S(1)} %all_to_all.21.refs_1_), channel_id=1, source_target_pairs={{0,1},{1,0},{2,3},{3,2},{4,5},{5,4},{6,7},{7,6},{8,9},{9,8},{10,11... | collective-permute-start | bytes 491528 | tf_op jit(solution)/shard_map/ppermute | solution.py:686
  131.5 3.0 %collective-permute-start.16 = (f32[3,8,8,128]{3,2,1,0:T(8,128)S(1)}, f32[3,8,8,128]{3,2,1,0:T(8,128)S(1)}, u32[]{:S(2)}, u32[]{:S(2)}) collective-permute-start(f32[3,8,8,128]{3,2,1,0:T(8,128)S(1)} %get-tuple-element.50.refs_4_.flow), channel_id=1, source_target_pairs={{0,32},{32,0},{64,96},{96,64},{128,160},{160,128},{192,224},{224,1... | collective-permute-start | bytes 294920 | tf_op jit(solution)/shard_map/ppermute | solution.py:686
  139.4 25.0 %collective-permute-start.20 = (f32[6,16,4,128]{3,2,1,0:T(4,128)S(1)}, f32[6,16,4,128]{3,2,1,0:T(4,128)S(1)}, u32[]{:S(2)}, u32[]{:S(2)}) collective-permute-start(f32[6,16,4,128]{3,2,1,0:T(4,128)S(1)} %get-tuple-element.53), channel_id=1, source_target_pairs={{0,1},{1,0},{2,3},{3,2},{4,5},{5,4},{6,7},{7,6},{8,9},{9,8},{10,11... | collective-permute-start | bytes 589832 | tf_op jit(solution)/shard_map/ppermute | solution.py:686
  139.8 24.6 %collective-permute-start.21 = (f32[6,16,4,128]{3,2,1,0:T(4,128)S(1)}, f32[6,16,4,128]{3,2,1,0:T(4,128)S(1)}, u32[]{:S(2)}, u32[]{:S(2)}) collective-permute-start(f32[6,16,4,128]{3,2,1,0:T(4,128)S(1)} %get-tuple-element.54), channel_id=1, source_target_pairs={{1,2},{2,1},{3,4},{4,3},{5,6},{6,5},{7,8},{8,7},{9,10},{10,9},{11,... | collective-permute-start | bytes 589832 | tf_op jit(solution)/shard_map/ppermute | solution.py:686
  168.6 8.1 %collective-permute-start.23 = (f32[2,12,4,128]{3,2,1,0:T(4,128)S(1)}, f32[2,12,4,128]{3,2,1,0:T(4,128)S(1)}, u32[]{:S(2)}, u32[]{:S(2)}) collective-permute-start(f32[2,12,4,128]{3,2,1,0:T(4,128)S(1)} %shard_map.45.mine), channel_id=1, source_target_pairs={{1,2},{2,1},{3,4},{4,3},{5,6},{6,5},{7,8},{8,7},{9,10},{10,9},{11,... | collective-permute-start | bytes 147464 | tf_op jit(solution)/shard_map/ppermute | solution.py:686
  172.5 4.2 %collective-permute-start.22 = (f32[2,12,4,128]{3,2,1,0:T(4,128)S(1)}, f32[2,12,4,128]{3,2,1,0:T(4,128)S(1)}, u32[]{:S(2)}, u32[]{:S(2)}) collective-permute-start(f32[2,12,4,128]{3,2,1,0:T(4,128)S(1)} %shard_map.45.mine), channel_id=1, source_target_pairs={{0,1},{1,0},{2,3},{3,2},{4,5},{5,4},{6,7},{7,6},{8,9},{9,8},{10,11... | collective-permute-start | bytes 147464 | tf_op jit(solution)/shard_map/ppermute | solution.py:686
  (4 other events, 108.9 us)

commit v4 on v3

--- a/solution.py
+++ b/solution.py
@@ -101,8 +101,25 @@
     return jnp.maximum(1.0 - jnp.abs(distance), 0.0)
 
 
+def thirds(a):
+    high = a.astype(jnp.bfloat16)
+    rest = a - high.astype(jnp.float32)
+    middle = rest.astype(jnp.bfloat16)
+    return [high, middle, (rest - middle.astype(jnp.float32)).astype(jnp.bfloat16)]
+
+
 def dot(a, b):
-    return jnp.dot(a, b, precision=lax.Precision.HIGHEST, preferred_element_type=jnp.float32)
+    terms = jnp.concatenate(thirds(a), axis=0)
+    got = jnp.dot(terms, b.astype(jnp.bfloat16), preferred_element_type=jnp.float32)
+    n = a.shape[0]
+    return got[0:n] + got[n : 2 * n] + got[2 * n :]
+
+
+def dot_left(a, b):
+    terms = jnp.concatenate(thirds(b), axis=1)
+    got = jnp.dot(a.astype(jnp.bfloat16), terms, preferred_element_type=jnp.float32)
+    n = b.shape[1]
+    return got[:, 0:n] + got[:, n : 2 * n] + got[:, 2 * n :]
 
 
 def fine_sweep(source, target, low, high, lev, tens):
@@ -545,7 +562,7 @@
     shape = (MROWS, 32)
     place = (iota(shape, 0) + (par[1] * 4 - 5)).astype(jnp.float32) * 0.25 - 0.375
     along = hat(place - iota(shape, 1).astype(jnp.float32))
-    rows = jnp.concatenate([dot(along, correction[c]) for c in range(3)], axis=0)
+    rows = jnp.concatenate([dot_left(along, correction[c]) for c in range(3)], axis=0)
     square = (128, 128)
     src, to = iota(square, 0), iota(square, 1)
     depth = hat((to % 64).astype(jnp.float32) * 0.25 - 0.375 - (src % 16).astype(jnp.float32))

time: 181 us -> 181 us (level)
  no operation moved by 1% of the time
where the time goes in v4:
time: 181 us; the launch traced here: 180 us
  starting transfers between devices  57.8 us (32%)
  blocking collectives  45.2 us (25%)
  waiting for transfers between devices  44.3 us (24%)
  Pallas kernels  31.2 us (17%)
    ppermute x24, starting transfers between devices, across(): return lax.ppermute(field, axes, pairs_of(lax.axis_size(axes), start))  46.7 us
    all_to_all x3, blocking collectives, shared(): return lax.all_to_all(message, axes, 0, 0, tiled=True)  45.2 us
    ppermute x24, waiting for transfers between devices, across(): return lax.ppermute(field, axes, pairs_of(lax.axis_size(axes), start))  38.6 us
    pallas_call x10, Pallas kernels, call(): pl.pallas_call(kernel, in_specs=specs, out_specs=[far if k in far_out els...  31.2 us
    all_to_all x1, starting transfers between devices, shared(): return lax.all_to_all(message, axes, 0, 0, tiled=True)  11.2 us
    all_to_all x1, waiting for transfers between devices, shared(): return lax.all_to_all(message, axes, 0, 0, tiled=True)  5.75 us
  transfers between devices with their start and end apart: 25, of which 15 were waited for; matrix products, arithmetic and copies ran while one was open for 0% of the time, Pallas kernels for 0%

profile of v4, /device:TPU:32, one launch (start us, length us, event | category | flops | bytes accessed | tf_op | source)
XLA Modules:
  0.0 180.0 jit_solution(5858518398154359129)
XLA Ops:
  7.9 3.6 %collective-permute-start.3 = (f32[5,28,4,128]{3,2,1,0:T(4,128)S(1)}, f32[5,28,4,128]{3,2,1,0:T(4,128)S(1)}, u32[]{:S(2)}, u32[]{:S(2)}) collective-permute-start(f32[5,28,4,128]{3,2,1,0:T(4,128)S(1)} %get-tuple-element.35), channel_id=1, source_target_pairs={{1,2},{2,1},{3,4},{4,3},{5,6},{6,5},{7,8},{8,7},{9,10},{10,9},{11,... | collective-permute-start | bytes 860168 | tf_op jit(solution)/shard_map/ppermute | solution.py:703
  11.5 3.6 %collective-permute-done.2.refs_2_ = f32[5,28,4,128]{3,2,1,0:T(4,128)S(1)} collective-permute-done((f32[5,28,4,128]{3,2,1,0:T(4,128)S(1)}, f32[5,28,4,128]{3,2,1,0:T(4,128)S(1)}, u32[]{:S(2)}, u32[]{:S(2)}) %collective-permute-start.2) | collective-permute-done | bytes 286752 | tf_op jit(solution)/shard_map/ppermute | solution.py:703
  15.1 5.8 %collective-permute-done.3.refs_3_ = f32[5,28,4,128]{3,2,1,0:T(4,128)S(1)} collective-permute-done((f32[5,28,4,128]{3,2,1,0:T(4,128)S(1)}, f32[5,28,4,128]{3,2,1,0:T(4,128)S(1)}, u32[]{:S(2)}, u32[]{:S(2)}) %collective-permute-start.3) | collective-permute-done | bytes 286752 | tf_op jit(solution)/shard_map/ppermute | solution.py:703
  20.9 4.5 %shard_map.38 = (f32[3,8,8,128]{3,2,1,0:T(8,128)S(1)}, f32[8,88,128]{2,1,0:T(8,128)S(1)}, f32[9,20,16,128]{3,2,1,0:T(8,128)}, f32[9,20,16,128]{3,2,1,0:T(8,128)}) custom-call(s32[2]{0:T(128)S(1)} %pad_add_fusion.par.refs_0_, f32[5,20,8,128]{3,2,1,0:T(8,128)S(1)} %get-tuple-element.33.refs_1_, f32[5,28,4,128]{3,2,1,0:T(4,128)S(1)} %collective-permute-done.2.refs_2_, ...), custom_call_target="tpu_custom_call" | custom-call | flops 20000000 | bytes 1000000 | tf_op jit(solution)/shard_map/pallas_call | solution.py:684
  25.5 14.2 %all_to_all.20.refs_1_ = f32[8,88,128]{2,1,0:T(8,128)S(1)} all-to-all(f32[8,88,128]{2,1,0:T(8,128)S(1)} %get-tuple-element.37), channel_id=1, replica_groups=mesh['gx_0'=4,'gx_1'=2,'gy_0'=8,'gy_1'=4] {'gx_0','gx_1'}, dimensions={0} | all-to-all | bytes 720896 | tf_op jit(solution)/shard_map/all_to_all | solution.py:711
  39.6 3.6 %collective-permute-start.7 = (f32[8,88,128]{2,1,0:T(8,128)S(1)}, f32[8,88,128]{2,1,0:T(8,128)S(1)}, u32[]{:S(2)}, u32[]{:S(2)}) collective-permute-start(f32[8,88,128]{2,1,0:T(8,128)S(1)} %all_to_all.20.refs_1_), channel_id=1, source_target_pairs={{1,2},{2,1},{3,4},{4,3},{5,6},{6,5},{7,8},{8,7},{9,10},{10,9},{11,... | collective-permute-start | bytes 1081352 | tf_op jit(solution)/shard_map/ppermute | solution.py:703
  47.0 6.6 %collective-permute-done.7.refs_3_ = f32[8,88,128]{2,1,0:T(8,128)S(1)} collective-permute-done((f32[8,88,128]{2,1,0:T(8,128)S(1)}, f32[8,88,128]{2,1,0:T(8,128)S(1)}, u32[]{:S(2)}, u32[]{:S(2)}) %collective-permute-start.7) | collective-permute-done | bytes 360480 | tf_op jit(solution)/shard_map/ppermute | solution.py:703
  53.6 3.9 %shard_map.39 = (f32[32,12,128]{2,1,0:T(8,128)}, f32[6,16,4,128]{3,2,1,0:T(4,128)S(1)}, f32[6,16,4,128]{3,2,1,0:T(4,128)S(1)}, f32[17,16,128]{2,1,0:T(8,128)}, f...) custom-call(s32[2]{0:T(128)S(1)} %pad_add_fusion.par.refs_0_, ...), custom_call_target="tpu_custom_call" | custom-call | flops 20000000 | bytes 1000000 | tf_op jit(solution)/shard_map/pallas_call | solution.py:684
  57.5 11.2 %all-to-all-start.1 = ((f32[32,12,128]{2,1,0:T(8,128)}), f32[32,12,128]{2,1,0:T(8,128)S(1)}, u32[]{:S(2)}, u32[]{:S(2)}) async-start(f32[32,12,128]{2,1,0:T(8,128)} %get-tuple-element.40), calls=%async_computation.1 | async-start | bytes 524288 | tf_op jit(solution)/shard_map/all_to_all | solution.py:711
  70.3 4.0 %collective-permute-start.9 = (f32[6,16,4,128]{3,2,1,0:T(4,128)S(1)}, f32[6,16,4,128]{3,2,1,0:T(4,128)S(1)}, u32[]{:S(2)}, u32[]{:S(2)}) collective-permute-start(f32[6,16,4,128]{3,2,1,0:T(4,128)S(1)} %get-tuple-element.39), channel_id=1, source_target_pairs={{1,2},{2,1},{3,4},{4,3},{5,6},{6,5},{7,8},{8,7},{9,10},{10,9},{11,... | collective-permute-start | bytes 589832 | tf_op jit(solution)/shard_map/ppermute | solution.py:703
  74.2 5.8 %all-to-all-done.1 = f32[32,12,128]{2,1,0:T(8,128)S(1)} async-done(((f32[32,12,128]{2,1,0:T(8,128)}), f32[32,12,128]{2,1,0:T(8,128)S(1)}, u32[]{:S(2)}, u32[]{:S(2)}) %all-to-all-start.1) | async-done | bytes 196640 | tf_op jit(solution)/shard_map/all_to_all | solution.py:711
  81.4 4.0 %shard_map.40 = (f32[2,12,4,128]{3,2,1,0:T(4,128)S(1)}, f32[6,32,128]{2,1,0:T(8,128)}) custom-call(s32[2]{0:T(128)S(1)} %pad_add_fusion.par.refs_0_, f32[384,128]{1,0:T(8,128)S(1)} %reshape.6.refs_1_, f32[17,16,128]{2,1,0:T(8,128)} %get-tuple-element.41.refs_2_, f32[11,16,16,128]{3,2,1,0:T(8,128)} %get-tuple-element.42.refs_3_, ...), custom_call_target="tpu_custom_call" | custom-call | flops 20000000 | bytes 1000000 | tf_op jit(solution)/shard_map/pallas_call | solution.py:684
  88.8 4.7 %collective-permute-done.11.eb = f32[2,12,4,128]{3,2,1,0:T(4,128)S(1)} collective-permute-done((f32[2,12,4,128]{3,2,1,0:T(4,128)S(1)}, f32[2,12,4,128]{3,2,1,0:T(4,128)S(1)}, u32[]{:S(2)}, u32[]{:S(2)}) %collective-permute-start.11) | collective-permute-done | bytes 49184 | tf_op jit(solution)/shard_map/ppermute | solution.py:703
  101.0 4.2 %collective-permute-start.15 = (f32[3,28,4,128]{3,2,1,0:T(4,128)S(1)}, f32[3,28,4,128]{3,2,1,0:T(4,128)S(1)}, u32[]{:S(2)}, u32[]{:S(2)}) collective-permute-start(f32[3,28,4,128]{3,2,1,0:T(4,128)S(1)} %get-tuple-element.49), channel_id=1, source_target_pairs={{1,2},{2,1},{3,4},{4,3},{5,6},{6,5},{7,8},{8,7},{9,10},{10,9},{11,... | collective-permute-start | bytes 516104 | tf_op jit(solution)/shard_map/ppermute | solution.py:703
  108.0 4.0 %collective-permute-done.15.refs_3_ = f32[3,28,4,128]{3,2,1,0:T(4,128)S(1)} collective-permute-done((f32[3,28,4,128]{3,2,1,0:T(4,128)S(1)}, f32[3,28,4,128]{3,2,1,0:T(4,128)S(1)}, u32[]{:S(2)}, u32[]{:S(2)}) %collective-permute-start.15) | collective-permute-done | bytes 172064 | tf_op jit(solution)/shard_map/ppermute | solution.py:703
  112.0 3.9 %shard_map.43 = (f32[3,8,8,128]{3,2,1,0:T(8,128)S(1)}, f32[8,40,128]{2,1,0:T(8,128)S(1)}, f32[9,20,16,128]{3,2,1,0:T(8,128)}) custom-call(s32[2]{0:T(128)S(1)} %pad_add_fusion.par.refs_0_, f32[3,20,8,128]{3,2,1,0:T(8,128)S(1)} %get-tuple-element.47.refs_1_, f32[3,28,4,128]{3,2,1,0:T(4,128)S(1)} %collective-permute-done.14.refs_2_, ...), custom_call_target="tpu_custom_call" | custom-call | flops 20000000 | bytes 1000000 | tf_op jit(solution)/shard_map/pallas_call | solution.py:684
  115.9 10.3 %all_to_all.21.refs_1_ = f32[8,40,128]{2,1,0:T(8,128)S(1)} all-to-all(f32[8,40,128]{2,1,0:T(8,128)S(1)} %get-tuple-element.51), channel_id=1, replica_groups=mesh['gx_0'=4,'gx_1'=2,'gy_0'=8,'gy_1'=4] {'gx_0','gx_1'}, dimensions={0} | all-to-all | bytes 327680 | tf_op jit(solution)/shard_map/all_to_all | solution.py:711
  126.2 4.2 %collective-permute-start.19 = (f32[8,40,128]{2,1,0:T(8,128)S(1)}, f32[8,40,128]{2,1,0:T(8,128)S(1)}, u32[]{:S(2)}, u32[]{:S(2)}) collective-permute-start(f32[8,40,128]{2,1,0:T(8,128)S(1)} %all_to_all.21.refs_1_), channel_id=1, source_target_pairs={{1,2},{2,1},{3,4},{4,3},{5,6},{6,5},{7,8},{8,7},{9,10},{10,9},{11,... | collective-permute-start | bytes 491528 | tf_op jit(solution)/shard_map/ppermute | solution.py:703
  139.4 3.9 %collective-permute-start.21 = (f32[6,16,4,128]{3,2,1,0:T(4,128)S(1)}, f32[6,16,4,128]{3,2,1,0:T(4,128)S(1)}, u32[]{:S(2)}, u32[]{:S(2)}) collective-permute-start(f32[6,16,4,128]{3,2,1,0:T(4,128)S(1)} %get-tuple-element.54), channel_id=1, source_target_pairs={{1,2},{2,1},{3,4},{4,3},{5,6},{6,5},{7,8},{8,7},{9,10},{10,9},{11,... | collective-permute-start | bytes 589832 | tf_op jit(solution)/shard_map/ppermute | solution.py:703
  143.3 20.7 %all_to_all.22 = f32[32,4,128]{2,1,0:T(4,128)S(1)} all-to-all(f32[32,4,128]{2,1,0:T(4,128)S(1)} %get-tuple-element.55), channel_id=1, replica_groups=mesh['gx_0'=4,'gx_1'=2,'gy_0'=8,'gy_1'=4] {'gy_0','gy_1'}, dimensions={0} | all-to-all | bytes 131072 | tf_op jit(solution)/shard_map/all_to_all | solution.py:711
  164.0 4.0 %shard_map.45.mine = f32[2,12,4,128]{3,2,1,0:T(4,128)S(1)} custom-call(s32[2]{0:T(128)S(1)} %pad_add_fusion.par.refs_0_, f32[128,128]{1,0:T(8,128)S(1)} %bitcast.5, f32[17,16,128]{2,1,0:T(8,128)} %get-tuple-element.56.refs_2_, f32[11,16,16,128]{3,2,1,0:T(8,128)} %get-tuple-element.57.refs_3_, f32[3,18,16,128]{3,2,1,0:T(8,128)} %get-tuple-element.58.refs_4_, ...), custom_call_target="tpu_custom_call" | custom-call | flops 20000000 | bytes 1000000 | tf_op jit(solution)/shard_map/pallas_call | solution.py:684
  168.0 4.0 %collective-permute-start.23 = (f32[2,12,4,128]{3,2,1,0:T(4,128)S(1)}, f32[2,12,4,128]{3,2,1,0:T(4,128)S(1)}, u32[]{:S(2)}, u32[]{:S(2)}) collective-permute-start(f32[2,12,4,128]{3,2,1,0:T(4,128)S(1)} %shard_map.45.mine), channel_id=1, source_target_pairs={{1,2},{2,1},{3,4},{4,3},{5,6},{6,5},{7,8},{8,7},{9,10},{10,9},{11,... | collective-permute-start | bytes 147464 | tf_op jit(solution)/shard_map/ppermute | solution.py:703
  172.0 4.0 %collective-permute-done.23.eb = f32[2,12,4,128]{3,2,1,0:T(4,128)S(1)} collective-permute-done((f32[2,12,4,128]{3,2,1,0:T(4,128)S(1)}, f32[2,12,4,128]{3,2,1,0:T(4,128)S(1)}, u32[]{:S(2)}, u32[]{:S(2)}) %collective-permute-start.23) | collective-permute-done | bytes 49184 | tf_op jit(solution)/shard_map/ppermute | solution.py:703
  176.1 3.7 %shard_map.46 = f32[3,8,8,128]{3,2,1,0:T(8,128)} custom-call(s32[2]{0:T(128)S(1)} %pad_add_fusion.par.refs_0_, f32[3,8,8,128]{3,2,1,0:T(8,128)S(1)} %get-tuple-element.50.refs_4_.flow, f32[3,8,8,128]{3,2,1,0:T(8,128)S(1)} %collective-permute-done.16.refs_5_.fa, f32[3,8,8,128]{3,2,1,0:T(8,128)S(1)} %collective-permute-done.17.refs_6_.fb, ...), custom_call_target="tpu_custom_call" | custom-call | flops 20000000 | bytes 1000000 | tf_op jit(solution)/shard_map/pallas_call | solution.py:684
  (48 shorter events, 37.3 us)
Async XLA Ops:
  0.9 3.7 %collective-permute-start.1 = (f32[5,8,8,128]{3,2,1,0:T(8,128)S(1)}, f32[5,8,8,128]{3,2,1,0:T(8,128)S(1)}, u32[]{:S(2)}, u32[]{:S(2)}) collective-permute-start(f32[5,8,8,128]{3,2,1,0:T(8,128)S(1)} %pad_maximum_fusion.own), channel_id=1, source_target_pairs={{32,64},{64,32},{96,128},{128,96},{160,192},{192,160},{33,65},{65,... | collective-permute-start | bytes 491528 | tf_op jit(solution)/shard_map/ppermute | solution.py:703
  1.6 4.0 %collective-permute-start = (f32[5,8,8,128]{3,2,1,0:T(8,128)S(1)}, f32[5,8,8,128]{3,2,1,0:T(8,128)S(1)}, u32[]{:S(2)}, u32[]{:S(2)}) collective-permute-start(f32[5,8,8,128]{3,2,1,0:T(8,128)S(1)} %pad_maximum_fusion.own), channel_id=1, source_target_pairs={{0,32},{32,0},{64,96},{96,64},{128,160},{160,128},{192,224},{224,1... | collective-permute-start | bytes 491528 | tf_op jit(solution)/shard_map/ppermute | solution.py:703
  6.2 8.9 %collective-permute-start.2 = (f32[5,28,4,128]{3,2,1,0:T(4,128)S(1)}, f32[5,28,4,128]{3,2,1,0:T(4,128)S(1)}, u32[]{:S(2)}, u32[]{:S(2)}) collective-permute-start(f32[5,28,4,128]{3,2,1,0:T(4,128)S(1)} %get-tuple-element.34), channel_id=1, source_target_pairs={{0,1},{1,0},{2,3},{3,2},{4,5},{5,4},{6,7},{7,6},{8,9},{9,8},{10,11... | collective-permute-start | bytes 860168 | tf_op jit(solution)/shard_map/ppermute | solution.py:703
  7.9 13.1 %collective-permute-start.3 = (f32[5,28,4,128]{3,2,1,0:T(4,128)S(1)}, f32[5,28,4,128]{3,2,1,0:T(4,128)S(1)}, u32[]{:S(2)}, u32[]{:S(2)}) collective-permute-start(f32[5,28,4,128]{3,2,1,0:T(4,128)S(1)} %get-tuple-element.35), channel_id=1, source_target_pairs={{1,2},{2,1},{3,4},{4,3},{5,6},{6,5},{7,8},{8,7},{9,10},{10,9},{11,... | collective-permute-start | bytes 860168 | tf_op jit(solution)/shard_map/ppermute | solution.py:703
  39.6 14.0 %collective-permute-start.7 = (f32[8,88,128]{2,1,0:T(8,128)S(1)}, f32[8,88,128]{2,1,0:T(8,128)S(1)}, u32[]{:S(2)}, u32[]{:S(2)}) collective-permute-start(f32[8,88,128]{2,1,0:T(8,128)S(1)} %all_to_all.20.refs_1_), channel_id=1, source_target_pairs={{1,2},{2,1},{3,4},{4,3},{5,6},{6,5},{7,8},{8,7},{9,10},{10,9},{11,... | collective-permute-start | bytes 1081352 | tf_op jit(solution)/shard_map/ppermute | solution.py:703
  43.3 10.4 %collective-permute-start.6 = (f32[8,88,128]{2,1,0:T(8,128)S(1)}, f32[8,88,128]{2,1,0:T(8,128)S(1)}, u32[]{:S(2)}, u32[]{:S(2)}) collective-permute-start(f32[8,88,128]{2,1,0:T(8,128)S(1)} %all_to_all.20.refs_1_), channel_id=1, source_target_pairs={{0,1},{1,0},{2,3},{3,2},{4,5},{5,4},{6,7},{7,6},{8,9},{9,8},{10,11... | collective-permute-start | bytes 1081352 | tf_op jit(solution)/shard_map/ppermute | solution.py:703
  44.0 3.0 %collective-permute-start.4 = (f32[3,8,8,128]{3,2,1,0:T(8,128)S(1)}, f32[3,8,8,128]{3,2,1,0:T(8,128)S(1)}, u32[]{:S(2)}, u32[]{:S(2)}) collective-permute-start(f32[3,8,8,128]{3,2,1,0:T(8,128)S(1)} %get-tuple-element.36.refs_4_.flow), channel_id=1, source_target_pairs={{0,32},{32,0},{64,96},{96,64},{128,160},{160,128},{192,224},{224,1... | collective-permute-start | bytes 294920 | tf_op jit(solution)/shard_map/ppermute | solution.py:703
  57.5 22.4 %all-to-all-start.1 = ((f32[32,12,128]{2,1,0:T(8,128)}), f32[32,12,128]{2,1,0:T(8,128)S(1)}, u32[]{:S(2)}, u32[]{:S(2)}) async-start(f32[32,12,128]{2,1,0:T(8,128)} %get-tuple-element.40), calls=%async_computation.1 | async-start | bytes 524288 | tf_op jit(solution)/shard_map/all_to_all | solution.py:711
  68.7 11.3 %collective-permute-start.8 = (f32[6,16,4,128]{3,2,1,0:T(4,128)S(1)}, f32[6,16,4,128]{3,2,1,0:T(4,128)S(1)}, u32[]{:S(2)}, u32[]{:S(2)}) collective-permute-start(f32[6,16,4,128]{3,2,1,0:T(4,128)S(1)} %get-tuple-element.38), channel_id=1, source_target_pairs={{0,1},{1,0},{2,3},{3,2},{4,5},{5,4},{6,7},{7,6},{8,9},{9,8},{10,11... | collective-permute-start | bytes 589832 | tf_op jit(solution)/shard_map/ppermute | solution.py:703
  70.3 11.2 %collective-permute-start.9 = (f32[6,16,4,128]{3,2,1,0:T(4,128)S(1)}, f32[6,16,4,128]{3,2,1,0:T(4,128)S(1)}, u32[]{:S(2)}, u32[]{:S(2)}) collective-permute-start(f32[6,16,4,128]{3,2,1,0:T(4,128)S(1)} %get-tuple-element.39), channel_id=1, source_target_pairs={{1,2},{2,1},{3,4},{4,3},{5,6},{6,5},{7,8},{8,7},{9,10},{10,9},{11,... | collective-permute-start | bytes 589832 | tf_op jit(solution)/shard_map/ppermute | solution.py:703
  85.4 8.1 %collective-permute-start.11 = (f32[2,12,4,128]{3,2,1,0:T(4,128)S(1)}, f32[2,12,4,128]{3,2,1,0:T(4,128)S(1)}, u32[]{:S(2)}, u32[]{:S(2)}) collective-permute-start(f32[2,12,4,128]{3,2,1,0:T(4,128)S(1)} %get-tuple-element.44.mine), channel_id=1, source_target_pairs={{1,2},{2,1},{3,4},{4,3},{5,6},{6,5},{7,8},{8,7},{9,10},{10,9},{11,... | collective-permute-start | bytes 147464 | tf_op jit(solution)/shard_map/ppermute | solution.py:703
  88.6 5.0 %collective-permute-start.10 = (f32[2,12,4,128]{3,2,1,0:T(4,128)S(1)}, f32[2,12,4,128]{3,2,1,0:T(4,128)S(1)}, u32[]{:S(2)}, u32[]{:S(2)}) collective-permute-start(f32[2,12,4,128]{3,2,1,0:T(4,128)S(1)} %get-tuple-element.44.mine), channel_id=1, source_target_pairs={{0,1},{1,0},{2,3},{3,2},{4,5},{5,4},{6,7},{7,6},{8,9},{9,8},{10,11... | collective-permute-start | bytes 147464 | tf_op jit(solution)/shard_map/ppermute | solution.py:703
  96.6 2.8 %collective-permute-start.13 = (f32[3,8,8,128]{3,2,1,0:T(8,128)S(1)}, f32[3,8,8,128]{3,2,1,0:T(8,128)S(1)}, u32[]{:S(2)}, u32[]{:S(2)}) collective-permute-start(f32[3,8,8,128]{3,2,1,0:T(8,128)S(1)} %shard_map.41.own), channel_id=1, source_target_pairs={{32,64},{64,32},{96,128},{128,96},{160,192},{192,160},{33,65},{65,... | collective-permute-start | bytes 294920 | tf_op jit(solution)/shard_map/ppermute | solution.py:703
  97.4 3.0 %collective-permute-start.12 = (f32[3,8,8,128]{3,2,1,0:T(8,128)S(1)}, f32[3,8,8,128]{3,2,1,0:T(8,128)S(1)}, u32[]{:S(2)}, u32[]{:S(2)}) collective-permute-start(f32[3,8,8,128]{3,2,1,0:T(8,128)S(1)} %shard_map.41.own), channel_id=1, source_target_pairs={{0,32},{32,0},{64,96},{96,64},{128,160},{160,128},{192,224},{224,1... | collective-permute-start | bytes 294920 | tf_op jit(solution)/shard_map/ppermute | solution.py:703
  100.9 7.0 %collective-permute-start.14 = (f32[3,28,4,128]{3,2,1,0:T(4,128)S(1)}, f32[3,28,4,128]{3,2,1,0:T(4,128)S(1)}, u32[]{:S(2)}, u32[]{:S(2)}) collective-permute-start(f32[3,28,4,128]{3,2,1,0:T(4,128)S(1)} %get-tuple-element.48), channel_id=1, source_target_pairs={{0,1},{1,0},{2,3},{3,2},{4,5},{5,4},{6,7},{7,6},{8,9},{9,8},{10,11... | collective-permute-start | bytes 516104 | tf_op jit(solution)/shard_map/ppermute | solution.py:703
  101.0 11.0 %collective-permute-start.15 = (f32[3,28,4,128]{3,2,1,0:T(4,128)S(1)}, f32[3,28,4,128]{3,2,1,0:T(4,128)S(1)}, u32[]{:S(2)}, u32[]{:S(2)}) collective-permute-start(f32[3,28,4,128]{3,2,1,0:T(4,128)S(1)} %get-tuple-element.49), channel_id=1, source_target_pairs={{1,2},{2,1},{3,4},{4,3},{5,6},{6,5},{7,8},{8,7},{9,10},{10,9},{11,... | collective-permute-start | bytes 516104 | tf_op jit(solution)/shard_map/ppermute | solution.py:703
  126.2 9.7 %collective-permute-start.19 = (f32[8,40,128]{2,1,0:T(8,128)S(1)}, f32[8,40,128]{2,1,0:T(8,128)S(1)}, u32[]{:S(2)}, u32[]{:S(2)}) collective-permute-start(f32[8,40,128]{2,1,0:T(8,128)S(1)} %all_to_all.21.refs_1_), channel_id=1, source_target_pairs={{1,2},{2,1},{3,4},{4,3},{5,6},{6,5},{7,8},{8,7},{9,10},{10,9},{11,... | collective-permute-start | bytes 491528 | tf_op jit(solution)/shard_map/ppermute | solution.py:703
  130.4 5.5 %collective-permute-start.18 = (f32[8,40,128]{2,1,0:T(8,128)S(1)}, f32[8,40,128]{2,1,0:T(8,128)S(1)}, u32[]{:S(2)}, u32[]{:S(2)}) collective-permute-start(f32[8,40,128]{2,1,0:T(8,128)S(1)} %all_to_all.21.refs_1_), channel_id=1, source_target_pairs={{0,1},{1,0},{2,3},{3,2},{4,5},{5,4},{6,7},{7,6},{8,9},{9,8},{10,11... | collective-permute-start | bytes 491528 | tf_op jit(solution)/shard_map/ppermute | solution.py:703
  130.5 2.7 %collective-permute-start.17 = (f32[3,8,8,128]{3,2,1,0:T(8,128)S(1)}, f32[3,8,8,128]{3,2,1,0:T(8,128)S(1)}, u32[]{:S(2)}, u32[]{:S(2)}) collective-permute-start(f32[3,8,8,128]{3,2,1,0:T(8,128)S(1)} %get-tuple-element.50.refs_4_.flow), channel_id=1, source_target_pairs={{32,64},{64,32},{96,128},{128,96},{160,192},{192,160},{33,65},{65,... | collective-permute-start | bytes 294920 | tf_op jit(solution)/shard_map/ppermute | solution.py:703
  131.2 3.0 %collective-permute-start.16 = (f32[3,8,8,128]{3,2,1,0:T(8,128)S(1)}, f32[3,8,8,128]{3,2,1,0:T(8,128)S(1)}, u32[]{:S(2)}, u32[]{:S(2)}) collective-permute-start(f32[3,8,8,128]{3,2,1,0:T(8,128)S(1)} %get-tuple-element.50.refs_4_.flow), channel_id=1, source_target_pairs={{0,32},{32,0},{64,96},{96,64},{128,160},{160,128},{192,224},{224,1... | collective-permute-start | bytes 294920 | tf_op jit(solution)/shard_map/ppermute | solution.py:703
  139.0 25.0 %collective-permute-start.20 = (f32[6,16,4,128]{3,2,1,0:T(4,128)S(1)}, f32[6,16,4,128]{3,2,1,0:T(4,128)S(1)}, u32[]{:S(2)}, u32[]{:S(2)}) collective-permute-start(f32[6,16,4,128]{3,2,1,0:T(4,128)S(1)} %get-tuple-element.53), channel_id=1, source_target_pairs={{0,1},{1,0},{2,3},{3,2},{4,5},{5,4},{6,7},{7,6},{8,9},{9,8},{10,11... | collective-permute-start | bytes 589832 | tf_op jit(solution)/shard_map/ppermute | solution.py:703
  139.4 24.6 %collective-permute-start.21 = (f32[6,16,4,128]{3,2,1,0:T(4,128)S(1)}, f32[6,16,4,128]{3,2,1,0:T(4,128)S(1)}, u32[]{:S(2)}, u32[]{:S(2)}) collective-permute-start(f32[6,16,4,128]{3,2,1,0:T(4,128)S(1)} %get-tuple-element.54), channel_id=1, source_target_pairs={{1,2},{2,1},{3,4},{4,3},{5,6},{6,5},{7,8},{8,7},{9,10},{10,9},{11,... | collective-permute-start | bytes 589832 | tf_op jit(solution)/shard_map/ppermute | solution.py:703
  168.0 8.1 %collective-permute-start.23 = (f32[2,12,4,128]{3,2,1,0:T(4,128)S(1)}, f32[2,12,4,128]{3,2,1,0:T(4,128)S(1)}, u32[]{:S(2)}, u32[]{:S(2)}) collective-permute-start(f32[2,12,4,128]{3,2,1,0:T(4,128)S(1)} %shard_map.45.mine), channel_id=1, source_target_pairs={{1,2},{2,1},{3,4},{4,3},{5,6},{6,5},{7,8},{8,7},{9,10},{10,9},{11,... | collective-permute-start | bytes 147464 | tf_op jit(solution)/shard_map/ppermute | solution.py:703
  171.9 4.2 %collective-permute-start.22 = (f32[2,12,4,128]{3,2,1,0:T(4,128)S(1)}, f32[2,12,4,128]{3,2,1,0:T(4,128)S(1)}, u32[]{:S(2)}, u32[]{:S(2)}) collective-permute-start(f32[2,12,4,128]{3,2,1,0:T(4,128)S(1)} %shard_map.45.mine), channel_id=1, source_target_pairs={{0,1},{1,0},{2,3},{3,2},{4,5},{5,4},{6,7},{7,6},{8,9},{9,8},{10,11... | collective-permute-start | bytes 147464 | tf_op jit(solution)/shard_map/ppermute | solution.py:703
  (4 other events, 108.7 us)
